TPU v7x, 32 devices: a whole 2x2x4 slice. The times are simulated.
32 devices in a mesh: ctx: 16 (over z, y, core), fsdp: 2 (over x).
Axes of the slice: x: 2, y: 2, z: 4, core: 2. Of those that a mesh axis runs over, the one named last changes fastest.
Arguments:
- block_input: bfloat16 [2, 16, 128, 1024], P(None, 'ctx', 'fsdp'), may hold values from -6 to 6
- dy: bfloat16 [2, 16, 128, 1024], P(None, 'ctx', 'fsdp'), may hold values from -6 to 6
- attn_gain: float32 [1024], replicated, may hold values from 0.25 to 1.75
- q_gain: float32 [64], replicated, may hold values from 0.7 to 1.4, as said below
- k_gain: float32 [64], replicated, may hold values from 0.7 to 1.4, as said below
- ffn_gain: float32 [1024], replicated, may hold values from 0.25 to 1.75
- wq: bfloat16 [1024, 1024], P('fsdp'), may hold values from -0.1875 to 0.1875
- wk: bfloat16 [1024, 512], P('fsdp'), may hold values from -0.1875 to 0.1875
- wv: bfloat16 [1024, 512], P('fsdp'), may hold values from -0.1875 to 0.1875
- wo: bfloat16 [1024, 1024], P('fsdp'), may hold values from -1.5 to 1.5
- w_gate: bfloat16 [1024, 4608], P('fsdp'), may hold values from -0.1875 to 0.1875
- w_up: bfloat16 [1024, 4608], P('fsdp'), may hold values from -0.1875 to 0.1875
- w_down: bfloat16 [4608, 1024], P('fsdp'), may hold values from -0.09375 to 0.09375
Outputs:
- block_output: bfloat16 [2, 16, 128, 1024], P(None, 'ctx', 'fsdp')
- dx: float32 [2, 16, 128, 1024], P(None, 'ctx', 'fsdp')
- d_attn_gain: float32 [1024], replicated
- d_q_gain: float32 [64], replicated
- d_k_gain: float32 [64], replicated
- d_ffn_gain: float32 [1024], replicated
- d_wq: float32 [1024, 1024], P(('ctx', 'fsdp'))
- d_wk: float32 [1024, 512], P(('ctx', 'fsdp'))
- d_wv: float32 [1024, 512], P(('ctx', 'fsdp'))
- d_wo: float32 [1024, 1024], P(('ctx', 'fsdp'))
- d_w_gate: float32 [1024, 4608], P(('ctx', 'fsdp'))
- d_w_up: float32 [1024, 4608], P(('ctx', 'fsdp'))
- d_w_down: float32 [4608, 1024], P(('ctx', 'fsdp'))
Inputs may be any that keep to these rules, and one draw needn't show every extreme that they name: `q_gain`: each entry is a positive gain. `k_gain`: each entry is a positive gain.
All inputs are finite; a program needn't handle non-finite values.
Results may differ from a plain program's by a relative error of at most 0.014.
Values may be sent and summed in bfloat16 or wider, within the bound.
A program may use at most 448 MiB of HBM per device.

v0:
```python
import math

import jax
import jax.numpy as jnp
from jax import lax
from jax.sharding import PartitionSpec as P

EPS = 1e-05
ROPE_BASE = 1000000.0


def rms_forward(inputs, gain_vec):
    inverse = lax.rsqrt(jnp.mean(inputs * inputs, axis=-1, keepdims=True) + EPS)
    return (inputs * inverse * gain_vec, inverse)


def rms_backward(inputs, inverse, gain_vec, grad_out):
    scaled = grad_out * gain_vec
    inner_mean = jnp.mean(scaled * inputs, axis=-1, keepdims=True)
    grad_in = inverse * scaled - inputs * (inverse * inverse * inverse) * inner_mean
    grad_gain = jnp.sum((grad_out * inputs * inverse).reshape(-1, inputs.shape[-1]), axis=0)
    return (grad_in, grad_gain)


def rope_tables(positions, head_width):
    frequency = ROPE_BASE ** (-2.0 * jnp.arange(head_width // 2, dtype=jnp.float32) / head_width)
    angles = positions.astype(jnp.float32)[:, None] * frequency[None, :]
    cosine = jnp.concatenate([jnp.cos(angles), jnp.cos(angles)], axis=-1)[:, None, :]
    sine_tab = jnp.concatenate([jnp.sin(angles), jnp.sin(angles)], axis=-1)[:, None, :]
    return (cosine, sine_tab)


def rotate(inputs):
    half_width = inputs.shape[-1] // 2
    return jnp.concatenate([-inputs[..., half_width:], inputs[..., :half_width]], axis=-1)


def unrotate(inputs):
    half_width = inputs.shape[-1] // 2
    return jnp.concatenate([inputs[..., half_width:], -inputs[..., :half_width]], axis=-1)


def token_position(group_index, member_index, within, block_part, fsdp_size, pair_count):
    block_len = block_part * fsdp_size
    early_pos = group_index * block_len + member_index * block_part + within
    late_pos = (
        (2 * pair_count - 1 - group_index) * block_len
        + member_index * block_part
        + within
        - block_part
    )
    return jnp.where(within < block_part, early_pos, late_pos)


def device_to_sequence(rows_arr, pair_count, fsdp_size, block_part):
    width = rows_arr.shape[1]
    shaped = rows_arr.reshape(pair_count, fsdp_size, 2, block_part, width)
    early = shaped[:, :, 0].reshape(-1, width)
    late = shaped[::-1, :, 1].reshape(-1, width)
    return jnp.concatenate([early, late], axis=0)


def sequence_to_device(rows_arr, pair_count, fsdp_size, block_part):
    width = rows_arr.shape[1]
    half_len = rows_arr.shape[0] // 2
    early = rows_arr[:half_len].reshape(pair_count, fsdp_size, block_part, width)
    late = rows_arr[half_len:].reshape(pair_count, fsdp_size, block_part, width)[::-1]
    return jnp.stack([early, late], axis=2).reshape(-1, width)


def local(
    block_input, dy, attn_gain, q_gain, k_gain, ffn_gain, wq, wk, wv, wo, w_gate, w_up, w_down
):
    pair_count = lax.axis_size("ctx")
    fsdp_size = lax.axis_size("fsdp")
    ctx_index = lax.axis_index("ctx")
    block_part = block_input.shape[2]
    block_len = block_part * fsdp_size
    local_rows = 2 * block_part
    model_width = block_input.shape[3]
    head_width = q_gain.shape[0]
    inputs = block_input.reshape(local_rows, model_width).astype(jnp.float32)
    cotangent = dy.reshape(local_rows, model_width)
    local_pos = token_position(
        ctx_index,
        lax.axis_index("fsdp"),
        jnp.arange(local_rows, dtype=jnp.int32),
        block_part,
        fsdp_size,
        pair_count,
    )
    wq_all, wk_all, wv_all, wo_all, gate_all, up_all, down_all = (
        lax.all_gather(wq, "fsdp", axis=0, tiled=True),
        lax.all_gather(wk, "fsdp", axis=0, tiled=True),
        lax.all_gather(wv, "fsdp", axis=0, tiled=True),
        lax.all_gather(wo, "fsdp", axis=0, tiled=True),
        lax.all_gather(w_gate, "fsdp", axis=0, tiled=True),
        lax.all_gather(w_up, "fsdp", axis=0, tiled=True),
        lax.all_gather(w_down, "fsdp", axis=0, tiled=True),
    )
    q_heads = wq_all.shape[1] // head_width
    kv_heads = wk_all.shape[1] // head_width
    query_group_size = q_heads // kv_heads
    kv_cols = kv_heads * head_width
    score_scale = 1.0 / math.sqrt(head_width)
    normed, inverse_in = rms_forward(inputs, attn_gain)
    normed_input_half = normed.astype(jnp.bfloat16)
    queries = jnp.dot(normed_input_half, wq_all, preferred_element_type=jnp.float32).reshape(
        local_rows, q_heads, head_width
    )
    key_unnormed = jnp.dot(normed_input_half, wk_all, preferred_element_type=jnp.float32).reshape(
        local_rows, kv_heads, head_width
    )
    value_rows_half = jnp.dot(normed_input_half, wv_all, preferred_element_type=jnp.float32).astype(
        jnp.bfloat16
    )
    q_normed, q_inverse = rms_forward(queries, q_gain)
    k_normed, k_inverse = rms_forward(key_unnormed, k_gain)
    cosine, sine_tab = rope_tables(local_pos, head_width)
    query_rotated = (q_normed * cosine + rotate(q_normed) * sine_tab).astype(jnp.bfloat16)
    k_rot = (k_normed * cosine + rotate(k_normed) * sine_tab).astype(jnp.bfloat16)
    query_grouped = query_rotated.reshape(local_rows, kv_heads, query_group_size, head_width)
    kv_local = jnp.concatenate([k_rot.reshape(local_rows, kv_cols), value_rows_half], axis=1)
    kv_all = lax.all_gather(kv_local, ("ctx", "fsdp"), axis=0, tiled=True)
    sequence_length = kv_all.shape[0]
    kv_seq = device_to_sequence(kv_all, pair_count, fsdp_size, block_part)
    blocks_per_step = min(8, 2 * pair_count)
    key_block = blocks_per_step * block_len
    step_count = 2 * pair_count // blocks_per_step + 1
    early_steps = ctx_index // blocks_per_step + 1
    late_needed = (2 * pair_count - ctx_index + blocks_per_step - 1) // blocks_per_step
    step_ids = jnp.arange(step_count, dtype=jnp.int32)

    def step_plan(step):
        is_late = step >= early_steps
        span = jnp.where(is_late, step - early_steps, step)
        valid = jnp.where(is_late, span < late_needed, True)
        key_start = jnp.minimum(span * key_block, sequence_length - key_block)
        row_start = jnp.where(is_late, block_part, 0)
        return (key_start, row_start, valid)

    def block_scores(kv_source, query_half, key_start, row_start, valid):
        kv_block = lax.dynamic_slice_in_dim(kv_source, key_start, key_block, 0)
        keys_blk = kv_block[:, :kv_cols].reshape(-1, kv_heads, head_width)
        values_blk = kv_block[:, kv_cols:].reshape(-1, kv_heads, head_width)
        scores = (
            jnp.einsum("bngd,knd->ngbk", query_half, keys_blk, preferred_element_type=jnp.float32)
            * score_scale
        )
        key_pos = key_start + jnp.arange(key_block, dtype=jnp.int32)
        query_pos = lax.dynamic_slice_in_dim(local_pos, row_start, block_part, 0)
        allowed = jnp.logical_and(key_pos[None, :] <= query_pos[:, None], valid)
        return (jnp.where(allowed, scores, -jnp.inf), keys_blk, values_blk)

    def forward_step(running, step):
        all_max, all_total, all_weighted = running
        key_start, row_start, valid = step_plan(step)
        query_half = lax.dynamic_slice_in_dim(query_grouped, row_start, block_part, 0)
        scores, keys_blk, values_blk = block_scores(kv_seq, query_half, key_start, row_start, valid)
        row_max = lax.dynamic_slice_in_dim(all_max, row_start, block_part, 2)
        row_total = lax.dynamic_slice_in_dim(all_total, row_start, block_part, 2)
        weighted = lax.dynamic_slice_in_dim(all_weighted, row_start, block_part, 2)
        new_max = jnp.maximum(row_max, jnp.max(scores, axis=-1))
        safe_max = jnp.where(jnp.isfinite(new_max), new_max, 0.0)
        rescale = jnp.exp(row_max - safe_max)
        exp_scores = jnp.exp(scores - safe_max[..., None])
        row_total = row_total * rescale + jnp.sum(exp_scores, axis=-1)
        weighted = weighted * rescale[..., None] + jnp.einsum(
            "ngbk,knd->ngbd",
            exp_scores.astype(jnp.bfloat16),
            values_blk,
            preferred_element_type=jnp.float32,
        )
        all_max = lax.dynamic_update_slice_in_dim(all_max, new_max, row_start, 2)
        all_total = lax.dynamic_update_slice_in_dim(all_total, row_total, row_start, 2)
        all_weighted = lax.dynamic_update_slice_in_dim(all_weighted, weighted, row_start, 2)
        return ((all_max, all_total, all_weighted), None)

    start_state = (
        jnp.full((kv_heads, query_group_size, local_rows), -jnp.inf, jnp.float32),
        jnp.zeros((kv_heads, query_group_size, local_rows), jnp.float32),
        jnp.zeros((kv_heads, query_group_size, local_rows, head_width), jnp.float32),
    )
    (row_max, row_total, weighted), _ = lax.scan(forward_step, start_state, step_ids)
    log_total = row_max + jnp.log(row_total)
    attention_head_rows = jnp.transpose(weighted / row_total[..., None], (2, 0, 1, 3))
    attn_bf = attention_head_rows.reshape(local_rows, q_heads * head_width).astype(jnp.bfloat16)
    residual = inputs + jnp.dot(attn_bf, wo_all, preferred_element_type=jnp.float32)
    ffn_normed, inverse_ffn = rms_forward(residual, ffn_gain)
    ffn_in = ffn_normed.astype(jnp.bfloat16)
    gate_pre = jnp.dot(ffn_in, gate_all, preferred_element_type=jnp.float32)
    up_pre = jnp.dot(ffn_in, up_all, preferred_element_type=jnp.float32)
    sigmoid_gate = jax.nn.sigmoid(gate_pre)
    silu_gate = gate_pre * sigmoid_gate
    hidden = (silu_gate * up_pre).astype(jnp.bfloat16)
    result = residual + jnp.dot(hidden, down_all, preferred_element_type=jnp.float32)
    d_w_down = jnp.dot(hidden.T, cotangent, preferred_element_type=jnp.float32)
    d_hidden = jnp.dot(cotangent, down_all.T, preferred_element_type=jnp.float32)
    d_gate = (d_hidden * up_pre * sigmoid_gate * (1.0 + gate_pre * (1.0 - sigmoid_gate))).astype(
        jnp.bfloat16
    )
    d_up = (d_hidden * silu_gate).astype(jnp.bfloat16)
    d_w_gate = jnp.dot(ffn_in.T, d_gate, preferred_element_type=jnp.float32)
    d_w_up = jnp.dot(ffn_in.T, d_up, preferred_element_type=jnp.float32)
    d_ffn_in = jnp.dot(d_gate, gate_all.T, preferred_element_type=jnp.float32) + jnp.dot(
        d_up, up_all.T, preferred_element_type=jnp.float32
    )
    d_res_norm, d_ffn_gain = rms_backward(residual, inverse_ffn, ffn_gain, d_ffn_in)
    d_residual = cotangent.astype(jnp.float32) + d_res_norm
    d_res_bf = d_residual.astype(jnp.bfloat16)
    d_wo = jnp.dot(attn_bf.T, d_res_bf, preferred_element_type=jnp.float32)
    attention_gradient = jnp.dot(d_res_bf, wo_all.T, preferred_element_type=jnp.float32).astype(
        jnp.bfloat16
    )
    grad_out_grouped = attention_gradient.reshape(
        local_rows, kv_heads, query_group_size, head_width
    )
    delta_rows = jnp.transpose(
        jnp.sum(grad_out_grouped.astype(jnp.float32) * attention_head_rows, axis=-1), (1, 2, 0)
    )

    def backward_step(running, step):
        grad_query, terms_seq = running
        key_start, row_start, valid = step_plan(step)
        query_half = lax.dynamic_slice_in_dim(query_grouped, row_start, block_part, 0)
        grad_half = lax.dynamic_slice_in_dim(grad_out_grouped, row_start, block_part, 0)
        delta_half = lax.dynamic_slice_in_dim(delta_rows, row_start, block_part, 2)
        log_half = lax.dynamic_slice_in_dim(log_total, row_start, block_part, 2)
        scores, keys_blk, values_blk = block_scores(kv_seq, query_half, key_start, row_start, valid)
        probs_f = jnp.exp(scores - log_half[..., None])
        grad_probs = jnp.einsum(
            "bngd,knd->ngbk", grad_half, values_blk, preferred_element_type=jnp.float32
        )
        grad_scores = (probs_f * (grad_probs - delta_half[..., None]) * score_scale).astype(
            jnp.bfloat16
        )
        query_term = jnp.einsum(
            "ngbk,knd->bngd", grad_scores, keys_blk, preferred_element_type=jnp.float32
        )
        old_query = lax.dynamic_slice_in_dim(grad_query, row_start, block_part, 0)
        grad_query = lax.dynamic_update_slice_in_dim(
            grad_query, old_query + query_term, row_start, 0
        )
        grad_keys = jnp.einsum(
            "ngbk,bngd->knd", grad_scores, query_half, preferred_element_type=jnp.float32
        ).reshape(key_block, kv_cols)
        grad_values = jnp.einsum(
            "ngbk,bngd->knd",
            probs_f.astype(jnp.bfloat16),
            grad_half,
            preferred_element_type=jnp.float32,
        ).reshape(key_block, kv_cols)
        old_terms = lax.dynamic_slice_in_dim(terms_seq, key_start, key_block, 0)
        terms_seq = lax.dynamic_update_slice_in_dim(
            terms_seq, old_terms + jnp.concatenate([grad_keys, grad_values], axis=1), key_start, 0
        )
        return ((grad_query, terms_seq), None)

    back_state = (
        jnp.zeros((local_rows, kv_heads, query_group_size, head_width), jnp.float32),
        jnp.zeros((sequence_length, 2 * kv_cols), jnp.float32),
    )
    (grad_query, terms_seq), _ = lax.scan(backward_step, back_state, step_ids)
    kv_terms = sequence_to_device(terms_seq, pair_count, fsdp_size, block_part)
    pair_share = lax.psum_scatter(kv_terms, "ctx", scatter_dimension=0, tiled=True)
    kv_grad = lax.psum_scatter(pair_share, "fsdp", scatter_dimension=0, tiled=True)
    grad_k_rot = kv_grad[:, :kv_cols].reshape(local_rows, kv_heads, head_width)
    grad_values_own = kv_grad[:, kv_cols:]
    grad_q_rot = grad_query.reshape(local_rows, q_heads, head_width)
    d_q_normed = grad_q_rot * cosine + unrotate(grad_q_rot * sine_tab)
    d_queries, d_q_gain = rms_backward(queries, q_inverse, q_gain, d_q_normed)
    d_k_normed = grad_k_rot * cosine + unrotate(grad_k_rot * sine_tab)
    key_gradient, d_k_gain = rms_backward(key_unnormed, k_inverse, k_gain, d_k_normed)
    dq_bf = d_queries.reshape(local_rows, q_heads * head_width).astype(jnp.bfloat16)
    key_gradient_half = key_gradient.reshape(local_rows, kv_cols).astype(jnp.bfloat16)
    value_gradient_half = grad_values_own.astype(jnp.bfloat16)
    d_wq = jnp.dot(normed_input_half.T, dq_bf, preferred_element_type=jnp.float32)
    d_wk = jnp.dot(normed_input_half.T, key_gradient_half, preferred_element_type=jnp.float32)
    d_wv = jnp.dot(normed_input_half.T, value_gradient_half, preferred_element_type=jnp.float32)
    d_normed = jnp.dot(dq_bf, wq_all.T, preferred_element_type=jnp.float32)
    d_normed = d_normed + jnp.dot(key_gradient_half, wk_all.T, preferred_element_type=jnp.float32)
    d_normed = d_normed + jnp.dot(value_gradient_half, wv_all.T, preferred_element_type=jnp.float32)
    d_inputs, d_attn_gain = rms_backward(inputs, inverse_in, attn_gain, d_normed)
    grad_in = d_residual + d_inputs
    part_q, part_k, part_v, part_o, part_gate, part_up, part_down = (
        lax.psum_scatter(d_wq, "ctx", scatter_dimension=0, tiled=True),
        lax.psum_scatter(d_wk, "ctx", scatter_dimension=0, tiled=True),
        lax.psum_scatter(d_wv, "ctx", scatter_dimension=0, tiled=True),
        lax.psum_scatter(d_wo, "ctx", scatter_dimension=0, tiled=True),
        lax.psum_scatter(d_w_gate, "ctx", scatter_dimension=0, tiled=True),
        lax.psum_scatter(d_w_up, "ctx", scatter_dimension=0, tiled=True),
        lax.psum_scatter(d_w_down, "ctx", scatter_dimension=0, tiled=True),
    )
    owned = (
        lax.psum_scatter(part_q, "fsdp", scatter_dimension=0, tiled=True),
        lax.psum_scatter(part_k, "fsdp", scatter_dimension=0, tiled=True),
        lax.psum_scatter(part_v, "fsdp", scatter_dimension=0, tiled=True),
        lax.psum_scatter(part_o, "fsdp", scatter_dimension=0, tiled=True),
        lax.psum_scatter(part_gate, "fsdp", scatter_dimension=0, tiled=True),
        lax.psum_scatter(part_up, "fsdp", scatter_dimension=0, tiled=True),
        lax.psum_scatter(part_down, "fsdp", scatter_dimension=0, tiled=True),
    )
    own_q, own_k, own_v, own_o, own_gate, own_up, own_down = owned
    sum_attn_gain, sum_q_gain, sum_k_gain, sum_ffn_gain = lax.psum(
        (d_attn_gain, d_q_gain, d_k_gain, d_ffn_gain), ("ctx", "fsdp")
    )
    return (
        result.astype(jnp.bfloat16).reshape(block_input.shape),
        grad_in.reshape(block_input.shape),
        sum_attn_gain,
        sum_q_gain,
        sum_k_gain,
        sum_ffn_gain,
        own_q,
        own_k,
        own_v,
        own_o,
        own_gate,
        own_up,
        own_down,
    )


def solution(mesh):
    placed = (
        P(None, "ctx", "fsdp", None),
        P(None, "ctx", "fsdp", None),
        P(),
        P(),
        P(),
        P(),
        P("fsdp", None),
        P("fsdp", None),
        P("fsdp", None),
        P("fsdp", None),
        P("fsdp", None),
        P("fsdp", None),
        P("fsdp", None),
    )
    return jax.shard_map(
        local,
        mesh=mesh,
        in_specs=placed,
        out_specs=(
            P(None, "ctx", "fsdp", None),
            P(None, "ctx", "fsdp", None),
            P(),
            P(),
            P(),
            P(),
            P(("ctx", "fsdp"), None),
            P(("ctx", "fsdp"), None),
            P(("ctx", "fsdp"), None),
            P(("ctx", "fsdp"), None),
            P(("ctx", "fsdp"), None),
            P(("ctx", "fsdp"), None),
            P(("ctx", "fsdp"), None),
        ),
        check_vma=False,
    )
```

profile of v0, /device:TPU:6, one launch (start us, length us, event | category | flops | bytes accessed | tf_op | source)
XLA Modules:
  0.0 2072.7 jit_solution(14699359552962047674)
XLA Ops:
  13.2 18.0 all-gather.9.cloned.1.call-done
  34.1 19.9 all-gather.11.cloned.1.call-done
  59.0 29.6 %all-gather.15.cloned.1.call-done = bf16[1024,1024]{1,0:T(8,128)(2,1)} async-done(((bf16[512,1024]{1,0:T(8,128)(2,1)}), bf16[1024,1024]{1,0:T(8,128)(2,1)}) %all-gather.15.cloned.1.call-update) | async-done | bytes 2097168 | tf_op jit(solution)/shard_map/all_gather | solution.py:93
  93.6 75.6 %all-gather.13.cloned.1.call-done = bf16[4096,1024]{1,0:T(8,128)(2,1)} async-done(((bf16[128,1024]{1,0:T(8,128)(2,1)}), bf16[4096,1024]{1,0:T(8,128)(2,1)}) %all-gather.13.cloned.1.call-update) | async-done | bytes 8388624 | tf_op jit(solution)/shard_map/all_gather | solution.py:124
  169.2 6.3 fusion.68
  180.8 7.7 pad_maximum_fusion.1
  188.5 11.2 copy.47
  199.9 92.6 %while.26 = (s32[]{:T(128)}, f32[8,2,128]{2,1,0:T(2,128)S(1)}, f32[8,2,128]{2,1,0:T(2,128)S(1)}, f32[8,2,128,64]{2,3,1,0:T(8,128)S(1)}, s32[5]{0:T(128)S(1)}, /*...) while((s32[]{:T(128)}, f32[8,2,128]{2,1,0:T(2,128)S(1)}, ...), condition=%wide.region_6.7_spmd, body=%wide.region_3.6_spmd.sunk | while | flops 280239104 | bytes 37311620 | solution.py:184
  294.9 26.9 %all-gather.21.cloned.1.call-done = bf16[1024,4608]{1,0:T(8,128)(2,1)} async-done(((bf16[512,4608]{1,0:T(8,128)(2,1)}), bf16[1024,4608]{1,0:T(8,128)(2,1)}) %all-gather.21.cloned.1.call-update) | async-done | bytes 9437200 | tf_op jit(solution)/shard_map/all_gather | solution.py:98
  321.8 6.5 fusion.72
  328.3 113.0 %all-gather.19.cloned.1.call-done = bf16[1024,4608]{1,0:T(8,128)(2,1)} async-done(((bf16[512,4608]{1,0:T(8,128)(2,1)}), bf16[1024,4608]{1,0:T(8,128)(2,1)}) %all-gather.19.cloned.1.call-update) | async-done | bytes 9437200 | tf_op jit(solution)/shard_map/all_gather | solution.py:97
  441.3 6.7 fusion.71
  448.0 112.9 %all-gather.23.cloned.1.call-done = bf16[4608,1024]{1,0:T(8,128)(2,1)} async-done(((bf16[2304,1024]{1,0:T(8,128)(2,1)}), bf16[4608,1024]{1,0:T(8,128)(2,1)}) %all-gather.23.cloned.1.call-update) | async-done | bytes 9437200 | tf_op jit(solution)/shard_map/all_gather | solution.py:99
  560.9 9.8 multiply_convert_fusion
  570.7 7.6 fusion.73
  583.6 8.0 broadcast_in_dim.36.clone
  591.5 252.7 %while.27 = (s32[]{:T(128)}, f32[128,8,2,64]{0,3,2,1:T(8,128)S(1)}, f32[4096,1024]{1,0:T(8,128)}, s32[5]{0:T(128)S(1)}, s32[]{:T(128)}, /*index=5*/bf16[4096,102...) while((s32[]{:T(128)}, f32[128,8,2,64]{0,3,2,1:T(8,128)S(1)}, ...), condition=%wide.region_11.12_spmd, body=%wide.region_10.11_spmd.sunk | while | flops 684917760 | bytes 83072184 | solution.py:263
  618.0 6.0 maximum_add_fusion.6
  629.4 11.8 dynamic_update_slice.24
  668.9 6.0 maximum_add_fusion.6
  680.3 11.8 dynamic_update_slice.24
  719.9 6.0 maximum_add_fusion.6
  731.2 11.8 dynamic_update_slice.24
  765.4 5.3 copy.88
  770.8 6.0 maximum_add_fusion.6
  782.1 11.8 dynamic_update_slice.24
  816.2 5.3 copy.88
  821.6 6.0 maximum_add_fusion.6
  832.9 11.3 dynamic_update_slice.24
  844.2 9.4 fusion.67
  860.1 6.1 copy.55
  866.3 177.6 %reduce-scatter.17.cloned.1.call-done = f32[256,1024]{1,0:T(8,128)} async-done(((f32[4096,1024]{1,0:T(8,128)}), f32[256,1024]{1,0:T(8,128)}) %reduce-scatter.17.cloned.1.call-update) | async-done | bytes 1048592 | tf_op jit(solution)/shard_map/reduce_scatter | solution.py:265
  1051.0 13.6 reduce-scatter.19.cloned.1.call-done
  1069.9 9.5 fusion.78
  1080.7 8.4 fusion.77
  1090.4 7.8 fusion.79
  1098.3 42.9 %reduce-scatter.33.cloned.1.call-done = f32[64,1024]{1,0:T(8,128)} async-done(((f32[1024,1024]{1,0:T(8,128)}), f32[64,1024]{1,0:T(8,128)}) %reduce-scatter.33.cloned.1.call-update) | async-done | bytes 262160 | tf_op jit(solution)/shard_map/reduce_scatter | solution.py:289
  1141.2 75.5 %reduce-scatter.21.cloned.1.call-done = f32[64,1024]{1,0:T(8,128)} async-done(((f32[1024,1024]{1,0:T(8,128)}), f32[64,1024]{1,0:T(8,128)}) %reduce-scatter.21.cloned.1.call-update) | async-done | bytes 262160 | tf_op jit(solution)/shard_map/reduce_scatter | solution.py:286
  1216.8 65.1 %reduce-scatter.29.cloned.1.call-done = f32[64,512]{1,0:T(8,128)} async-done(((f32[1024,512]{1,0:T(8,128)}), f32[64,512]{1,0:T(8,128)}) %reduce-scatter.29.cloned.1.call-update) | async-done | bytes 131088 | tf_op jit(solution)/shard_map/reduce_scatter | solution.py:288
  1282.0 64.3 %reduce-scatter.25.cloned.1.call-done = f32[64,512]{1,0:T(8,128)} async-done(((f32[1024,512]{1,0:T(8,128)}), f32[64,512]{1,0:T(8,128)}) %reduce-scatter.25.cloned.1.call-update) | async-done | bytes 131088 | tf_op jit(solution)/shard_map/reduce_scatter | solution.py:287
  1346.4 197.3 %reduce-scatter.41.cloned.1.call-done = f32[64,4608]{1,0:T(8,128)} async-done(((f32[1024,4608]{1,0:T(8,128)}), f32[64,4608]{1,0:T(8,128)}) %reduce-scatter.41.cloned.1.call-update) | async-done | bytes 1179664 | tf_op jit(solution)/shard_map/reduce_scatter | solution.py:291
  1543.8 197.1 %reduce-scatter.37.cloned.1.call-done = f32[64,4608]{1,0:T(8,128)} async-done(((f32[1024,4608]{1,0:T(8,128)}), f32[64,4608]{1,0:T(8,128)}) %reduce-scatter.37.cloned.1.call-update) | async-done | bytes 1179664 | tf_op jit(solution)/shard_map/reduce_scatter | solution.py:290
  1740.9 197.1 %reduce-scatter.45.cloned.1.call-done = f32[288,1024]{1,0:T(8,128)} async-done(((f32[4608,1024]{1,0:T(8,128)}), f32[288,1024]{1,0:T(8,128)}) %reduce-scatter.45.cloned.1.call-update) | async-done | bytes 1179664 | tf_op jit(solution)/shard_map/reduce_scatter | solution.py:292
  1940.5 5.9 fusion.43
  1947.6 40.0 %all-reduce = (f32[1024]{0:T(1024)}, f32[64]{0:T(128)}, f32[64]{0:T(128)}, f32[1024]{0:T(1024)}) all-reduce(f32[1024]{0:T(1024)S(1)} %get-tuple-element.209, f32[64]{0:T(128)S(1)} %get-tuple-element.207, f32[64]{0:T(128)S(1)} %get-tuple-element.211, f32[1024]{0:T(1024)S(1)} %copy-done.43), channel_id=1, replica_groups=mesh['ctx'=16,'fsdp'=2] {'ctx','fsdp'}, use_global_device_ids=true, to_apply=%region_18.19 | all-reduce | flops 2176 | bytes 17408 | tf_op jit(solution)/shard_map/psum | solution.py:304
  1991.5 24.7 %reduce-scatter.43.cloned.1.call-done = f32[32,4608]{1,0:T(8,128)} async-done(((f32[64,4608]{1,0:T(8,128)}), f32[32,4608]{1,0:T(8,128)}) %reduce-scatter.43.cloned.1.call-update) | async-done | bytes 589840 | tf_op jit(solution)/shard_map/reduce_scatter | solution.py:300
  2016.1 24.7 %reduce-scatter.39.cloned.1.call-done = f32[32,4608]{1,0:T(8,128)} async-done(((f32[64,4608]{1,0:T(8,128)}), f32[32,4608]{1,0:T(8,128)}) %reduce-scatter.39.cloned.1.call-update) | async-done | bytes 589840 | tf_op jit(solution)/shard_map/reduce_scatter | solution.py:299
  2040.8 24.5 %reduce-scatter.47.cloned.1.call-done = f32[144,1024]{1,0:T(8,128)} async-done(((f32[288,1024]{1,0:T(8,128)}), f32[144,1024]{1,0:T(8,128)}) %reduce-scatter.47.cloned.1.call-update) | async-done | bytes 589840 | tf_op jit(solution)/shard_map/reduce_scatter | solution.py:301
  (390 shorter events, 285.8 us)
Async XLA Ops:
  7.2 26.5 %copy-start.44 = (f32[64]{0:T(128)S(1)}, f32[64]{0:T(128)}, u32[]{:S(2)}) copy-start(f32[64]{0:T(128)} %param.21) | copy-start | bytes 772
  7.2 23.9 %all-gather.9.cloned.1.call-start = ((), (), s32[]{:S(2)}) async-start(), calls=%async_computation.16 | async-start | bytes 1572864 | tf_op jit(solution)/shard_map/all_gather | solution.py:94
  7.9 46.1 %all-gather.11.cloned.1.call-start = ((), (), s32[]{:S(2)}) async-start(), calls=%async_computation.17 | async-start | bytes 1572864 | tf_op jit(solution)/shard_map/all_gather | solution.py:95
  8.7 80.0 %all-gather.15.cloned.1.call-start = ((), (), s32[]{:S(2)}) async-start(), calls=%async_computation.19 | async-start | bytes 3145728 | tf_op jit(solution)/shard_map/all_gather | solution.py:93
  9.4 159.8 %all-gather.13.cloned.1.call-start = ((), (), s32[]{:S(2)}) async-start(), calls=%async_computation.18 | async-start | bytes 8650752 | tf_op jit(solution)/shard_map/all_gather | solution.py:124
  10.8 82.3 %copy-start.31 = (f32[128,64]{0,1:T(8,128)}, f32[128,64]{0,1:T(8,128)S(1)}, u32[]{:S(2)}) copy-start(f32[128,64]{0,1:T(8,128)S(1)} %get-tuple-element.308) | copy-start | bytes 98308
  10.8 82.3 %copy-start.33 = (f32[128,64]{0,1:T(8,128)}, f32[128,64]{0,1:T(8,128)S(1)}, u32[]{:S(2)}) copy-start(f32[128,64]{0,1:T(8,128)S(1)} %get-tuple-element.309) | copy-start | bytes 98308
  10.9 45.4 %copy-start.48 = (f32[128]{0:T(128)}, f32[128]{0:T(128)S(1)}, u32[]{:S(2)}) copy-start(f32[128]{0:T(128)S(1)} %rsqrt.50) | copy-start | bytes 1540
  12.0 44.3 %copy-start.24 = (bf16[128,1024]{1,0:T(8,128)(2,1)}, bf16[128,1024]{1,0:T(8,128)(2,1)S(1)}, u32[]{:S(2)}) copy-start(bf16[128,1024]{1,0:T(8,128)(2,1)S(1)} %fusion.51) | copy-start | bytes 786436
  13.1 78.4 %copy-start.17 = (bf16[2,1,64,1024]{3,2,1,0:T(8,128)(2,1)}, bf16[2,1,64,1024]{3,2,1,0:T(8,128)(2,1)S(1)}, u32[]{:S(2)}) copy-start(bf16[2,1,64,1024]{3,2,1,0:T(8,128)(2,1)S(1)} %fusion.49) | copy-start | bytes 786436
  33.7 23.7 %copy-start.37 = (f32[128,8]{0,1:T(8,128)}, f32[128,8]{0,1:T(8,128)S(1)}, u32[]{:S(2)}) copy-start(f32[128,8]{0,1:T(8,128)S(1)} %get-tuple-element.295) | copy-start | bytes 12292
  56.3 236.2 %all-gather.17.cloned.1.call-start = ((), (), s32[]{:S(2)}) async-start(), calls=%async_computation.20 | async-start | bytes 3145728 | tf_op jit(solution)/shard_map/all_gather | solution.py:96
  56.9 264.9 %all-gather.21.cloned.1.call-start = ((), (), s32[]{:S(2)}) async-start(), calls=%async_computation.22 | async-start | bytes 14155776 | tf_op jit(solution)/shard_map/all_gather | solution.py:98
  57.5 383.9 %all-gather.19.cloned.1.call-start = ((), (), s32[]{:S(2)}) async-start(), calls=%async_computation.21 | async-start | bytes 14155776 | tf_op jit(solution)/shard_map/all_gather | solution.py:97
  58.2 502.7 %all-gather.23.cloned.1.call-start = ((), (), s32[]{:S(2)}) async-start(), calls=%async_computation.23 | async-start | bytes 14155776 | tf_op jit(solution)/shard_map/all_gather | solution.py:99
  59.0 34.0 %copy-start.46 = (f32[64]{0:T(128)S(1)}, f32[64]{0:T(128)}, u32[]{:S(2)}) copy-start(f32[64]{0:T(128)} %param.20) | copy-start | bytes 772
  59.0 984.9 %reduce-scatter.17.cloned.1.call-start = ((), (), s32[]{:S(2)}) async-start(), calls=%async_computation.24 | async-start | bytes 17825792 | tf_op jit(solution)/shard_map/reduce_scatter | solution.py:265
  92.9 82.6 %copy-start.35 = (f32[128,16]{0,1:T(8,128)}, f32[128,16]{0,1:T(8,128)S(1)}, u32[]{:S(2)}) copy-start(f32[128,16]{0,1:T(8,128)S(1)} %get-tuple-element.293) | copy-start | bytes 24580
  199.8 92.7 %copy-start.10 = (bf16[2,1,64,1024]{3,2,1,0:T(8,128)(2,1)S(1)}, bf16[2,1,64,1024]{3,2,1,0:T(8,128)(2,1)}, u32[]{:S(2)}) copy-start(bf16[2,1,64,1024]{3,2,1,0:T(8,128)(2,1)} %param.17) | copy-start | bytes 786436
  199.9 94.9 %copy-start.40 = (f32[1024]{0:T(1024)S(1)}, f32[1024]{0:T(1024)}, u32[]{:S(2)}) copy-start(f32[1024]{0:T(1024)} %param.22) | copy-start | bytes 12292
  292.5 35.8 %copy-start.26 = (bf16[128,8,2,64]{0,3,2,1:T(8,128)(2,1)}, bf16[128,8,2,64]{0,3,2,1:T(8,128)(2,1)S(1)}, u32[]{:S(2)}) copy-start(bf16[128,8,2,64]{0,3,2,1:T(8,128)(2,1)S(1)} %bitcast_convert_fusion) | copy-start | bytes 786436
  294.7 287.4 %copy-start.3 = (f32[128,1024]{1,0:T(8,128)}, f32[128,1024]{1,0:T(8,128)S(1)}, u32[]{:S(2)}) copy-start(f32[128,1024]{1,0:T(8,128)S(1)} %get-tuple-element.305) | copy-start | bytes 1572868
  294.9 146.4 %copy-start.8 = (bf16[128,1024]{1,0:T(8,128)(2,1)}, bf16[128,1024]{1,0:T(8,128)(2,1)S(1)}, u32[]{:S(2)}) copy-start(bf16[128,1024]{1,0:T(8,128)(2,1)S(1)} %multiply_convert_fusion.3) | copy-start | bytes 786436
  328.3 232.6 %copy-start.29 = (bf16[2,1,64,1024]{3,2,1,0:T(8,128)(2,1)S(1)}, bf16[2,1,64,1024]{3,2,1,0:T(8,128)(2,1)}, u32[]{:S(2)}) copy-start(bf16[2,1,64,1024]{3,2,1,0:T(8,128)(2,1)} %param.18) | copy-start | bytes 786436
  441.3 137.1 %slice-start = ((s8[9437184]{0:T(1024)(128)(4,1)}), s8[1048576]{0:T(1024)(128)(4,1)S(1)}, s32[]{:S(2)}) async-start(s8[9437184]{0:T(1024)(128)(4,1)} %bitcast.236), calls=%async_computation.40 | async-start | bytes 2097152
  560.9 17.5 slice-start.1
  560.9 17.5 slice-start.2
  866.2 177.7 %copy-start.14 = (f32[128,1024]{1,0:T(8,128)S(1)}, f32[128,1024]{1,0:T(8,128)}, u32[]{:S(2)}) copy-start(f32[128,1024]{1,0:T(8,128)} %copy-done.13) | copy-start | bytes 1572868
  866.2 177.7 %copy-start.27 = (bf16[128,8,2,64]{0,3,2,1:T(8,128)(2,1)S(1)}, bf16[128,8,2,64]{0,3,2,1:T(8,128)(2,1)}, u32[]{:S(2)}) copy-start(bf16[128,8,2,64]{0,3,2,1:T(8,128)(2,1)} %copy-done.26) | copy-start | bytes 786436
  866.3 198.3 %reduce-scatter.19.cloned.1.call-start = ((), (), s32[]{:S(2)}) async-start(), calls=%async_computation.25 | async-start | bytes 1572864 | tf_op jit(solution)/shard_map/reduce_scatter | solution.py:266
  1043.9 97.3 %reduce-scatter.33.cloned.1.call-start = ((), (), s32[]{:S(2)}) async-start(), calls=%async_computation.32 | async-start | bytes 4456448 | tf_op jit(solution)/shard_map/reduce_scatter | solution.py:289
  1046.7 170.1 %reduce-scatter.21.cloned.1.call-start = ((), (), s32[]{:S(2)}) async-start(), calls=%async_computation.26 | async-start | bytes 4456448 | tf_op jit(solution)/shard_map/reduce_scatter | solution.py:286
  1050.9 16.8 copy-start.16
  1050.9 16.9 copy-start.42
  1050.9 231.0 %reduce-scatter.29.cloned.1.call-start = ((), (), s32[]{:S(2)}) async-start(), calls=%async_computation.30 | async-start | bytes 2228224 | tf_op jit(solution)/shard_map/reduce_scatter | solution.py:288
  1067.4 278.9 %reduce-scatter.25.cloned.1.call-start = ((), (), s32[]{:S(2)}) async-start(), calls=%async_computation.28 | async-start | bytes 2228224 | tf_op jit(solution)/shard_map/reduce_scatter | solution.py:287
  1069.9 473.9 %reduce-scatter.41.cloned.1.call-start = ((), (), s32[]{:S(2)}) async-start(), calls=%async_computation.36 | async-start | bytes 20054016 | tf_op jit(solution)/shard_map/reduce_scatter | solution.py:291
  1079.4 661.4 %reduce-scatter.37.cloned.1.call-start = ((), (), s32[]{:S(2)}) async-start(), calls=%async_computation.34 | async-start | bytes 20054016 | tf_op jit(solution)/shard_map/reduce_scatter | solution.py:290
  1089.1 848.9 %reduce-scatter.45.cloned.1.call-start = ((), (), s32[]{:S(2)}) async-start(), calls=%async_computation.38 | async-start | bytes 20054016 | tf_op jit(solution)/shard_map/reduce_scatter | solution.py:292
  1098.2 839.8 %copy-start.49 = (f32[128]{0:T(128)S(1)}, f32[128]{0:T(128)}, u32[]{:S(2)}) copy-start(f32[128]{0:T(128)} %copy-done.48) | copy-start | bytes 1540
  1098.2 842.2 %copy-start.4 = (f32[128,1024]{1,0:T(8,128)S(1)}, f32[128,1024]{1,0:T(8,128)}, u32[]{:S(2)}) copy-start(f32[128,1024]{1,0:T(8,128)} %copy-done.3) | copy-start | bytes 1572868
  1098.3 890.4 %reduce-scatter.35.cloned.1.call-start = ((), (), s32[]{:S(2)}) async-start(), calls=%async_computation.33 | async-start | bytes 393216 | tf_op jit(solution)/shard_map/reduce_scatter | solution.py:298
  1141.2 847.5 %reduce-scatter.23.cloned.1.call-start = ((), (), s32[]{:S(2)}) async-start(), calls=%async_computation.27 | async-start | bytes 393216 | tf_op jit(solution)/shard_map/reduce_scatter | solution.py:295
  1216.8 771.9 %reduce-scatter.31.cloned.1.call-start = ((), (), s32[]{:S(2)}) async-start(), calls=%async_computation.31 | async-start | bytes 196608 | tf_op jit(solution)/shard_map/reduce_scatter | solution.py:297
  1282.0 709.5 %reduce-scatter.27.cloned.1.call-start = ((), (), s32[]{:S(2)}) async-start(), calls=%async_computation.29 | async-start | bytes 196608 | tf_op jit(solution)/shard_map/reduce_scatter | solution.py:296
  1346.4 669.8 %reduce-scatter.43.cloned.1.call-start = ((), (), s32[]{:S(2)}) async-start(), calls=%async_computation.37 | async-start | bytes 1769472 | tf_op jit(solution)/shard_map/reduce_scatter | solution.py:300
  1543.8 497.1 %reduce-scatter.39.cloned.1.call-start = ((), (), s32[]{:S(2)}) async-start(), calls=%async_computation.35 | async-start | bytes 1769472 | tf_op jit(solution)/shard_map/reduce_scatter | solution.py:299
  1740.9 324.5 %reduce-scatter.47.cloned.1.call-start = ((), (), s32[]{:S(2)}) async-start(), calls=%async_computation.39 | async-start | bytes 1769472 | tf_op jit(solution)/shard_map/reduce_scatter | solution.py:301
  (42 other events, 257.6 us)
Sparse Core Ops, SparseCore 0:
  9.5 21.5 all-gather.8
  32.7 21.2 all-gather.10
  55.5 33.0 all-gather.14
  92.1 77.0 all-gather.12
  170.6 31.6 all-gather.16
  203.7 117.9 all-gather.20
  323.3 117.9 all-gather.18
  442.9 117.9 all-gather.22
  866.4 177.4 reduce-scatter.16
  1046.0 18.5 reduce-scatter.18
  1068.5 72.6 reduce-scatter.32
  1144.9 71.8 reduce-scatter.20
  1220.5 61.4 reduce-scatter.28
  1285.6 60.7 reduce-scatter.24
  1350.3 193.3 reduce-scatter.40
  1547.7 193.1 reduce-scatter.36
  1744.8 193.1 reduce-scatter.44
  1940.7 9.9 reduce-scatter.34
  1953.5 11.8 reduce-scatter.22
  1968.0 10.2 reduce-scatter.30
  1981.1 10.3 reduce-scatter.26
  1994.3 21.8 reduce-scatter.42
  2019.0 21.8 reduce-scatter.38
  2043.5 21.8 reduce-scatter.46
where the time goes:
time: 2090 us; the launch traced here: 2070 us
  waiting for transfers between devices  1510 us (72%)
  local copies, waits for them, and re-layouts  286 us (14%)
  matrix products  143 us (7%)
  other arithmetic  58.5 us (3%)
  blocking collectives  40 us (2%)
    reduce_scatter x1, waiting for transfers between devices, local(): lax.psum_scatter(d_w_up, 'ctx', scatter_dimension=0, tiled=True)  197 us
    reduce_scatter x1, waiting for transfers between devices, local(): lax.psum_scatter(d_w_down, 'ctx', scatter_dimension=0, tiled=True)  197 us
    reduce_scatter x1, waiting for transfers between devices, local(): lax.psum_scatter(d_w_gate, 'ctx', scatter_dimension=0, tiled=True)  197 us
    reduce_scatter x1, waiting for transfers between devices, local(): lax.psum_scatter(kv_terms, 'ctx', scatter_dimension=0, tiled=True)  178 us
    all_gather x1, waiting for transfers between devices, local(): lax.all_gather(w_gate, 'fsdp', axis=0, tiled=True)  113 us
    all_gather x1, waiting for transfers between devices, local(): lax.all_gather(w_down, 'fsdp', axis=0, tiled=True)  113 us
    dynamic_update_slice x10, local copies, waits for them, and re-layouts, backward_step(): lax.dynamic_update_slice_in_dim(terms_seq, old_terms + jnp.concatenate([g...  85.3 us
    all_gather x1, waiting for transfers between devices, local(): kv_all = lax.all_gather(kv_local, ('ctx', 'fsdp'), axis=0, tiled=True)  75.6 us
  transfers between devices with their start and end apart: 24, of which 20 were waited for; matrix products, arithmetic and copies ran while one was open for 9% of the time, Pallas kernels for 0%

commit v1 on v0

v1 whole, which is shorter than its diff:
```python
import functools
import math

import jax
import jax.numpy as jnp
from jax import lax
from jax.experimental import pallas as pl
from jax.experimental.pallas import tpu as pltpu
from jax.sharding import Mesh
from jax.sharding import PartitionSpec as P

EPS = 1e-05
ROPE_BASE = 1000000.0
F32 = jnp.float32
BF16 = jnp.bfloat16
HEAD = 64
BLOCK = 128
GROUP = ("inner", "fsdp")
EVERY = ("outer", "inner", "fsdp")


def dot(a, b, dims=((1,), (0,))):
    return lax.dot_general(a, b, (dims, ((), ())), preferred_element_type=F32)


def rms_forward(inputs, gain_vec):
    inverse = lax.rsqrt(jnp.mean(inputs * inputs, axis=-1, keepdims=True) + EPS)
    return (inputs * inverse * gain_vec, inverse)


def rms_backward(inputs, inverse, gain_vec, grad_out):
    scaled = grad_out * gain_vec
    inner_mean = jnp.mean(scaled * inputs, axis=-1, keepdims=True)
    grad_in = inverse * scaled - inputs * (inverse * inverse * inverse) * inner_mean
    grad_gain = jnp.sum((grad_out * inputs * inverse).reshape(-1, inputs.shape[-1]), axis=0)
    return (grad_in, grad_gain)


def rope_tables(positions, head_width):
    frequency = ROPE_BASE ** (-2.0 * jnp.arange(head_width // 2, dtype=F32) / head_width)
    angles = positions.astype(F32)[:, None] * frequency[None, :]
    cosine = jnp.concatenate([jnp.cos(angles), jnp.cos(angles)], axis=-1)[:, None, :]
    sine_tab = jnp.concatenate([jnp.sin(angles), jnp.sin(angles)], axis=-1)[:, None, :]
    return (cosine, sine_tab)


def rotate(inputs):
    half_width = inputs.shape[-1] // 2
    return jnp.concatenate([-inputs[..., half_width:], inputs[..., :half_width]], axis=-1)


def unrotate(inputs):
    half_width = inputs.shape[-1] // 2
    return jnp.concatenate([inputs[..., half_width:], -inputs[..., :half_width]], axis=-1)


SCORE = 1.0 / math.sqrt(HEAD)
SCORE2 = SCORE * math.log2(math.e)


def attn_fwd_kernel(steps, outer_ref, qt_ref, kv_ref, out_ref, total_ref):
    outer = outer_ref[0]
    half = kv_ref.shape[0] // (2 * steps)
    sub = half // 2
    wide = 2 * sub

    def block(rows, size, cols, mask, acc, total):
        kv = kv_ref[pl.ds(pl.multiple_of(rows, sub), size), :]
        probs = jnp.exp2(dot(kv, qt_ref[:, cols]) * SCORE2)
        if mask is not None:
            probs = jnp.where(mask, probs, 0.0)
        total = total + jnp.sum(probs.reshape(size // 8, 8, wide), axis=0)
        acc = acc + dot(kv, probs.astype(BF16), ((0,), (0,)))
        return acc, total

    key = lax.broadcasted_iota(jnp.int32, (sub, wide), 0)
    query = lax.broadcasted_iota(jnp.int32, (sub, wide), 1) % sub
    diagonal = key <= query
    for late in range(2):
        for part in range(2):
            cols = pl.ds((late * 2 + part) * wide, wide)

            def full(m, carry):
                if late:
                    rows = jnp.where(m < steps, m * 2, (outer + 1 + m - steps) * 2 + 1) * half
                else:
                    rows = m * 2 * half
                return block(rows, half, cols, None, *carry)

            count = 2 * steps - 1 - outer if late else outer
            own = (outer * 2 + late) * half
            carry = (jnp.zeros((2 * HEAD, wide), F32), jnp.zeros((8, wide), F32))
            carry = lax.fori_loop(0, count, full, carry)
            if part:
                carry = block(own, sub, cols, None, *carry)
            acc, total = block(own + part * sub, sub, cols, diagonal, *carry)
            total = jnp.sum(total, axis=0, keepdims=True)
            out_ref[:, cols] = acc[HEAD:] / total
            total_ref[:, cols] = jnp.log2(total)


def attn_bwd_kernel(
    steps, outer_ref, qt_ref, q_ref, gt_ref, g_ref, kv_ref, log_ref, delta_ref, dq_ref, dkv_ref
):
    outer = outer_ref[0]
    half = kv_ref.shape[0] // (2 * steps)
    sub = half // 2
    wide = 2 * sub
    dkv_ref[...] = jnp.zeros_like(dkv_ref)

    def block(rows, size, cols, mask, acc):
        rows = pl.ds(pl.multiple_of(rows, sub), size)
        kv = kv_ref[rows, :]
        probs = jnp.exp2(dot(kv, qt_ref[:, cols]) * SCORE2 - log_ref[:, cols])
        if mask is not None:
            probs = jnp.where(mask, probs, 0.0)
        grads = dot(kv, gt_ref[:, cols])
        grads = (probs * (grads - delta_ref[:, cols]) * SCORE).astype(BF16)
        dkv_ref[rows, :] += dot(grads, q_ref[cols, :]) + dot(probs.astype(BF16), g_ref[cols, :])
        return acc + dot(kv, grads, ((0,), (0,)))

    key = lax.broadcasted_iota(jnp.int32, (sub, wide), 0)
    query = lax.broadcasted_iota(jnp.int32, (sub, wide), 1) % sub
    diagonal = key <= query
    for late in range(2):
        for part in range(2):
            cols = pl.ds((late * 2 + part) * wide, wide)

            def full(m, acc):
                if late:
                    rows = jnp.where(m < steps, m * 2, (outer + 1 + m - steps) * 2 + 1) * half
                else:
                    rows = m * 2 * half
                return block(rows, half, cols, None, acc)

            count = 2 * steps - 1 - outer if late else outer
            own = (outer * 2 + late) * half
            acc = lax.fori_loop(0, count, full, jnp.zeros((2 * HEAD, wide), F32))
            if part:
                acc = block(own, sub, cols, None, acc)
            acc = block(own + part * sub, sub, cols, diagonal, acc)
            dq_ref[:, cols] = acc[:HEAD]


SMEM = pl.BlockSpec(memory_space=pltpu.SMEM)
VMEM = pl.BlockSpec(memory_space=pltpu.VMEM)


def attn_fwd(outer, qt, kv, steps):
    cols = qt.shape[1]
    work = kv.shape[0] * cols // 2
    return pl.pallas_call(
        functools.partial(attn_fwd_kernel, steps),
        out_shape=(
            jax.ShapeDtypeStruct((HEAD, cols), F32),
            jax.ShapeDtypeStruct((1, cols), F32),
        ),
        in_specs=[SMEM, VMEM, VMEM],
        out_specs=[VMEM, VMEM],
        cost_estimate=pl.CostEstimate(
            flops=work * 512, transcendentals=work, bytes_accessed=4 << 20
        ),
        name="attn_fwd",
    )(outer, qt, kv)


def attn_bwd(outer, qt, q, gt, g, kv, log_total, delta, steps):
    cols = qt.shape[1]
    work = kv.shape[0] * cols // 2
    return pl.pallas_call(
        functools.partial(attn_bwd_kernel, steps),
        out_shape=(
            jax.ShapeDtypeStruct((HEAD, cols), F32),
            jax.ShapeDtypeStruct(kv.shape, F32),
        ),
        in_specs=[SMEM] + [VMEM] * 7,
        out_specs=[VMEM, VMEM],
        cost_estimate=pl.CostEstimate(
            flops=work * 1280, transcendentals=work, bytes_accessed=8 << 20
        ),
        name="attn_bwd",
    )(outer, qt, q, gt, g, kv, log_total, delta)


def swap(array, axis_size):
    return lax.ppermute(array, "fsdp", [(k, (k + 1) % axis_size) for k in range(axis_size)])


def local(
    block_input, dy, attn_gain, q_gain, k_gain, ffn_gain, wq, wk, wv, wo, w_gate, w_up, w_down
):
    steps = lax.axis_size("outer")
    inner_size = lax.axis_size("inner")
    fsdp_size = lax.axis_size("fsdp")
    outer = lax.axis_index("outer")
    inner = lax.axis_index("inner")
    fsdp = lax.axis_index("fsdp")
    group = inner_size * fsdp_size
    lane = fsdp * inner_size + inner
    part = block_input.shape[2]
    width = block_input.shape[3]
    block_len = part * fsdp_size
    rows = 2 * part
    half = inner_size * block_len
    pairs = steps * inner_size
    kv_heads = group

    def gather(arr):
        arr = lax.all_gather(arr.reshape(2, part, -1), GROUP, axis=0, tiled=False)
        arr = arr.reshape(inner_size, fsdp_size, 2, part, -1)
        early = arr[:, :, 0].reshape(half, -1)
        late = arr[::-1, :, 1].reshape(half, -1)
        return jnp.concatenate([early, late], axis=0)

    def by_device(arr):
        early = arr[:half].reshape(inner_size, fsdp_size, part, -1)
        late = arr[half:].reshape(inner_size, fsdp_size, part, -1)[::-1]
        return jnp.stack([early, late], axis=2).reshape(group, rows, -1)

    def scatter(arr):
        return lax.psum_scatter(by_device(arr), GROUP, scatter_dimension=0, tiled=False)

    def heads_to_tokens(arr):
        got = lax.all_to_all(by_device(arr), GROUP, split_axis=0, concat_axis=0, tiled=True)
        got = got.reshape(inner_size, fsdp_size, rows, -1)
        return jnp.transpose(got, (2, 1, 0, 3)).reshape(rows, -1)

    def tokens_to_heads(arr):
        cut = arr.reshape(rows, fsdp_size, inner_size, -1)
        cut = jnp.transpose(cut, (2, 1, 0, 3)).reshape(group, rows, -1)
        got = lax.all_to_all(cut, GROUP, split_axis=0, concat_axis=0, tiled=True)
        got = got.reshape(inner_size, fsdp_size, 2, part, -1)
        early = got[:, :, 0].reshape(half, -1)
        late = got[::-1, :, 1].reshape(half, -1)
        return jnp.concatenate([early, late], axis=0)

    def join(mine, other):
        return jnp.where(
            fsdp == 0,
            jnp.concatenate([mine, other], axis=0),
            jnp.concatenate([other, mine], axis=0),
        )

    def cols_of(arr, start, size):
        return lax.dynamic_slice_in_dim(arr, start, size, 1)

    def slice_exchange(arr, start, other_start, size):
        mine = cols_of(arr, start, size)
        return join(mine, swap(cols_of(arr, other_start, size), fsdp_size))

    other_lane = (1 - fsdp) * inner_size + inner

    qkv = lambda n: jnp.concatenate(
        [
            cols_of(wq, n * 2 * HEAD, 2 * HEAD),
            cols_of(wk, n * HEAD, HEAD),
            cols_of(wv, n * HEAD, HEAD),
        ],
        axis=1,
    )
    w_qkv = join(qkv(lane), swap(qkv(other_lane), fsdp_size))
    wo_all = join(wo, swap(wo, fsdp_size))
    ff = w_gate.shape[1]
    tiles = 2 * ff // group // BLOCK
    reach = (tiles + 1) // 2 * BLOCK
    own_ff = ff // group
    step_ff = (tiles // 2) * BLOCK

    def ff_start(f):
        return ((f * inner_size + inner) // 2) * tiles * BLOCK + (inner % 2) * step_ff

    gate_w = slice_exchange(w_gate, ff_start(fsdp), ff_start(1 - fsdp), reach)
    up_w = slice_exchange(w_up, ff_start(fsdp), ff_start(1 - fsdp), reach)
    down_start = (inner // 2) * tiles * BLOCK + (inner % 2) * step_ff
    down_w = lax.dynamic_slice_in_dim(w_down, down_start, reach, 0)
    col = jnp.arange(reach, dtype=jnp.int32)
    pad = reach - own_ff
    valid = jnp.where(inner % 2 == 0, col < own_ff, col >= pad)[None, :]

    wq_all = join(wq, swap(wq, fsdp_size))
    wk_all = join(wk, swap(wk, fsdp_size))
    wv_all = join(wv, swap(wv, fsdp_size))

    inputs = block_input.reshape(rows, width).astype(F32)
    cotangent = dy.reshape(rows, width)
    cot_group = gather(cotangent)
    normed, inverse_in = rms_forward(inputs, attn_gain)
    normed_group = gather(normed.astype(BF16))
    proj = dot(normed_group, w_qkv)
    queries = proj[:, : 2 * HEAD].reshape(2 * half, 2, HEAD)
    key_unnormed = proj[:, 2 * HEAD : 3 * HEAD].reshape(2 * half, 1, HEAD)
    value_rows = proj[:, 3 * HEAD :].astype(BF16)
    q_normed, q_inverse = rms_forward(queries, q_gain)
    k_normed, k_inverse = rms_forward(key_unnormed, k_gain)
    within = jnp.arange(half, dtype=jnp.int32)
    positions = jnp.concatenate(
        [outer * half + within, (2 * steps - 1 - outer) * half + within], axis=0
    )
    cosine, sine_tab = rope_tables(positions, HEAD)
    q_rot = (q_normed * cosine + rotate(q_normed) * sine_tab).astype(BF16)
    k_rot = (k_normed * cosine + rotate(k_normed) * sine_tab).astype(BF16)
    kv_own = jnp.concatenate([k_rot[:, 0], value_rows], axis=1)
    kv = lax.all_gather(kv_own, "outer", axis=0, tiled=True)

    sub = half // 2

    def to_cols(arr):
        return jnp.transpose(arr.reshape(2, 2, sub, 2, -1), (0, 1, 3, 2, 4)).reshape(4 * half, -1)

    def from_cols(arr):
        return jnp.transpose(arr.reshape(2, 2, 2, sub, -1), (0, 1, 3, 2, 4)).reshape(2 * half, -1)

    q_cols = jnp.pad(to_cols(q_rot), ((0, 0), (0, HEAD)))
    q_t = q_cols.T
    outer_arr = outer.reshape(1)
    attn_t, log2_total = attn_fwd(outer_arr, q_t, kv, steps)
    attn = from_cols(attn_t.T)
    attn_bf = attn.astype(BF16)
    attn_rows = heads_to_tokens(attn_bf)
    residual = inputs + dot(attn_rows, wo_all)
    ffn_normed, inverse_ffn = rms_forward(residual, ffn_gain)
    ffn_in = gather(ffn_normed.astype(BF16))
    gate_pre = dot(ffn_in, gate_w)
    up_pre = dot(ffn_in, up_w)
    sigmoid_gate = jax.nn.sigmoid(gate_pre)
    silu_gate = gate_pre * sigmoid_gate
    hidden = jnp.where(valid, silu_gate * up_pre, 0.0).astype(BF16)
    result = residual + scatter(dot(hidden, down_w))

    d_hidden = jnp.where(valid, dot(cot_group, down_w, ((1,), (1,))), 0.0)
    d_gate = (d_hidden * up_pre * sigmoid_gate * (1.0 + gate_pre * (1.0 - sigmoid_gate))).astype(
        BF16
    )
    d_up = (d_hidden * silu_gate).astype(BF16)
    d_ffn_in = scatter(dot(d_gate, gate_w, ((1,), (1,))) + dot(d_up, up_w, ((1,), (1,))))
    d_w_down = dot(hidden, cot_group, ((0,), (0,)))
    d_w_gate = dot(ffn_in, d_gate, ((0,), (0,)))
    d_w_up = dot(ffn_in, d_up, ((0,), (0,)))
    d_res_norm, d_ffn_gain = rms_backward(residual, inverse_ffn, ffn_gain, d_ffn_in)
    d_residual = cotangent.astype(F32) + d_res_norm
    d_res_bf = d_residual.astype(BF16)
    attn_grad = tokens_to_heads(dot(d_res_bf, wo_all, ((1,), (1,))).astype(BF16))
    d_res_group = gather(d_res_bf)
    d_wo = dot(attn_bf, d_res_group, ((0,), (0,)))
    delta = jnp.sum((attn_grad.astype(F32) * attn).reshape(2 * half, 2, HEAD), axis=-1)
    g_cols = jnp.pad(to_cols(attn_grad.reshape(2 * half, 2, HEAD)), ((0, 0), (HEAD, 0)))
    delta_cols = to_cols(delta[..., None]).reshape(1, 4 * half)
    dq_t, d_kv = attn_bwd(
        outer_arr, q_t, q_cols, g_cols.T, g_cols, kv, log2_total, delta_cols, steps
    )
    d_kv = lax.psum_scatter(d_kv, "outer", scatter_dimension=0, tiled=True)
    grad_q_rot = from_cols(dq_t.T).reshape(2 * half, 2, HEAD)
    grad_k_rot = d_kv[:, :HEAD].reshape(2 * half, 1, HEAD)
    d_q_normed = grad_q_rot * cosine + unrotate(grad_q_rot * sine_tab)
    d_queries, d_q_gain = rms_backward(queries, q_inverse, q_gain, d_q_normed)
    d_k_normed = grad_k_rot * cosine + unrotate(grad_k_rot * sine_tab)
    d_keys, d_k_gain = rms_backward(key_unnormed, k_inverse, k_gain, d_k_normed)
    d_qkv = jnp.concatenate(
        [d_queries.reshape(2 * half, 2 * HEAD), d_keys[:, 0], d_kv[:, HEAD:]], axis=1
    ).astype(BF16)
    d_w_qkv = dot(normed_group, d_qkv, ((0,), (0,)))
    rows_qkv = heads_to_tokens(d_qkv).reshape(rows, group, 4 * HEAD)
    dq_rows = rows_qkv[:, :, : 2 * HEAD].reshape(rows, -1)
    dk_rows = rows_qkv[:, :, 2 * HEAD : 3 * HEAD].reshape(rows, -1)
    dv_rows = rows_qkv[:, :, 3 * HEAD :].reshape(rows, -1)
    d_normed = dot(dq_rows, wq_all, ((1,), (1,)))
    d_normed = d_normed + dot(dk_rows, wk_all, ((1,), (1,)))
    d_normed = d_normed + dot(dv_rows, wv_all, ((1,), (1,)))
    d_inputs, d_attn_gain = rms_backward(inputs, inverse_in, attn_gain, d_normed)
    grad_in = d_residual + d_inputs

    def rows_out(arr):
        part_sum = lax.psum_scatter(arr, "outer", scatter_dimension=0, tiled=True)
        got = lax.all_to_all(part_sum, GROUP, split_axis=0, concat_axis=0, tiled=True)
        got = got.reshape(inner_size, fsdp_size, -1, arr.shape[1])
        return jnp.transpose(got, (1, 0, 2, 3)).reshape(group, -1, arr.shape[1])

    def windows(arr):
        pair = arr.reshape(group // 2, 2, arr.shape[1], reach)
        first, second = pair[:, 0], pair[:, 1]
        whole = jnp.concatenate(
            [
                first[..., :step_ff],
                first[..., step_ff:] + second[..., : reach - step_ff],
                second[..., reach - step_ff :],
            ],
            axis=-1,
        )
        return jnp.transpose(whole, (1, 0, 2)).reshape(arr.shape[1], ff)

    own_gate = windows(rows_out(d_w_gate))
    own_up = windows(rows_out(d_w_up))
    own_qkv = jnp.transpose(rows_out(d_w_qkv), (1, 0, 2))
    own_q = own_qkv[:, :, : 2 * HEAD].reshape(-1, wq.shape[1])
    own_k = own_qkv[:, :, 2 * HEAD : 3 * HEAD].reshape(-1, wk.shape[1])
    own_v = own_qkv[:, :, 3 * HEAD :].reshape(-1, wv.shape[1])
    down_rows = lax.dynamic_slice_in_dim(d_w_down, jnp.where(inner % 2 == 0, 0, pad), own_ff, 0)
    down_sum = lax.psum_scatter(down_rows, "outer", scatter_dimension=0, tiled=True)
    wo_sum = lax.psum_scatter(d_wo, "outer", scatter_dimension=0, tiled=True)
    moves = []
    for z in range(steps):
        for i in range(inner_size):
            for f in range(fsdp_size):
                moves.append((z * group + i * fsdp_size + f, steps * (f * inner_size + i) + z))
    moved = lax.ppermute(jnp.concatenate([down_sum, wo_sum], axis=0), EVERY, moves)
    own_down = moved[: down_sum.shape[0]]
    own_o = moved[down_sum.shape[0] :]
    gains = lax.psum(
        jnp.concatenate([d_attn_gain, d_ffn_gain, jnp.pad(d_q_gain, (0, 0)), d_k_gain]), EVERY
    )
    return (
        result.astype(BF16).reshape(block_input.shape),
        grad_in.reshape(block_input.shape),
        gains[:width],
        gains[2 * width : 2 * width + HEAD],
        gains[2 * width + HEAD :],
        gains[width : 2 * width],
        own_q,
        own_k,
        own_v,
        own_o,
        own_gate,
        own_up,
        own_down,
    )


def solution(mesh):
    ctx, fsdp = mesh.shape["ctx"], mesh.shape["fsdp"]
    inner = 8 // fsdp
    grid = Mesh(mesh.devices.reshape(ctx // inner, inner, fsdp), EVERY)
    tokens = P(None, ("outer", "inner"), "fsdp", None)
    shard = P("fsdp", None)
    owned = P(EVERY, None)
    return jax.shard_map(
        local,
        mesh=grid,
        in_specs=(tokens, tokens) + (P(),) * 4 + (shard,) * 7,
        out_specs=(tokens, tokens) + (P(),) * 4 + (owned,) * 7,
        check_vma=False,
    )
```

time: 2090 us -> 670 us (0.32)
  waiting for transfers between devices: 1510 us -> 269 us
  local copies, waits for them, and re-layouts: 286 us -> 117 us
  matrix products: 143 us -> 62.5 us
  blocking collectives: 40 us -> 83.7 us
  starting transfers between devices: 1.2 us -> 34.4 us
  Pallas kernels: 0 us -> 28.1 us
    reduce_scatter x16 -> x8, waiting for transfers between devices: 1110 us -> 211 us  [the longest x2 85.3 us: scatter(): lax.psum_scatter(by_device(arr), GROUP, scatter_dimension=0, tiled=False)]
    all_gather x8 -> x5, waiting for transfers between devices: 396 us -> 51.9 us  [the longest x4 41 us: gather(): arr = lax.all_gather(arr.reshape(2, part, -1), GROUP, axis=0, tiled=False)]
    dynamic_update_slice x30 -> x0, local copies, waits for them, and re-layouts: 132 us -> none  [the longest x10 85.3 us: backward_step(): lax.dynamic_update_slice_in_dim(terms_seq, old_terms + jnp.concatenate([g...]
    dot_general x56 -> x17, matrix products: 143 us -> 62.5 us  [dot(): return lax.dot_general(a, b, (dims, ((), ())), preferred_element_type=F32)]
    dynamic_slice x35 -> x6, local copies, waits for them, and re-layouts: 60 us -> 9.69 us  [the longest x5 8.14 us: cols_of(): return lax.dynamic_slice_in_dim(arr, start, size, 1)]
    psum x1, blocking collectives: 40 us -> 75.1 us  [local(): lax.psum(jnp.concatenate([d_attn_gain, d_ffn_gain, jnp.pad(d_q_gain, (0,...]
    add x22 -> x4, other arithmetic: 30.7 us -> 1.5 us  [the longest x2 1.49 us: windows(): first[..., step_ff:] + second[..., :reach - step_ff]]
    pallas_call x0 -> x2, Pallas kernels: none -> 28.1 us  [the longest x1 17.1 us: attn_bwd(): pl.pallas_call(functools.partial(attn_bwd_kernel, steps), out_shape=(jax....]
  transfers between devices with their start and end apart: 24 -> 26, of which waited for: 20 -> 12; matrix products, arithmetic and copies ran while one was open for 9% -> 30% of each run, Pallas kernels for 0% -> 4%
where the time goes in v1:
time: 670 us; the launch traced here: 657 us
  waiting for transfers between devices  269 us (40%)
  local copies, waits for them, and re-layouts  117 us (17%)
  blocking collectives  83.7 us (12%)
  matrix products  62.5 us (9%)
  other arithmetic  47.1 us (7%)
  starting transfers between devices  34.4 us (5%)
  Pallas kernels  28.1 us (4%)
  between operations  15.2 us (2%)
    reduce_scatter x2, waiting for transfers between devices, scatter(): lax.psum_scatter(by_device(arr), GROUP, scatter_dimension=0, tiled=False)  85.3 us
    psum x1, blocking collectives, local(): lax.psum(jnp.concatenate([d_attn_gain, d_ffn_gain, jnp.pad(d_q_gain, (0,...  75.1 us
    dot_general x17, matrix products, dot(): return lax.dot_general(a, b, (dims, ((), ())), preferred_element_type=F32)  62.5 us
    all_gather x4, waiting for transfers between devices, gather(): arr = lax.all_gather(arr.reshape(2, part, -1), GROUP, axis=0, tiled=False)  41 us
    reduce_scatter x1, waiting for transfers between devices, local(): d_kv = lax.psum_scatter(d_kv, 'outer', scatter_dimension=0, tiled=True)  40 us
    reduce_scatter x3, waiting for transfers between devices, rows_out(): part_sum = lax.psum_scatter(arr, 'outer', scatter_dimension=0, tiled=True)  39.1 us
    reduce_scatter x1, waiting for transfers between devices, local(): wo_sum = lax.psum_scatter(d_wo, 'outer', scatter_dimension=0, tiled=True)  23.3 us
    reduce_scatter x1, waiting for transfers between devices, local(): lax.psum_scatter(down_rows, 'outer', scatter_dimension=0, tiled=True)  23.3 us
  transfers between devices with their start and end apart: 26, of which 12 were waited for; matrix products, arithmetic and copies ran while one was open for 30% of the time, Pallas kernels for 4%

profile of v1, /device:TPU:6, one launch (start us, length us, event | category | flops | bytes accessed | tf_op | source)
XLA Modules:
  0.0 656.5 jit_solution(12741346074597970728)
XLA Ops:
  16.1 23.4 %all-gather.7.cloned.1.call-done = bf16[8,2,64,1024]{3,2,1,0:T(8,128)(2,1)} async-done(((bf16[1,2,64,1024]{3,2,1,0:T(8,128)(2,1)}), bf16[8,2,64,1024]{3,2,1,0:T(8,128)(2,1)}) %all-gather.7.cloned.1.call-update) | async-done | bytes 2097168 | tf_op jit(solution)/shard_map/all_gather | solution.py:209
  39.5 2.8 fusion.107
  43.4 2.4 fusion.15
  67.3 10.9 %all-gather.9.cloned.1.call-done.kv_ref = bf16[4096,128]{1,0:T(8,128)(2,1)} async-done(((bf16[1024,128]{1,0:T(8,128)(2,1)}), bf16[4096,128]{1,0:T(8,128)(2,1)}) %all-gather.9.cloned.1.call-update) | async-done | bytes 1048592 | tf_op jit(solution)/shard_map/all_gather | solution.py:303
  78.3 11.1 %attn_fwd.1 = (f32[64,2048]{1,0:T(8,128)}, f32[1,2048]{1,0:T(1,128)}) custom-call(s32[1]{0:T(128)} %bitcast.2.outer_ref, bf16[128,2048]{1,0:T(8,128)(2,1)} %copy.191.qt_ref, bf16[4096,128]{1,0:T(8,128)(2,1)} %all-gather.9.cloned.1.call-done.kv_ref), custom_call_target="tpu_custom_call" | custom-call | flops 2147483648 | bytes 4194304 | tf_op jit(solution)/shard_map/attn_fwd/pallas_call | solution.py:152
  101.8 4.5 all-to-all-start
  107.1 3.8 all-to-all-done
  112.7 3.4 multiply_reduce_fusion.4
  117.9 2.5 constant_dynamic-slice_fusion.2
  121.2 2.5 constant_dynamic-slice_fusion.4
  124.8 3.2 fusion.105
  128.0 2.3 rev.31
  130.3 5.2 fusion.13
  135.5 17.1 %all-gather.11.cloned.1.call-done = bf16[8,2,64,1024]{3,2,1,0:T(8,128)(2,1)} async-done(((bf16[1,2,64,1024]{3,2,1,0:T(8,128)(2,1)}), bf16[8,2,64,1024]{3,2,1,0:T(8,128)(2,1)}) %all-gather.11.cloned.1.call-update) | async-done | bytes 2097168 | tf_op jit(solution)/shard_map/all_gather | solution.py:209
  152.6 3.1 fusion.106
  155.7 2.3 rev.29
  158.1 4.3 fusion.78
  162.4 5.3 multiply_convert_fusion.1
  167.7 4.1 fusion.77
  171.8 3.2 convolution_add_fusion
  175.8 2.3 pad_maximum_fusion.1
  178.6 3.5 fusion.19
  183.0 2.3 pad_maximum_fusion
  185.4 5.5 fusion.100
  190.9 5.6 fusion.99
  196.6 32.8 %reduce-scatter.11.cloned.1.call-done = f32[1,128,1024]{2,1,0:T(8,128)} async-done(((f32[8,128,1024]{2,1,0:T(8,128)}), f32[1,128,1024]{2,1,0:T(8,128)}) %reduce-scatter.11.cloned.1.call-update) | async-done | bytes 524304 | tf_op jit(solution)/shard_map/reduce_scatter | solution.py:221
  231.4 52.4 %reduce-scatter.9.cloned.1.call-done = f32[1,128,1024]{2,1,0:T(8,128)} async-done(((f32[8,128,1024]{2,1,0:T(8,128)}), f32[1,128,1024]{2,1,0:T(8,128)}) %reduce-scatter.9.cloned.1.call-update) | async-done | bytes 524304 | tf_op jit(solution)/shard_map/reduce_scatter | solution.py:221
  283.9 2.6 fusion.101
  286.6 3.9 convolution_convert_fusion
  293.3 8.6 %all_to_all.42 = bf16[8,128,128]{2,1,0:T(8,128)(2,1)S(1)} all-to-all(bf16[8,128,128]{2,1,0:T(8,128)(2,1)S(1)} %bitcast.312), channel_id=1, replica_groups=mesh['outer'=4,'inner'=4,'fsdp'=2] {'inner','fsdp'}, dimensions={0} | all-to-all | bytes 524288 | tf_op jit(solution)/shard_map/all_to_all | solution.py:231
  311.8 2.3 fusion.111
  321.7 2.3 reshape.488
  326.2 17.1 %attn_bwd.1 = (f32[64,2048]{1,0:T(8,128)}, f32[4096,128]{1,0:T(8,128)}) custom-call(s32[1]{0:T(128)} %bitcast.2.outer_ref, bf16[128,2048]{1,0:T(8,128)(2,1)} %copy.191.qt_ref, bf16[2048,128]{1,0:T(8,128)(2,1)} %get-tuple-element.135.q_ref, bf16[128,2048]{1,0:T(8,128)(2,1)} %copy.209.gt_ref, bf16[2048,128]{1,0:T(8,128)(2,1)} %get-tuple-element.133.g_ref, ...), custom_call_target="tpu_custom_call" | custom-call | flops 5368709120 | bytes 8388608 | tf_op jit(solution)/shard_map/attn_bwd/pallas_call | solution.py:170
  343.4 3.5 fusion.12
  348.5 6.0 all-to-all-start.4
  354.5 39.1 %reduce-scatter.23.cloned.1.call-done = f32[256,640]{1,0:T(8,128)} async-done(((f32[1024,640]{1,0:T(8,128)}), f32[256,640]{1,0:T(8,128)}) %reduce-scatter.23.cloned.1.call-update) | async-done | bytes 655376 | tf_op jit(solution)/shard_map/reduce_scatter | solution.py:373
  393.5 4.6 all-to-all-start.5
  406.3 2.3 reshape.474
  430.3 2.8 fusion.104
  434.2 2.9 fusion.7
  437.0 40.0 %reduce-scatter.13.cloned.1.call-done = f32[1024,128]{1,0:T(8,128)} async-done(((f32[4096,128]{1,0:T(8,128)}), f32[1024,128]{1,0:T(8,128)}) %reduce-scatter.13.cloned.1.call-update) | async-done | bytes 524304 | tf_op jit(solution)/shard_map/reduce_scatter | solution.py:351
  485.9 4.6 all-to-all-start.2
  490.8 3.0 fusion.14
  503.0 23.3 %reduce-scatter.17.cloned.1.call-done = f32[144,1024]{1,0:T(8,128)} async-done(((f32[576,1024]{1,0:T(8,128)}), f32[144,1024]{1,0:T(8,128)}) %reduce-scatter.17.cloned.1.call-update) | async-done | bytes 589840 | tf_op jit(solution)/shard_map/reduce_scatter | solution.py:398
  526.3 23.3 %reduce-scatter.19.cloned.1.call-done = f32[32,1024]{1,0:T(8,128)} async-done(((f32[128,1024]{1,0:T(8,128)}), f32[32,1024]{1,0:T(8,128)}) %reduce-scatter.19.cloned.1.call-update) | async-done | bytes 131088 | tf_op jit(solution)/shard_map/reduce_scatter | solution.py:399
  558.8 2.9 fusion.73
  561.8 75.1 %psum.7 = f32[2176]{0:T(1024)S(1)} all-reduce(f32[2176]{0:T(1024)S(1)} %concatenate.192), channel_id=1, replica_groups=mesh['outer'=4,'inner'=4,'fsdp'=2] {'outer','inner','fsdp'}, use_global_device_ids=true, to_apply=%region_16.17 | all-reduce | flops 2176 | bytes 17408 | tf_op jit(solution)/shard_map/psum | solution.py:408
  637.9 4.7 all-to-all-start.3
  (303 shorter events, 144.7 us)
Async XLA Ops:
  7.2 32.4 %all-gather.7.cloned.1.call-start = ((), (), s32[]{:S(2)}) async-start(), calls=%async_computation.14 | async-start | bytes 2359296 | tf_op jit(solution)/shard_map/all_gather | solution.py:209
  10.1 68.1 %all-gather.9.cloned.1.call-start = ((), (), s32[]{:S(2)}) async-start(), calls=%async_computation.15 | async-start | bytes 1310720 | tf_op jit(solution)/shard_map/all_gather | solution.py:303
  13.6 29.8 %collective-permute-start = (bf16[512,256]{1,0:T(8,128)(2,1)S(1)}, bf16[512,256]{1,0:T(8,128)(2,1)S(1)}, u32[]{:S(2)}, u32[]{:S(2)}) collective-permute-start(bf16[512,256]{1,0:T(8,128)(2,1)S(1)} %pad_maximum_fusion.15), channel_id=1, source_target_pairs={{0,1},{1,0},{2,3},{3,2},{4,5},{5,4},{6,7},{7,6},{8,9},{9,8},{10,11... | collective-permute-start | bytes 786440 | tf_op jit(solution)/shard_map/ppermute | solution.py:186
  16.1 30.8 %copy-start = (f32[1024,32]{1,0:T(8,128)}, f32[1024,32]{1,0:T(8,128)S(1)}, u32[]{:S(2)}) copy-start(f32[1024,32]{1,0:T(8,128)S(1)} %get-tuple-element.159) | copy-start | bytes 393220
  48.3 7.0 %copy-start.38 = (f32[64]{0:T(128)S(1)}, f32[64]{0:T(128)}, u32[]{:S(2)}) copy-start(f32[64]{0:T(128)} %param.16) | copy-start | bytes 772
  49.2 75.6 %all-gather.15.cloned.1.call-start = ((), (), s32[]{:S(2)}) async-start(), calls=%async_computation.26 | async-start | bytes 2359296 | tf_op jit(solution)/shard_map/all_gather | solution.py:209
  49.2 63.5 %collective-permute-start.1 = (bf16[512,1024]{1,0:T(8,128)(2,1)}, bf16[512,1024]{1,0:T(8,128)(2,1)}, u32[]{:S(2)}, u32[]{:S(2)}) collective-permute-start(bf16[512,1024]{1,0:T(8,128)(2,1)} %param.22), channel_id=1, source_target_pairs={{0,1},{1,0},{2,3},{3,2},{4,5},{5,4},{6,7},{7,6},{8,9},{9,8},{10,11... | collective-permute-start | bytes 3145736 | tf_op jit(solution)/shard_map/ppermute | solution.py:186
  92.9 13.4 %copy-start.5 = (bf16[2,1,64,1024]{3,2,1,0:T(8,128)(2,1)S(1)}, bf16[2,1,64,1024]{3,2,1,0:T(8,128)(2,1)}, u32[]{:S(2)}) copy-start(bf16[2,1,64,1024]{3,2,1,0:T(8,128)(2,1)} %param.13) | copy-start | bytes 786436
  101.8 9.2 %all-to-all-start = ((bf16[8,128,128]{2,1,0:T(8,128)(2,1)}), bf16[8,128,128]{2,1,0:T(8,128)(2,1)}, u32[]{:S(2)}, u32[]{:S(2)}) async-start(bf16[8,128,128]{2,1,0:T(8,128)(2,1)} %bitcast.309), calls=%async_computation | async-start | bytes 524288 | tf_op jit(solution)/shard_map/all_to_all | solution.py:224
  106.3 46.4 %all-gather.11.cloned.1.call-start = ((), (), s32[]{:S(2)}) async-start(), calls=%async_computation.16 | async-start | bytes 2359296 | tf_op jit(solution)/shard_map/all_gather | solution.py:209
  112.7 4.2 copy-start.31
  117.8 111.7 %reduce-scatter.11.cloned.1.call-start = ((), (), s32[]{:S(2)}) async-start(), calls=%async_computation.18 | async-start | bytes 4718592 | tf_op jit(solution)/shard_map/reduce_scatter | solution.py:221
  120.3 37.7 %collective-permute-start.3 = (bf16[512,640]{1,0:T(8,128)(2,1)}, bf16[512,640]{1,0:T(8,128)(2,1)}, u32[]{:S(2)}, u32[]{:S(2)}) collective-permute-start(bf16[512,640]{1,0:T(8,128)(2,1)} %get-tuple-element.101), channel_id=1, source_target_pairs={{0,1},{1,0},{2,3},{3,2},{4,5},{5,4},{6,7},{7,6},{8,9},{9,8},{10,11... | collective-permute-start | bytes 1966088 | tf_op jit(solution)/shard_map/ppermute | solution.py:186
  123.6 38.7 %collective-permute-start.2 = (bf16[512,640]{1,0:T(8,128)(2,1)}, bf16[512,640]{1,0:T(8,128)(2,1)}, u32[]{:S(2)}, u32[]{:S(2)}) collective-permute-start(bf16[512,640]{1,0:T(8,128)(2,1)} %get-tuple-element.99), channel_id=1, source_target_pairs={{0,1},{1,0},{2,3},{3,2},{4,5},{5,4},{6,7},{7,6},{8,9},{9,8},{10,11... | collective-permute-start | bytes 1966088 | tf_op jit(solution)/shard_map/ppermute | solution.py:186
  158.1 4.3 copy-start.7
  158.1 4.3 copy-start.20
  158.1 4.3 copy-start.25
  158.1 4.3 copy-start.46
  162.4 5.3 copy-start.26
  167.7 4.1 copy-start.18
  178.2 105.7 %reduce-scatter.9.cloned.1.call-start = ((), (), s32[]{:S(2)}) async-start(), calls=%async_computation.17 | async-start | bytes 4718592 | tf_op jit(solution)/shard_map/reduce_scatter | solution.py:221
  185.3 163.2 %reduce-scatter.21.cloned.1.call-start = ((), (), s32[]{:S(2)}) async-start(), calls=%async_computation.24 | async-start | bytes 3276800 | tf_op jit(solution)/shard_map/reduce_scatter | solution.py:373
  190.9 202.6 %reduce-scatter.23.cloned.1.call-start = ((), (), s32[]{:S(2)}) async-start(), calls=%async_computation.25 | async-start | bytes 3276800 | tf_op jit(solution)/shard_map/reduce_scatter | solution.py:373
  196.6 233.7 %all-gather.13.cloned.1.call-start = ((), (), s32[]{:S(2)}) async-start(), calls=%async_computation.22 | async-start | bytes 2359296 | tf_op jit(solution)/shard_map/all_gather | solution.py:209
  286.5 190.5 %reduce-scatter.13.cloned.1.call-start = ((), (), s32[]{:S(2)}) async-start(), calls=%async_computation.19 | async-start | bytes 2621440 | tf_op jit(solution)/shard_map/reduce_scatter | solution.py:351
  307.9 10.0 %copy-start.27 = (bf16[4,2,1,64,128]{4,3,1,0,2:T(8,128)(2,1)S(1)}, bf16[4,2,1,64,128]{4,3,1,0,2:T(8,128)(2,1)}, u32[]{:S(2)}) copy-start(bf16[4,2,1,64,128]{4,3,1,0,2:T(8,128)(2,1)} %get-tuple-element.148) | copy-start | bytes 393220
  343.3 182.9 %reduce-scatter.17.cloned.1.call-start = ((), (), s32[]{:S(2)}) async-start(), calls=%async_computation.21 | async-start | bytes 2949120 | tf_op jit(solution)/shard_map/reduce_scatter | solution.py:398
  348.5 52.3 %copy-start.41 = (f32[2,64]{1,0:T(2,128)S(1)}, f32[2,64]{1,0:T(2,128)}, u32[]{:S(2)}) copy-start(f32[2,64]{1,0:T(2,128)} %copy-done.40) | copy-start | bytes 1540
  348.5 52.4 %copy-start.39 = (f32[64]{0:T(128)S(1)}, f32[64]{0:T(128)}, u32[]{:S(2)}) copy-start(f32[64]{0:T(128)} %param.16) | copy-start | bytes 772
  348.5 45.0 %all-to-all-start.4 = ((f32[8,32,640]{2,1,0:T(8,128)}), f32[8,32,640]{2,1,0:T(8,128)}, u32[]{:S(2)}, u32[]{:S(2)}) async-start(f32[8,32,640]{2,1,0:T(8,128)} %bitcast.325), calls=%async_computation.11 | async-start | bytes 1310720 | tf_op jit(solution)/shard_map/all_to_all | solution.py:374
  393.5 21.2 %all-to-all-start.5 = ((f32[8,32,640]{2,1,0:T(8,128)}), f32[8,32,640]{2,1,0:T(8,128)}, u32[]{:S(2)}, u32[]{:S(2)}) async-start(f32[8,32,640]{2,1,0:T(8,128)} %bitcast.324), calls=%async_computation.13 | async-start | bytes 1310720 | tf_op jit(solution)/shard_map/all_to_all | solution.py:374
  398.2 151.4 %reduce-scatter.19.cloned.1.call-start = ((), (), s32[]{:S(2)}) async-start(), calls=%async_computation.23 | async-start | bytes 655360 | tf_op jit(solution)/shard_map/reduce_scatter | solution.py:399
  398.2 156.6 %collective-permute-start.6 = (bf16[512,512]{1,0:T(8,128)(2,1)}, bf16[512,512]{1,0:T(8,128)(2,1)}, u32[]{:S(2)}, u32[]{:S(2)}) collective-permute-start(bf16[512,512]{1,0:T(8,128)(2,1)} %param.21), channel_id=1, source_target_pairs={{0,1},{1,0},{2,3},{3,2},{4,5},{5,4},{6,7},{7,6},{8,9},{9,8},{10,11... | collective-permute-start | bytes 1572872 | tf_op jit(solution)/shard_map/ppermute | solution.py:186
  398.7 158.1 %collective-permute-start.5 = (bf16[512,512]{1,0:T(8,128)(2,1)}, bf16[512,512]{1,0:T(8,128)(2,1)}, u32[]{:S(2)}, u32[]{:S(2)}) collective-permute-start(bf16[512,512]{1,0:T(8,128)(2,1)} %param.20), channel_id=1, source_target_pairs={{0,1},{1,0},{2,3},{3,2},{4,5},{5,4},{6,7},{7,6},{8,9},{9,8},{10,11... | collective-permute-start | bytes 1572872 | tf_op jit(solution)/shard_map/ppermute | solution.py:186
  400.2 158.5 %collective-permute-start.4 = (bf16[512,1024]{1,0:T(8,128)(2,1)}, bf16[512,1024]{1,0:T(8,128)(2,1)}, u32[]{:S(2)}, u32[]{:S(2)}) collective-permute-start(bf16[512,1024]{1,0:T(8,128)(2,1)} %param.19), channel_id=1, source_target_pairs={{0,1},{1,0},{2,3},{3,2},{4,5},{5,4},{6,7},{7,6},{8,9},{9,8},{10,11... | collective-permute-start | bytes 3145736 | tf_op jit(solution)/shard_map/ppermute | solution.py:186
  400.9 7.7 %copy-start.43 = (f32[128]{0:T(128)}, f32[128]{0:T(128)S(1)}, u32[]{:S(2)}) copy-start(f32[128]{0:T(128)S(1)} %rsqrt.61) | copy-start | bytes 1540
  402.5 8.0 %copy-start.9 = (bf16[2,2,2,256,64]{3,1,0,4,2:T(2,128)(2,1)S(1)}, bf16[2,2,2,256,64]{3,1,0,4,2:T(2,128)(2,1)}, u32[]{:S(2)}) copy-start(bf16[2,2,2,256,64]{3,1,0,4,2:T(2,128)(2,1)} %copy-done.8) | copy-start | bytes 786436
  414.8 4.2 copy-start.23
  414.8 4.2 copy-start.24
  437.0 41.5 %copy-start.1 = (f32[1024,32]{1,0:T(8,128)S(1)}, f32[1024,32]{1,0:T(8,128)}, u32[]{:S(2)}) copy-start(f32[1024,32]{1,0:T(8,128)} %copy-done) | copy-start | bytes 393220
  437.0 41.5 %copy-start.37 = (f32[64]{0:T(128)S(1)}, f32[64]{0:T(128)}, u32[]{:S(2)}) copy-start(f32[64]{0:T(128)} %param.17) | copy-start | bytes 772
  482.1 8.6 %copy-start.19 = (bf16[4,2,1,64,1024]{4,3,2,1,0:T(8,128)(2,1)S(1)}, bf16[4,2,1,64,1024]{4,3,2,1,0:T(8,128)(2,1)}, u32[]{:S(2)}) copy-start(bf16[4,2,1,64,1024]{4,3,2,1,0:T(8,128)(2,1)} %rev.27) | copy-start | bytes 3145732
  485.9 67.1 %all-to-all-start.2 = ((bf16[8,128,256]{2,1,0:T(8,128)(2,1)}), bf16[8,128,256]{2,1,0:T(8,128)(2,1)}, u32[]{:S(2)}, u32[]{:S(2)}) async-start(bf16[8,128,256]{2,1,0:T(8,128)(2,1)} %bitcast.68), calls=%async_computation.5 | async-start | bytes 1048576 | tf_op jit(solution)/shard_map/all_to_all | solution.py:224
  490.5 147.4 %reduce-scatter.15.cloned.1.call-start = ((), (), s32[]{:S(2)}) async-start(), calls=%async_computation.20 | async-start | bytes 1310720 | tf_op jit(solution)/shard_map/reduce_scatter | solution.py:373
  550.8 93.1 %collective-permute-start.7 = (f32[176,1024]{1,0:T(8,128)S(1)}, f32[176,1024]{1,0:T(8,128)S(1)}, u32[]{:S(2)}, u32[]{:S(2)}) collective-permute-start(f32[176,1024]{1,0:T(8,128)S(1)} %pad_maximum_fusion.9), channel_id=1, source_target_pairs={{0,0},{1,16},{2,4},{3,20},{4,8},{5,24},{6,12},{7,28},{8,1},{9,17},... | collective-permute-start | bytes 2162696 | tf_op jit(solution)/shard_map/ppermute | solution.py:405
  558.8 78.1 %copy-start.16 = (f32[128,1024]{1,0:T(8,128)S(1)}, f32[128,1024]{1,0:T(8,128)}, u32[]{:S(2)}) copy-start(f32[128,1024]{1,0:T(8,128)} %get-tuple-element.94) | copy-start | bytes 1572868
  558.8 78.1 %copy-start.45 = (f32[128]{0:T(128)S(1)}, f32[128]{0:T(128)}, u32[]{:S(2)}) copy-start(f32[128]{0:T(128)} %multiply_multiply_fusion.4) | copy-start | bytes 1540
  637.9 9.3 %all-to-all-start.3 = ((f32[8,32,256]{2,1,0:T(8,128)}), f32[8,32,256]{2,1,0:T(8,128)S(1)}, u32[]{:S(2)}, u32[]{:S(2)}) async-start(f32[8,32,256]{2,1,0:T(8,128)} %bitcast.335), calls=%async_computation.7 | async-start | bytes 524288 | tf_op jit(solution)/shard_map/all_to_all | solution.py:374
  (26 other events, 46.6 us)
Sparse Core Ops, SparseCore 0:
  10.4 29.0 all-gather.6
  49.3 28.8 all-gather.8
  80.1 26.2 all-gather.14
  117.9 34.7 all-gather.10
  178.3 51.1 reduce-scatter.10
  232.7 51.1 reduce-scatter.8
  286.2 53.1 reduce-scatter.20
  341.7 51.7 reduce-scatter.22
  395.4 34.8 all-gather.12
  432.5 44.5 reduce-scatter.12
  479.3 46.9 reduce-scatter.16
  528.4 21.1 reduce-scatter.18
  551.9 59.0 reduce-scatter.14

commit v2 on v1

--- a/solution.py
+++ b/solution.py
@@ -56,47 +56,6 @@
 
 SCORE = 1.0 / math.sqrt(HEAD)
 SCORE2 = SCORE * math.log2(math.e)
-
-
-def attn_fwd_kernel(steps, outer_ref, qt_ref, kv_ref, out_ref, total_ref):
-    outer = outer_ref[0]
-    half = kv_ref.shape[0] // (2 * steps)
-    sub = half // 2
-    wide = 2 * sub
-
-    def block(rows, size, cols, mask, acc, total):
-        kv = kv_ref[pl.ds(pl.multiple_of(rows, sub), size), :]
-        probs = jnp.exp2(dot(kv, qt_ref[:, cols]) * SCORE2)
-        if mask is not None:
-            probs = jnp.where(mask, probs, 0.0)
-        total = total + jnp.sum(probs.reshape(size // 8, 8, wide), axis=0)
-        acc = acc + dot(kv, probs.astype(BF16), ((0,), (0,)))
-        return acc, total
-
-    key = lax.broadcasted_iota(jnp.int32, (sub, wide), 0)
-    query = lax.broadcasted_iota(jnp.int32, (sub, wide), 1) % sub
-    diagonal = key <= query
-    for late in range(2):
-        for part in range(2):
-            cols = pl.ds((late * 2 + part) * wide, wide)
-
-            def full(m, carry):
-                if late:
-                    rows = jnp.where(m < steps, m * 2, (outer + 1 + m - steps) * 2 + 1) * half
-                else:
-                    rows = m * 2 * half
-                return block(rows, half, cols, None, *carry)
-
-            count = 2 * steps - 1 - outer if late else outer
-            own = (outer * 2 + late) * half
-            carry = (jnp.zeros((2 * HEAD, wide), F32), jnp.zeros((8, wide), F32))
-            carry = lax.fori_loop(0, count, full, carry)
-            if part:
-                carry = block(own, sub, cols, None, *carry)
-            acc, total = block(own + part * sub, sub, cols, diagonal, *carry)
-            total = jnp.sum(total, axis=0, keepdims=True)
-            out_ref[:, cols] = acc[HEAD:] / total
-            total_ref[:, cols] = jnp.log2(total)
 
 
 def attn_bwd_kernel(
@@ -142,26 +101,461 @@
             dq_ref[:, cols] = acc[:HEAD]
 
 
+def place():
+    outer, inner, fsdp = (lax.axis_index(name) for name in EVERY)
+    return outer, inner, fsdp
+
+
+def remote(src, dst, send, recv, device):
+    return pltpu.make_async_remote_copy(
+        src_ref=src,
+        dst_ref=dst,
+        send_sem=send,
+        recv_sem=recv,
+        device_id=device,
+        device_id_type=pl.DeviceIdType.MESH,
+    )
+
+
+def greet(devices):
+    barrier = pltpu.get_barrier_semaphore()
+    for device in devices:
+        pl.semaphore_signal(
+            barrier, inc=1, device_id=device, device_id_type=pl.DeviceIdType.MESH
+        )
+    return lambda: pl.semaphore_wait(barrier, len(devices))
+
+
+def chip_peer(k):
+    outer, inner, fsdp = place()
+    chip = ((inner // 2) * 2 + fsdp + k) % 4
+    return (outer, (chip // 2) * 2 + inner % 2, chip % 2)
+
+
+def sibling():
+    outer, inner, fsdp = place()
+    return (outer, inner + 1 - 2 * (inner % 2), fsdp)
+
+
+def group_peer(k):
+    outer, inner, fsdp = place()
+    member = (inner * 2 + fsdp + k) % 8
+    return (outer, member // 2, member % 2)
+
+
+def member_of(device):
+    return device[1] * 2 + device[2]
+
+
+def early_row(member, part):
+    return pl.multiple_of(member * part, part)
+
+
+def late_row(member, part):
+    return pl.multiple_of((3 - member // 2) * 2 * part + (member % 2) * part, part)
+
+
+class Gather:
+    def __init__(self, own, land, send, recv):
+        self.own, self.land, self.send, self.recv = own, land, send, recv
+        self.mine = member_of(place())
+        self.started = []
+
+    def copy(self, src, member, piece, slot, device):
+        dst = self.land(member)[piece]
+        copy = remote(
+            src, dst, self.send.at[piece, slot], self.recv.at[piece, member], device
+        )
+        copy.start()
+        self.started.append(copy)
+
+    def start(self):
+        for k in (1, 2, 3, 0):
+            device = chip_peer(k) if k else sibling()
+            for piece, src in enumerate(self.own):
+                self.copy(src, self.mine, piece, k, device)
+
+    def wait(self, member):
+        for piece, dst in enumerate(self.land(member)):
+            remote(
+                dst, dst, self.send.at[piece, 0], self.recv.at[piece, member], sibling()
+            ).wait_recv()
+
+    def pass_on(self, k):
+        member = member_of(chip_peer(k))
+        self.wait(member)
+        for piece, dst in enumerate(self.land(member)):
+            self.copy(dst, member, piece, 3 + k, sibling())
+        return member
+
+    def others(self):
+        near = sibling()
+        yield member_of(near)
+        for k in (1, 2, 3):
+            chip = ((near[1] // 2) * 2 + near[2] + k) % 4
+            yield ((chip // 2) * 2 + near[1] % 2) * 2 + chip % 2
+
+    def drain(self):
+        for copy in self.started:
+            copy.wait_send()
+
+
+def rms_rows(values, gain):
+    inverse = lax.rsqrt(jnp.mean(values * values, axis=-1, keepdims=True) + EPS)
+    return values * inverse * gain
+
+
+def head_inverse(values, low):
+    squares = values * values
+    first = jnp.sum(jnp.where(low, squares, 0.0), axis=-1, keepdims=True)
+    second = jnp.sum(jnp.where(low, 0.0, squares), axis=-1, keepdims=True)
+    return jnp.where(
+        low, lax.rsqrt(first * (1.0 / HEAD) + EPS), lax.rsqrt(second * (1.0 / HEAD) + EPS)
+    )
+
+
+def halves(values, front):
+    quarter = HEAD // 2
+    return jnp.where(
+        front,
+        pltpu.roll(values, values.shape[-1] - quarter, 1),
+        pltpu.roll(values, quarter, 1),
+    )
+
+
+def front_kernel(
+    x_ref,
+    gain_ref,
+    mine_ref,
+    other_ref,
+    cos_ref,
+    sin_ref,
+    qg_ref,
+    kg_ref,
+    normed_out,
+    proj_ref,
+    q_ref,
+    qt_ref,
+    kv_ref,
+    own,
+    land,
+    send,
+    recv,
+    out_sem,
+):
+    _, _, fsdp = place()
+    part = x_ref.shape[1]
+    half = land.shape[1]
+    width = land.shape[2]
+    sub = half // 2
+    depth = width // 2
+    ready = greet([sibling()] + [chip_peer(k) for k in (1, 2, 3)])
+    for late in range(2):
+        rows = x_ref[late].astype(F32)
+        own[late] = rms_rows(rows, gain_ref[...]).astype(BF16)
+    ready()
+
+    def slots(member):
+        return [
+            land.at[0, pl.ds(early_row(member, part), part)],
+            land.at[1, pl.ds(late_row(member, part), part)],
+        ]
+
+    gather = Gather([own.at[0], own.at[1]], slots, send, recv)
+    gather.start()
+    member = member_of(place())
+    land[0, pl.ds(early_row(member, part), part)] = own[0]
+    land[1, pl.ds(late_row(member, part), part)] = own[1]
+    for k in (1, 3, 2):
+        gather.pass_on(k)
+    for member in gather.others():
+        gather.wait(member)
+    out = pltpu.make_async_copy(land, normed_out, out_sem)
+    out.start()
+
+    lane = lax.broadcasted_iota(jnp.int32, (sub, 2 * HEAD), 1)
+    low = lane < HEAD
+    front = lane % HEAD < HEAD // 2
+    mine_at = pl.ds(pl.multiple_of(fsdp * depth, depth), depth)
+    other_at = pl.ds(pl.multiple_of((1 - fsdp) * depth, depth), depth)
+
+    @pl.loop(0, 4)
+    def _(tile):
+        late = tile // 2
+        inside = pl.ds(pl.multiple_of((tile % 2) * sub, sub), sub)
+        rows = pl.ds(pl.multiple_of(tile * sub, sub), sub)
+        proj = dot(land[late, inside, mine_at], mine_ref[...])
+        proj = proj + dot(land[late, inside, other_at], other_ref[...])
+        proj_ref[rows, :] = proj
+        cos, sin = cos_ref[rows, :], sin_ref[rows, :]
+        raw = proj[:, : 2 * HEAD]
+        normed = raw * head_inverse(raw, low) * qg_ref[...]
+        rotated = normed * cos + halves(normed, front) * sin
+        second = pltpu.roll(rotated, HEAD, 1)
+        for head, values in enumerate((rotated, second)):
+            values = jnp.where(low, values, 0.0)
+            cols = pl.ds(pl.multiple_of(tile * 2 * sub + head * sub, sub), sub)
+            q_ref[cols, :] = values.astype(BF16)
+            qt_ref[:, cols] = values.T.astype(BF16)
+        raw = proj[:, 2 * HEAD :]
+        normed = raw * head_inverse(raw, low) * kg_ref[...]
+        rotated = normed * cos + halves(normed, front) * sin
+        kv_ref[rows, :] = jnp.where(low, rotated, raw).astype(BF16)
+
+    gather.drain()
+    out.wait()
+
+
+def middle_kernel(
+    steps,
+    x_ref,
+    dy_ref,
+    qt_ref,
+    kv_ref,
+    wo_mine,
+    wo_other,
+    gain_ref,
+    kv_out,
+    cot_out,
+    attn_t_ref,
+    log_ref,
+    attn_ref,
+    residual_ref,
+    ffn_ref,
+    kv_all,
+    acc_ref,
+    total_ref,
+    token_rows,
+    dy_send,
+    dy_recv,
+    kv_send,
+    kv_recv,
+    swap_send,
+    swap_recv,
+    out_sem,
+):
+    outer, inner, fsdp = place()
+    me = member_of((outer, inner, fsdp))
+    part = x_ref.shape[1]
+    half = kv_ref.shape[0] // 2
+    sub = half // 2
+    wide = 2 * sub
+    width = x_ref.shape[2]
+    depth = width // 2
+
+    def outer_peer(k):
+        return ((outer + k) % steps, inner, fsdp)
+
+    ready = greet(
+        [outer_peer(k) for k in range(1, steps)] + [group_peer(k) for k in range(1, 8)]
+    )
+    kv_all[outer] = kv_ref[...]
+    acc_ref[...] = jnp.zeros_like(acc_ref)
+    total_ref[...] = jnp.zeros_like(total_ref)
+    ready()
+    for k in range(1, steps):
+        remote(
+            kv_ref, kv_all.at[outer], kv_send.at[k], kv_recv.at[outer], outer_peer(steps - k)
+        ).start()
+    cot = Gather(
+        [dy_ref.at[n] for n in range(2)],
+        lambda member: [cot_out.at[member, n] for n in range(2)],
+        dy_send,
+        dy_recv,
+    )
+    cot.start()
+    own_dy = pltpu.make_async_copy(dy_ref, cot_out.at[me], out_sem.at[0])
+    own_dy.start()
+
+    def block(slot, row, size, col, mask):
+        kv = kv_all[slot, pl.ds(pl.multiple_of(row, sub), size), :]
+        cols = pl.ds(pl.multiple_of(col, wide), wide)
+        probs = jnp.exp2(dot(kv, qt_ref[:, cols]) * SCORE2)
+        if mask is not None:
+            probs = jnp.where(mask, probs, 0.0)
+        total_ref[:, cols] += jnp.sum(probs.reshape(size // 8, 8, wide), axis=0)
+        acc_ref[:, cols] += dot(kv, probs.astype(BF16), ((0,), (0,)))
+
+    key = lax.broadcasted_iota(jnp.int32, (sub, wide), 0)
+    query = lax.broadcasted_iota(jnp.int32, (sub, wide), 1) % sub
+    diagonal = key <= query
+
+    @pl.loop(0, 2)
+    def _(late):
+        block(outer, late * half, sub, late * 2 * wide, diagonal)
+        block(outer, late * half, sub, late * 2 * wide + wide, None)
+        block(outer, late * half + sub, sub, late * 2 * wide + wide, diagonal)
+
+    @pl.loop(0, 2)
+    def _(n):
+        block(outer, 0, half, (2 + n) * wide, None)
+
+    @pl.loop(1, steps)
+    def _(k):
+        slot = (outer + k) % steps
+        late = jnp.where(slot < outer, 0, 1)
+        remote(
+            kv_ref, kv_all.at[slot], kv_send.at[k], kv_recv.at[slot], outer_peer(k)
+        ).wait_recv()
+
+        @pl.loop(0, 2)
+        def _(n):
+            block(slot, 0, half, (2 + n) * wide, None)
+            block(slot, late * half, half, (late * 2 + n) * wide, None)
+
+    kv_copy = pltpu.make_async_copy(kv_all, kv_out, out_sem.at[1])
+    kv_copy.start()
+
+    @pl.loop(0, 4)
+    def _(tile):
+        heads = []
+        for head in range(2):
+            cols = pl.ds(pl.multiple_of(tile * wide + head * sub, sub), sub)
+            total = jnp.sum(total_ref[:, cols], axis=0, keepdims=True)
+            values = acc_ref[HEAD:, cols] / total
+            attn_t_ref[:, cols] = values
+            log_ref[:, cols] = jnp.log2(total)
+            heads.append(values)
+        inside = pl.ds(pl.multiple_of((tile % 2) * sub, sub), sub)
+        attn_ref[tile // 2, inside, :] = jnp.concatenate(heads, axis=0).T.astype(BF16)
+
+    lane = fsdp * 4 + inner
+
+    def chunk(member):
+        return [
+            attn_ref.at[0, pl.ds(early_row(member, part), part)],
+            attn_ref.at[1, pl.ds(late_row(member, part), part)],
+        ]
+
+    def landing(source):
+        cols = pl.ds(pl.multiple_of(source * 2 * HEAD, 2 * HEAD), 2 * HEAD)
+        return [token_rows.at[n, :, cols] for n in range(2)]
+
+    swaps = []
+    for k in range(1, 8):
+        device = group_peer(k)
+        for n in range(2):
+            swaps.append(
+                remote(
+                    chunk(member_of(device))[n],
+                    landing(lane)[n],
+                    swap_send.at[n, k],
+                    swap_recv.at[n, lane],
+                    device,
+                )
+            )
+            swaps[-1].start()
+    own_cols = pl.ds(pl.multiple_of(lane * 2 * HEAD, 2 * HEAD), 2 * HEAD)
+    token_rows[0, :, own_cols] = attn_ref[0, pl.ds(early_row(me, part), part), :]
+    token_rows[1, :, own_cols] = attn_ref[1, pl.ds(late_row(me, part), part), :]
+    for k in range(1, 8):
+        device = group_peer(k)
+        source = device[2] * 4 + device[1]
+        for n in range(2):
+            remote(
+                landing(source)[n],
+                landing(source)[n],
+                swap_send.at[n, k],
+                swap_recv.at[n, source],
+                device,
+            ).wait_recv()
+
+    mine_at = pl.ds(pl.multiple_of(fsdp * depth, depth), depth)
+    other_at = pl.ds(pl.multiple_of((1 - fsdp) * depth, depth), depth)
+    for n in range(2):
+        values = dot(token_rows[n, :, mine_at], wo_mine[...])
+        values = values + dot(token_rows[n, :, other_at], wo_other[...])
+        values = values + x_ref[n].astype(F32)
+        residual_ref[n] = values
+        ffn_ref[n] = rms_rows(values, gain_ref[...]).astype(BF16)
+
+    for k in (1, 3, 2):
+        cot.pass_on(k)
+    for member in cot.others():
+        cot.wait(member)
+    cot.drain()
+    for copy in swaps:
+        copy.wait_send()
+    for k in range(1, steps):
+        remote(
+            kv_ref, kv_all.at[outer], kv_send.at[k], kv_recv.at[outer], outer_peer(steps - k)
+        ).wait_send()
+    own_dy.wait()
+    kv_copy.wait()
+
+
 SMEM = pl.BlockSpec(memory_space=pltpu.SMEM)
 VMEM = pl.BlockSpec(memory_space=pltpu.VMEM)
-
-
-def attn_fwd(outer, qt, kv, steps):
-    cols = qt.shape[1]
-    work = kv.shape[0] * cols // 2
+ANY = pl.BlockSpec(memory_space=pl.ANY)
+DMA = pltpu.SemaphoreType.DMA
+
+
+def params(collective):
+    return pltpu.CompilerParams(
+        collective_id=collective, has_side_effects=True, vmem_limit_bytes=60 << 20
+    )
+
+
+def front(x, gain, mine, other, cos, sin, q_gain, k_gain):
+    part, width = x.shape[1:]
+    tokens = cos.shape[0]
+    half = tokens // 2
     return pl.pallas_call(
-        functools.partial(attn_fwd_kernel, steps),
+        front_kernel,
         out_shape=(
-            jax.ShapeDtypeStruct((HEAD, cols), F32),
-            jax.ShapeDtypeStruct((1, cols), F32),
+            jax.ShapeDtypeStruct((2, half, width), BF16),
+            jax.ShapeDtypeStruct((tokens, 4 * HEAD), F32),
+            jax.ShapeDtypeStruct((2 * tokens, 2 * HEAD), BF16),
+            jax.ShapeDtypeStruct((2 * HEAD, 2 * tokens), BF16),
+            jax.ShapeDtypeStruct((tokens, 2 * HEAD), BF16),
         ),
-        in_specs=[SMEM, VMEM, VMEM],
-        out_specs=[VMEM, VMEM],
-        cost_estimate=pl.CostEstimate(
-            flops=work * 512, transcendentals=work, bytes_accessed=4 << 20
+        in_specs=[VMEM] * 8,
+        out_specs=[ANY, VMEM, VMEM, VMEM, VMEM],
+        scratch_shapes=[
+            pltpu.VMEM((2, part, width), BF16),
+            pltpu.VMEM((2, half, width), BF16),
+            DMA((2, 8)),
+            DMA((2, 8)),
+            DMA,
+        ],
+        compiler_params=params(0),
+        name="front",
+    )(x, gain, mine, other, cos, sin, q_gain, k_gain)
+
+
+def middle(x, dy, qt, kv, wo_mine, wo_other, gain, steps):
+    part, width = x.shape[1:]
+    tokens = kv.shape[0]
+    half = tokens // 2
+    return pl.pallas_call(
+        functools.partial(middle_kernel, steps),
+        out_shape=(
+            jax.ShapeDtypeStruct((steps, tokens, 2 * HEAD), BF16),
+            jax.ShapeDtypeStruct((8, 2, part, width), BF16),
+            jax.ShapeDtypeStruct((HEAD, 2 * tokens), F32),
+            jax.ShapeDtypeStruct((1, 2 * tokens), F32),
+            jax.ShapeDtypeStruct((2, half, 2 * HEAD), BF16),
+            jax.ShapeDtypeStruct((2, part, width), F32),
+            jax.ShapeDtypeStruct((2, part, width), BF16),
         ),
-        name="attn_fwd",
-    )(outer, qt, kv)
+        in_specs=[VMEM] * 7,
+        out_specs=[ANY, ANY] + [VMEM] * 5,
+        scratch_shapes=[
+            pltpu.VMEM((steps, tokens, 2 * HEAD), BF16),
+            pltpu.VMEM((2 * HEAD, 2 * tokens), F32),
+            pltpu.VMEM((8, 2 * tokens), F32),
+            pltpu.VMEM((2, part, width), BF16),
+            DMA((2, 8)),
+            DMA((2, 8)),
+            DMA((steps,)),
+            DMA((steps,)),
+            DMA((2, 8)),
+            DMA((2, 8)),
+            DMA((2,)),
+        ],
+        compiler_params=params(1),
+        name="middle",
+    )(x, dy, qt, kv, wo_mine, wo_other, gain)
 
 
 def attn_bwd(outer, qt, q, gt, g, kv, log_total, delta, steps):
@@ -258,8 +652,10 @@
         ],
         axis=1,
     )
-    w_qkv = join(qkv(lane), swap(qkv(other_lane), fsdp_size))
-    wo_all = join(wo, swap(wo, fsdp_size))
+    qkv_mine = qkv(lane)
+    qkv_other = swap(qkv(other_lane), fsdp_size)
+    wo_other = swap(wo, fsdp_size)
+    wo_all = join(wo, wo_other)
     ff = w_gate.shape[1]
     tiles = 2 * ff // group // BLOCK
     reach = (tiles + 1) // 2 * BLOCK
@@ -281,27 +677,38 @@
     wk_all = join(wk, swap(wk, fsdp_size))
     wv_all = join(wv, swap(wv, fsdp_size))
 
-    inputs = block_input.reshape(rows, width).astype(F32)
+    x = block_input.reshape(2, part, width)
+    inputs = x.reshape(rows, width).astype(F32)
     cotangent = dy.reshape(rows, width)
-    cot_group = gather(cotangent)
-    normed, inverse_in = rms_forward(inputs, attn_gain)
-    normed_group = gather(normed.astype(BF16))
-    proj = dot(normed_group, w_qkv)
-    queries = proj[:, : 2 * HEAD].reshape(2 * half, 2, HEAD)
-    key_unnormed = proj[:, 2 * HEAD : 3 * HEAD].reshape(2 * half, 1, HEAD)
-    value_rows = proj[:, 3 * HEAD :].astype(BF16)
-    q_normed, q_inverse = rms_forward(queries, q_gain)
-    k_normed, k_inverse = rms_forward(key_unnormed, k_gain)
     within = jnp.arange(half, dtype=jnp.int32)
     positions = jnp.concatenate(
         [outer * half + within, (2 * steps - 1 - outer) * half + within], axis=0
     )
     cosine, sine_tab = rope_tables(positions, HEAD)
-    q_rot = (q_normed * cosine + rotate(q_normed) * sine_tab).astype(BF16)
-    k_rot = (k_normed * cosine + rotate(k_normed) * sine_tab).astype(BF16)
-    kv_own = jnp.concatenate([k_rot[:, 0], value_rows], axis=1)
-    kv = lax.all_gather(kv_own, "outer", axis=0, tiled=True)
-
+    front_sign = jnp.where(jnp.arange(HEAD) < HEAD // 2, -1.0, 1.0).astype(F32)
+    cos2 = jnp.tile(cosine[:, 0], (1, 2))
+    sin2 = jnp.tile(sine_tab[:, 0] * front_sign, (1, 2))
+    q_gain2 = jnp.tile(q_gain, 2)[None]
+    k_gain2 = jnp.tile(k_gain, 2)[None]
+    normed_group, proj, q_cols, q_t, kv_own = front(
+        x, attn_gain[None], qkv_mine, qkv_other, cos2, sin2, q_gain2, k_gain2
+    )
+    normed_group = normed_group.reshape(2 * half, width)
+    kv, cot_group, attn_t, log2_total, attn_bf, residual, ffn_rows = middle(
+        x, dy.reshape(2, part, width), q_t, kv_own, wo, wo_other, ffn_gain[None], steps
+    )
+    kv = kv.reshape(-1, 2 * HEAD)
+    cot_group = cot_group.reshape(group * rows, width)
+    attn_bf = attn_bf.reshape(2 * half, 2 * HEAD)
+    residual = residual.reshape(rows, width)
+    inverse_ffn = lax.rsqrt(jnp.mean(residual * residual, axis=-1, keepdims=True) + EPS)
+    inverse_in = lax.rsqrt(jnp.mean(inputs * inputs, axis=-1, keepdims=True) + EPS)
+    queries = proj[:, : 2 * HEAD].reshape(2 * half, 2, HEAD)
+    key_unnormed = proj[:, 2 * HEAD : 3 * HEAD].reshape(2 * half, 1, HEAD)
+    q_inverse = lax.rsqrt(jnp.mean(queries * queries, axis=-1, keepdims=True) + EPS)
+    k_inverse = lax.rsqrt(
+        jnp.mean(key_unnormed * key_unnormed, axis=-1, keepdims=True) + EPS
+    )
     sub = half // 2
 
     def to_cols(arr):
@@ -310,29 +717,28 @@
     def from_cols(arr):
         return jnp.transpose(arr.reshape(2, 2, 2, sub, -1), (0, 1, 3, 2, 4)).reshape(2 * half, -1)
 
-    q_cols = jnp.pad(to_cols(q_rot), ((0, 0), (0, HEAD)))
-    q_t = q_cols.T
     outer_arr = outer.reshape(1)
-    attn_t, log2_total = attn_fwd(outer_arr, q_t, kv, steps)
     attn = from_cols(attn_t.T)
-    attn_bf = attn.astype(BF16)
-    attn_rows = heads_to_tokens(attn_bf)
-    residual = inputs + dot(attn_rows, wo_all)
-    ffn_normed, inverse_ffn = rms_forward(residual, ffn_gain)
-    ffn_in = gather(ffn_normed.astype(BF16))
+    ffn_in = lax.all_gather(ffn_rows.reshape(rows, width), GROUP, axis=0, tiled=True)
+
+    def scatter_members(arr):
+        return lax.psum_scatter(
+            arr.reshape(group, rows, width), GROUP, scatter_dimension=0, tiled=False
+        )
+
     gate_pre = dot(ffn_in, gate_w)
     up_pre = dot(ffn_in, up_w)
     sigmoid_gate = jax.nn.sigmoid(gate_pre)
     silu_gate = gate_pre * sigmoid_gate
     hidden = jnp.where(valid, silu_gate * up_pre, 0.0).astype(BF16)
-    result = residual + scatter(dot(hidden, down_w))
+    result = residual + scatter_members(dot(hidden, down_w))
 
     d_hidden = jnp.where(valid, dot(cot_group, down_w, ((1,), (1,))), 0.0)
     d_gate = (d_hidden * up_pre * sigmoid_gate * (1.0 + gate_pre * (1.0 - sigmoid_gate))).astype(
         BF16
     )
     d_up = (d_hidden * silu_gate).astype(BF16)
-    d_ffn_in = scatter(dot(d_gate, gate_w, ((1,), (1,))) + dot(d_up, up_w, ((1,), (1,))))
+    d_ffn_in = scatter_members(dot(d_gate, gate_w, ((1,), (1,))) + dot(d_up, up_w, ((1,), (1,))))
     d_w_down = dot(hidden, cot_group, ((0,), (0,)))
     d_w_gate = dot(ffn_in, d_gate, ((0,), (0,)))
     d_w_up = dot(ffn_in, d_up, ((0,), (0,)))

time: 670 us -> 637 us (0.951)
  Pallas kernels: 28.1 us -> 97.8 us
  local copies, waits for them, and re-layouts: 117 us -> 70.2 us
  other arithmetic: 47.1 us -> 23.5 us
  waiting for transfers between devices: 269 us -> 257 us
  blocking collectives: 83.7 us -> 74.8 us
  matrix products: 62.5 us -> 54.6 us
    pallas_call x1 -> x2, Pallas kernels: 11.1 us -> 80.9 us  [the longest x1 43.9 us: middle(): pl.pallas_call(functools.partial(middle_kernel, steps), out_shape=(jax.Sh...]
    all_gather x4 -> x1, waiting for transfers between devices: 41 us -> 0.01 us  [gather(): arr = lax.all_gather(arr.reshape(2, part, -1), GROUP, axis=0, tiled=False)]
    ppermute x7, waiting for transfers between devices: 0.02 us -> 18.2 us  [swap(): lax.ppermute(array, 'fsdp', [(k, (k + 1) % axis_size) for k in range(axis...]
    reduce_scatter x3, waiting for transfers between devices: 39.1 us -> 54 us  [rows_out(): part_sum = lax.psum_scatter(arr, 'outer', scatter_dimension=0, tiled=True)]
    reduce_scatter x1, waiting for transfers between devices: 40 us -> 28.9 us  [local(): d_kv = lax.psum_scatter(d_kv, 'outer', scatter_dimension=0, tiled=True)]
    all_to_all x3, waiting for transfers between devices: 1.85 us -> 10.5 us  [rows_out(): lax.all_to_all(part_sum, GROUP, split_axis=0, concat_axis=0, tiled=True)]
    all_to_all x1 -> x0, blocking collectives: 8.62 us -> none  [tokens_to_heads(): got = lax.all_to_all(cut, GROUP, split_axis=0, concat_axis=0, tiled=True)]
    slice x4 -> x1, local copies, waits for them, and re-layouts: 11.8 us -> 3.22 us  [gather(): early = arr[:, :, 0].reshape(half, -1)]
  transfers between devices with their start and end apart: 26 -> 23, of which waited for: 12 -> 13; matrix products, arithmetic and copies ran while one was open for 30% -> 19% of each run, Pallas kernels for 4% -> 9%
where the time goes in v2:
time: 637 us; the launch traced here: 627 us
  waiting for transfers between devices  257 us (40%)
  Pallas kernels  97.8 us (15%)
  blocking collectives  74.8 us (12%)
  local copies, waits for them, and re-layouts  70.2 us (11%)
  matrix products  54.6 us (9%)
  starting transfers between devices  33.5 us (5%)
  other arithmetic  23.5 us (4%)
  between operations  15.4 us (2%)
    reduce_scatter x2, waiting for transfers between devices, scatter_members(): lax.psum_scatter(arr.reshape(group, rows, width), GROUP, scatter_dimensio...  83.6 us
    psum x1, blocking collectives, local(): lax.psum(jnp.concatenate([d_attn_gain, d_ffn_gain, jnp.pad(d_q_gain, (0,...  74.8 us
    dot_general x15, matrix products, dot(): return lax.dot_general(a, b, (dims, ((), ())), preferred_element_type=F32)  54.6 us
    reduce_scatter x3, waiting for transfers between devices, rows_out(): part_sum = lax.psum_scatter(arr, 'outer', scatter_dimension=0, tiled=True)  54 us
    pallas_call x1, Pallas kernels, middle(): pl.pallas_call(functools.partial(middle_kernel, steps), out_shape=(jax.Sh...  43.9 us
    pallas_call x1, Pallas kernels, front(): pl.pallas_call(front_kernel, out_shape=(jax.ShapeDtypeStruct((2, half, wi...  37 us
    reduce_scatter x1, waiting for transfers between devices, local(): d_kv = lax.psum_scatter(d_kv, 'outer', scatter_dimension=0, tiled=True)  28.9 us
    reduce_scatter x1, waiting for transfers between devices, local(): lax.psum_scatter(down_rows, 'outer', scatter_dimension=0, tiled=True)  25.9 us
  transfers between devices with their start and end apart: 23, of which 13 were waited for; matrix products, arithmetic and copies ran while one was open for 19% of the time, Pallas kernels for 9%

profile of v2, /device:TPU:6, one launch (start us, length us, event | category | flops | bytes accessed | tf_op | source)
XLA Modules:
  0.0 626.5 jit_solution(13339484027984715960)
XLA Ops:
  13.4 1.9 multiply_sine_fusion
  21.9 37.0 %front.1 = (bf16[2,512,1024]{2,1,0:T(8,128)(2,1)}, f32[1024,256]{1,0:T(8,128)}, bf16[2048,128]{1,0:T(8,128)(2,1)}, bf16[128,2048]{1,0:T(8,128)(2,1)}, bf16[1024,128]{1,0:T(8,128)(2,1)}) custom-call(bf16[2,64,1024]{2,1,0:T(8,128)(2,1)} %bitcast.214, f32[1,1024]{1,0:T(1,128)} %bitcast.260, bf16[512,256]{1,0:T(8,128)(2,1)} %pad_maximum_fusion.6.mine_ref, ...), custom_call_target="tpu_custom_call" | custom-call | tf_op jit(solution)/shard_map/front/pallas_call | solution.py:503
  58.9 43.9 %middle.1 = (bf16[4,1024,128]{2,1,0:T(8,128)(2,1)}, bf16[8,2,64,1024]{3,2,1,0:T(8,128)(2,1)}, f32[64,2048]{1,0:T(8,128)}, f32[1,2048]{1,0:T(1,128)}, bf16[2,512,...) custom-call(bf16[2,64,1024]{2,1,0:T(8,128)(2,1)} %bitcast.215, ...), custom_call_target="tpu_custom_call" | custom-call | tf_op jit(solution)/shard_map/middle/pallas_call | solution.py:530
  103.0 2.2 constant_dynamic-slice_fusion.2
  106.3 2.2 constant_dynamic-slice_fusion.4
  109.6 5.2 fusion.22
  114.9 13.5 %collective-permute-done.3 = bf16[512,640]{1,0:T(8,128)(2,1)} collective-permute-done((bf16[512,640]{1,0:T(8,128)(2,1)}, bf16[512,640]{1,0:T(8,128)(2,1)}, u32[]{:S(2)}, u32[]{:S(2)}) %collective-permute-start.3) | collective-permute-done | bytes 655392 | tf_op jit(solution)/shard_map/ppermute | solution.py:580
  128.3 8.0 %all-gather.4.cloned.1.call-done = bf16[1024,1024]{1,0:T(8,128)(2,1)} async-done(((bf16[128,1024]{1,0:T(8,128)(2,1)}), bf16[1024,1024]{1,0:T(8,128)(2,1)}) %all-gather.4.cloned.1.call-update) | async-done | bytes 2097168 | tf_op jit(solution)/shard_map/all_gather | solution.py:722
  136.4 3.9 fusion.60
  140.3 4.7 collective-permute-done.2
  145.8 4.1 multiply_convert_fusion.1
  150.0 4.2 fusion.59
  154.2 3.8 convolution_add_fusion
  158.1 5.1 fusion.24
  165.1 4.8 fusion.85
  171.3 4.9 fusion.84
  176.3 30.3 %reduce-scatter.11.cloned.1.call-done = f32[1,128,1024]{2,1,0:T(8,128)} async-done(((f32[8,128,1024]{2,1,0:T(8,128)}), f32[1,128,1024]{2,1,0:T(8,128)}) %reduce-scatter.11.cloned.1.call-update) | async-done | bytes 524304 | tf_op jit(solution)/shard_map/reduce_scatter | solution.py:725
  207.9 53.3 %reduce-scatter.9.cloned.1.call-done = f32[1,128,1024]{2,1,0:T(8,128)} async-done(((f32[8,128,1024]{2,1,0:T(8,128)}), f32[1,128,1024]{2,1,0:T(8,128)}) %reduce-scatter.9.cloned.1.call-update) | async-done | bytes 524304 | tf_op jit(solution)/shard_map/reduce_scatter | solution.py:725
  261.2 2.3 add_convert_fusion
  264.8 2.5 fusion.21
  268.2 4.8 all-to-all-start
  273.5 4.1 all-to-all-done
  282.5 16.9 %attn_bwd.1 = (f32[64,2048]{1,0:T(8,128)}, f32[4096,128]{1,0:T(8,128)}) custom-call(s32[1]{0:T(128)} %bitcast.19.outer_ref, bf16[128,2048]{1,0:T(8,128)(2,1)} %get-tuple-element.27.qt_ref, bf16[2048,128]{1,0:T(8,128)(2,1)} %get-tuple-element.33.q_ref, bf16[128,2048]{1,0:T(8,128)(2,1)} %copy.170.gt_ref, bf16[2048,128]{1,0:T(8,128)(2,1)} %get-tuple-element.145.g_ref, ...), custom_call_target="tpu_custom_call" | custom-call | flops 5368709120 | bytes 8388608 | tf_op jit(solution)/shard_map/attn_bwd/pallas_call | solution.py:564
  301.0 2.9 fusion.83
  309.4 7.1 %reduce-scatter.23.cloned.1.call-done = f32[256,640]{1,0:T(8,128)} async-done(((f32[1024,640]{1,0:T(8,128)}), f32[256,640]{1,0:T(8,128)}) %reduce-scatter.23.cloned.1.call-update) | async-done | bytes 655376 | tf_op jit(solution)/shard_map/reduce_scatter | solution.py:779
  316.6 4.6 all-to-all-start.4
  323.7 46.8 %reduce-scatter.21.cloned.1.call-done = f32[256,640]{1,0:T(8,128)} async-done(((f32[1024,640]{1,0:T(8,128)}), f32[256,640]{1,0:T(8,128)}) %reduce-scatter.21.cloned.1.call-update) | async-done | bytes 655376 | tf_op jit(solution)/shard_map/reduce_scatter | solution.py:779
  370.6 4.2 all-to-all-start.3
  377.7 8.6 %all-to-all-done.3 = f32[8,32,640]{2,1,0:T(8,128)S(1)} async-done(((f32[8,32,640]{2,1,0:T(8,128)}), f32[8,32,640]{2,1,0:T(8,128)S(1)}, u32[]{:S(2)}, u32[]{:S(2)}) %all-to-all-start.3) | async-done | bytes 655392 | tf_op jit(solution)/shard_map/all_to_all | solution.py:780
  400.1 2.0 copy.180
  402.1 2.0 copy.177
  404.2 2.6 reshape.494
  406.8 2.5 subtract_convert_fusion.1
  409.4 3.2 fusion.74
  412.6 2.3 rev.11
  414.9 2.8 fusion.13
  417.8 28.9 %reduce-scatter.13.cloned.1.call-done = f32[1024,128]{1,0:T(8,128)} async-done(((f32[4096,128]{1,0:T(8,128)}), f32[1024,128]{1,0:T(8,128)}) %reduce-scatter.13.cloned.1.call-update) | async-done | bytes 524304 | tf_op jit(solution)/shard_map/reduce_scatter | solution.py:757
  450.6 4.6 all-to-all-start.1
  455.2 3.4 fusion.82
  468.2 1.9 fusion.40
  470.1 25.9 %reduce-scatter.17.cloned.1.call-done = f32[144,1024]{1,0:T(8,128)} async-done(((f32[576,1024]{1,0:T(8,128)}), f32[144,1024]{1,0:T(8,128)}) %reduce-scatter.17.cloned.1.call-update) | async-done | bytes 589840 | tf_op jit(solution)/shard_map/reduce_scatter | solution.py:804
  495.9 23.5 %reduce-scatter.19.cloned.1.call-done = f32[32,1024]{1,0:T(8,128)} async-done(((f32[128,1024]{1,0:T(8,128)}), f32[32,1024]{1,0:T(8,128)}) %reduce-scatter.19.cloned.1.call-update) | async-done | bytes 131088 | tf_op jit(solution)/shard_map/reduce_scatter | solution.py:805
  520.6 2.4 collective-permute-start.7
  524.7 2.0 fusion.26
  526.8 2.1 fusion.32
  529.0 2.8 fusion.50
  531.9 74.8 %psum.7 = f32[2176]{0:T(1024)S(1)} all-reduce(f32[2176]{0:T(1024)S(1)} %concatenate.138), channel_id=1, replica_groups=mesh['outer'=4,'inner'=4,'fsdp'=2] {'outer','inner','fsdp'}, use_global_device_ids=true, to_apply=%region_16.17 | all-reduce | flops 2176 | bytes 17408 | tf_op jit(solution)/shard_map/psum | solution.py:814
  607.7 4.7 all-to-all-start.2
  (263 shorter events, 78.6 us)
Async XLA Ops:
  7.2 4.7 copy-start.32
  7.2 129.2 %all-gather.4.cloned.1.call-start = ((), (), s32[]{:S(2)}) async-start(), calls=%async_computation.13 | async-start | bytes 2359296 | tf_op jit(solution)/shard_map/all_gather | solution.py:722
  11.4 10.5 %collective-permute-start = (bf16[512,256]{1,0:T(8,128)(2,1)}, bf16[512,256]{1,0:T(8,128)(2,1)}, u32[]{:S(2)}, u32[]{:S(2)}) collective-permute-start(bf16[512,256]{1,0:T(8,128)(2,1)} %pad_maximum_fusion.7), channel_id=1, source_target_pairs={{0,1},{1,0},{2,3},{3,2},{4,5},{5,4},{6,7},{7,6},{8,9},{9,8},{10,11... | collective-permute-start | bytes 786440 | tf_op jit(solution)/shard_map/ppermute | solution.py:580
  11.9 46.9 %collective-permute-start.1 = (bf16[512,1024]{1,0:T(8,128)(2,1)S(1)}, bf16[512,1024]{1,0:T(8,128)(2,1)}, u32[]{:S(2)}, u32[]{:S(2)}) collective-permute-start(bf16[512,1024]{1,0:T(8,128)(2,1)S(1)} %copy-done.32), channel_id=1, source_target_pairs={{0,1},{1,0},{2,3},{3,2},{4,5},{5,4},{6,7},{7,6},{8,9},{9,8},{10,11... | collective-permute-start | bytes 3145736 | tf_op jit(solution)/shard_map/ppermute | solution.py:580
  102.8 103.9 %reduce-scatter.11.cloned.1.call-start = ((), (), s32[]{:S(2)}) async-start(), calls=%async_computation.15 | async-start | bytes 4718592 | tf_op jit(solution)/shard_map/reduce_scatter | solution.py:725
  105.3 31.1 %copy-start.36 = (bf16[512,640]{1,0:T(8,128)(2,1)}, bf16[512,640]{1,0:T(8,128)(2,1)S(1)}, u32[]{:S(2)}) copy-start(bf16[512,640]{1,0:T(8,128)(2,1)S(1)} %get-tuple-element.120) | copy-start | bytes 1966084
  105.3 23.0 %collective-permute-start.3 = (bf16[512,640]{1,0:T(8,128)(2,1)}, bf16[512,640]{1,0:T(8,128)(2,1)}, u32[]{:S(2)}, u32[]{:S(2)}) collective-permute-start(bf16[512,640]{1,0:T(8,128)(2,1)} %get-tuple-element.121), channel_id=1, source_target_pairs={{0,1},{1,0},{2,3},{3,2},{4,5},{5,4},{6,7},{7,6},{8,9},{9,8},{10,11... | collective-permute-start | bytes 1966088 | tf_op jit(solution)/shard_map/ppermute | solution.py:580
  108.6 36.4 %collective-permute-start.2 = (bf16[512,640]{1,0:T(8,128)(2,1)}, bf16[512,640]{1,0:T(8,128)(2,1)S(1)}, u32[]{:S(2)}, u32[]{:S(2)}) collective-permute-start(bf16[512,640]{1,0:T(8,128)(2,1)} %get-tuple-element.119), channel_id=1, source_target_pairs={{0,1},{1,0},{2,3},{3,2},{4,5},{5,4},{6,7},{7,6},{8,9},{9,8},{10,11... | collective-permute-start | bytes 1966088 | tf_op jit(solution)/shard_map/ppermute | solution.py:580
  136.4 9.4 %copy-start.44 = (bf16[1024,1024]{1,0:T(8,128)(2,1)S(1)}, bf16[1024,1024]{1,0:T(8,128)(2,1)}, u32[]{:S(2)}) copy-start(bf16[1024,1024]{1,0:T(8,128)(2,1)} %all-gather.4.cloned.1.call-done) | copy-start | bytes 6291460
  136.4 9.4 %copy-start.47 = (f32[1024,640]{1,0:T(8,128)S(1)}, f32[1024,640]{1,0:T(8,128)}, u32[]{:S(2)}) copy-start(f32[1024,640]{1,0:T(8,128)} %fusion.22) | copy-start | bytes 7864324
  145.8 4.2 copy-start.37
  149.9 4.2 copy-start.48
  150.0 4.2 copy-start.25
  150.0 8.2 %copy-start.24 = (bf16[1024,640]{1,0:T(8,128)(2,1)}, bf16[1024,640]{1,0:T(8,128)(2,1)S(1)}, u32[]{:S(2)}) copy-start(bf16[1024,640]{1,0:T(8,128)(2,1)S(1)} %get-tuple-element.117) | copy-start | bytes 3932164
  150.0 4.2 copy-start.35
  158.1 103.1 %reduce-scatter.9.cloned.1.call-start = ((), (), s32[]{:S(2)}) async-start(), calls=%async_computation.14 | async-start | bytes 4718592 | tf_op jit(solution)/shard_map/reduce_scatter | solution.py:725
  163.3 153.3 %reduce-scatter.23.cloned.1.call-start = ((), (), s32[]{:S(2)}) async-start(), calls=%async_computation.21 | async-start | bytes 3276800 | tf_op jit(solution)/shard_map/reduce_scatter | solution.py:779
  170.0 200.6 %reduce-scatter.21.cloned.1.call-start = ((), (), s32[]{:S(2)}) async-start(), calls=%async_computation.20 | async-start | bytes 3276800 | tf_op jit(solution)/shard_map/reduce_scatter | solution.py:779
  176.2 30.4 %copy-start.2 = (f32[2,64,1024]{2,1,0:T(8,128)S(1)}, f32[2,64,1024]{2,1,0:T(8,128)}, u32[]{:S(2)}) copy-start(f32[2,64,1024]{2,1,0:T(8,128)} %get-tuple-element.29) | copy-start | bytes 1572868
  176.2 30.4 %copy-start.39 = (f32[1024]{0:T(1024)S(1)}, f32[1024]{0:T(1024)}, u32[]{:S(2)}) copy-start(f32[1024]{0:T(1024)} %param.18) | copy-start | bytes 12292
  176.2 85.0 %copy-start.17 = (bf16[2,1,64,1024]{3,2,1,0:T(8,128)(2,1)S(1)}, bf16[2,1,64,1024]{3,2,1,0:T(8,128)(2,1)}, u32[]{:S(2)}) copy-start(bf16[2,1,64,1024]{3,2,1,0:T(8,128)(2,1)} %param.14) | copy-start | bytes 786436
  176.2 233.1 %all-gather.6.cloned.1.call-start = ((), (), s32[]{:S(2)}) async-start(), calls=%async_computation.22 | async-start | bytes 2359296 | tf_op jit(solution)/shard_map/all_gather | solution.py:603
  206.6 57.0 %copy-start.3 = (f32[1,128,1024]{2,1,0:T(8,128)S(1)}, f32[1,128,1024]{2,1,0:T(8,128)}, u32[]{:S(2)}) copy-start(f32[1,128,1024]{2,1,0:T(8,128)} %reduce-scatter.11.cloned.1.call-done) | copy-start | bytes 1572868
  261.2 3.6 copy-start.33
  264.8 8.2 %copy-start.38 = (f32[64,2048]{1,0:T(8,128)S(1)}, f32[64,2048]{1,0:T(8,128)}, u32[]{:S(2)}) copy-start(f32[64,2048]{1,0:T(8,128)} %get-tuple-element.36) | copy-start | bytes 1572868
  268.2 9.4 %all-to-all-start = ((bf16[8,128,128]{2,1,0:T(8,128)(2,1)}), bf16[8,128,128]{2,1,0:T(8,128)(2,1)S(1)}, u32[]{:S(2)}, u32[]{:S(2)}) async-start(bf16[8,128,128]{2,1,0:T(8,128)(2,1)} %bitcast.21), calls=%async_computation.2 | async-start | bytes 524288 | tf_op jit(solution)/shard_map/all_to_all | solution.py:625
  273.0 173.7 %reduce-scatter.13.cloned.1.call-start = ((), (), s32[]{:S(2)}) async-start(), calls=%async_computation.16 | async-start | bytes 2621440 | tf_op jit(solution)/shard_map/reduce_scatter | solution.py:757
  299.4 196.5 %reduce-scatter.17.cloned.1.call-start = ((), (), s32[]{:S(2)}) async-start(), calls=%async_computation.18 | async-start | bytes 2949120 | tf_op jit(solution)/shard_map/reduce_scatter | solution.py:804
  305.5 3.1 copy-start.19
  305.5 15.7 %copy-start.8 = (bf16[2,1,64,1024]{3,2,1,0:T(8,128)(2,1)S(1)}, bf16[2,1,64,1024]{3,2,1,0:T(8,128)(2,1)}, u32[]{:S(2)}) copy-start(bf16[2,1,64,1024]{3,2,1,0:T(8,128)(2,1)} %param.13) | copy-start | bytes 786436
  305.5 16.0 %copy-start = (f32[1024,256]{1,0:T(8,128)S(1)}, f32[1024,256]{1,0:T(8,128)}, u32[]{:S(2)}) copy-start(f32[1024,256]{1,0:T(8,128)} %get-tuple-element.32) | copy-start | bytes 3145732
  305.5 219.2 %collective-permute-start.5 = (bf16[512,512]{1,0:T(8,128)(2,1)}, bf16[512,512]{1,0:T(8,128)(2,1)}, u32[]{:S(2)}, u32[]{:S(2)}) collective-permute-start(bf16[512,512]{1,0:T(8,128)(2,1)} %param.20), channel_id=1, source_target_pairs={{0,1},{1,0},{2,3},{3,2},{4,5},{5,4},{6,7},{7,6},{8,9},{9,8},{10,11... | collective-permute-start | bytes 1572872 | tf_op jit(solution)/shard_map/ppermute | solution.py:580
  306.5 220.4 %collective-permute-start.6 = (bf16[512,512]{1,0:T(8,128)(2,1)}, bf16[512,512]{1,0:T(8,128)(2,1)}, u32[]{:S(2)}, u32[]{:S(2)}) collective-permute-start(bf16[512,512]{1,0:T(8,128)(2,1)} %param.21), channel_id=1, source_target_pairs={{0,1},{1,0},{2,3},{3,2},{4,5},{5,4},{6,7},{7,6},{8,9},{9,8},{10,11... | collective-permute-start | bytes 1572872 | tf_op jit(solution)/shard_map/ppermute | solution.py:580
  307.6 221.3 %collective-permute-start.4 = (bf16[512,1024]{1,0:T(8,128)(2,1)}, bf16[512,1024]{1,0:T(8,128)(2,1)}, u32[]{:S(2)}, u32[]{:S(2)}) collective-permute-start(bf16[512,1024]{1,0:T(8,128)(2,1)} %param.19), channel_id=1, source_target_pairs={{0,1},{1,0},{2,3},{3,2},{4,5},{5,4},{6,7},{7,6},{8,9},{9,8},{10,11... | collective-permute-start | bytes 3145736 | tf_op jit(solution)/shard_map/ppermute | solution.py:580
  316.6 54.0 %all-to-all-start.4 = ((f32[8,32,640]{2,1,0:T(8,128)}), f32[8,32,640]{2,1,0:T(8,128)}, u32[]{:S(2)}, u32[]{:S(2)}) async-start(f32[8,32,640]{2,1,0:T(8,128)} %bitcast.243), calls=%async_computation.12 | async-start | bytes 1310720 | tf_op jit(solution)/shard_map/all_to_all | solution.py:780
  370.6 15.8 %all-to-all-start.3 = ((f32[8,32,640]{2,1,0:T(8,128)}), f32[8,32,640]{2,1,0:T(8,128)S(1)}, u32[]{:S(2)}, u32[]{:S(2)}) async-start(f32[8,32,640]{2,1,0:T(8,128)} %bitcast.242), calls=%async_computation.10 | async-start | bytes 1310720 | tf_op jit(solution)/shard_map/all_to_all | solution.py:780
  374.8 144.6 %reduce-scatter.19.cloned.1.call-start = ((), (), s32[]{:S(2)}) async-start(), calls=%async_computation.19 | async-start | bytes 655360 | tf_op jit(solution)/shard_map/reduce_scatter | solution.py:805
  399.3 7.5 %copy-start.1 = (f32[1024,128]{1,0:T(8,128)S(1)}, f32[1024,128]{1,0:T(8,128)}, u32[]{:S(2)}) copy-start(f32[1024,128]{1,0:T(8,128)} %copy.157.cos_ref) | copy-start | bytes 1572868
  417.8 30.5 %copy-start.5 = (f32[1024,32]{1,0:T(8,128)S(1)}, f32[1024,32]{1,0:T(8,128)}, u32[]{:S(2)}) copy-start(f32[1024,32]{1,0:T(8,128)} %copy-done.4) | copy-start | bytes 393220
  450.6 72.3 %all-to-all-start.1 = ((bf16[8,128,256]{2,1,0:T(8,128)(2,1)}), bf16[8,128,256]{2,1,0:T(8,128)(2,1)}, u32[]{:S(2)}, u32[]{:S(2)}) async-start(bf16[8,128,256]{2,1,0:T(8,128)(2,1)} %bitcast.47), calls=%async_computation.4 | async-start | bytes 1048576 | tf_op jit(solution)/shard_map/all_to_all | solution.py:618
  455.2 152.5 %reduce-scatter.15.cloned.1.call-start = ((), (), s32[]{:S(2)}) async-start(), calls=%async_computation.17 | async-start | bytes 1310720 | tf_op jit(solution)/shard_map/reduce_scatter | solution.py:779
  455.2 3.4 copy-start.28
  455.2 3.4 copy-start.29
  458.7 3.8 copy-start.16
  459.7 3.3 copy-start.14
  520.6 93.0 %collective-permute-start.7 = (f32[176,1024]{1,0:T(8,128)S(1)}, f32[176,1024]{1,0:T(8,128)S(1)}, u32[]{:S(2)}, u32[]{:S(2)}) collective-permute-start(f32[176,1024]{1,0:T(8,128)S(1)} %pad_maximum_fusion), channel_id=1, source_target_pairs={{0,0},{1,16},{2,4},{3,20},{4,8},{5,24},{6,12},{7,28},{8,1},{9,17},... | collective-permute-start | bytes 2162696 | tf_op jit(solution)/shard_map/ppermute | solution.py:811
  529.0 77.7 %copy-start.22 = (f32[128,1024]{1,0:T(8,128)S(1)}, f32[128,1024]{1,0:T(8,128)}, u32[]{:S(2)}) copy-start(f32[128,1024]{1,0:T(8,128)} %copy-done.21) | copy-start | bytes 1572868
  607.7 9.3 %all-to-all-start.2 = ((f32[8,32,256]{2,1,0:T(8,128)}), f32[8,32,256]{2,1,0:T(8,128)S(1)}, u32[]{:S(2)}, u32[]{:S(2)}) async-start(f32[8,32,256]{2,1,0:T(8,128)} %bitcast.253), calls=%async_computation.6 | async-start | bytes 524288 | tf_op jit(solution)/shard_map/all_to_all | solution.py:780
  (24 other events, 38.3 us)
Sparse Core Ops, SparseCore 0:
  102.9 33.4 all-gather.3
  158.2 48.4 reduce-scatter.10
  210.0 51.1 reduce-scatter.8
  263.4 53.1 reduce-scatter.22
  318.7 51.7 reduce-scatter.20
  372.3 27.4 all-gather.5
  402.1 44.5 reduce-scatter.12
  449.0 46.9 reduce-scatter.16
  498.2 21.1 reduce-scatter.18
  521.5 59.1 reduce-scatter.14

commit v3 on v2

v3 whole, which is shorter than its diff:
```python
import functools
import math

import jax
import jax.numpy as jnp
from jax import lax
from jax.experimental import pallas as pl
from jax.experimental.pallas import tpu as pltpu
from jax.sharding import Mesh
from jax.sharding import PartitionSpec as P

EPS = 1e-05
ROPE_BASE = 1000000.0
F32 = jnp.float32
BF16 = jnp.bfloat16
HEAD = 64
BLOCK = 128
GROUP = ("inner", "fsdp")
EVERY = ("outer", "inner", "fsdp")


def dot(a, b, dims=((1,), (0,))):
    return lax.dot_general(a, b, (dims, ((), ())), preferred_element_type=F32)


SCORE = 1.0 / math.sqrt(HEAD)
SCORE2 = SCORE * math.log2(math.e)


def place():
    outer, inner, fsdp = (lax.axis_index(name) for name in EVERY)
    return outer, inner, fsdp


def remote(src, dst, send, recv, device):
    return pltpu.make_async_remote_copy(
        src_ref=src,
        dst_ref=dst,
        send_sem=send,
        recv_sem=recv,
        device_id=device,
        device_id_type=pl.DeviceIdType.MESH,
    )


def greet(devices):
    barrier = pltpu.get_barrier_semaphore()
    for device in devices:
        pl.semaphore_signal(
            barrier, inc=1, device_id=device, device_id_type=pl.DeviceIdType.MESH
        )
    return lambda: pl.semaphore_wait(barrier, len(devices))


def chip_peer(k, other_core=0):
    outer, inner, fsdp = place()
    chip = ((inner // 2) * 2 + fsdp + k) % 4
    return (outer, (chip // 2) * 2 + (inner + other_core) % 2, chip % 2)


def sibling():
    outer, inner, fsdp = place()
    return (outer, inner + 1 - 2 * (inner % 2), fsdp)


def group_peer(k):
    outer, inner, fsdp = place()
    member = (inner * 2 + fsdp + k) % 8
    return (outer, member // 2, member % 2)


def member_of(device):
    return device[1] * 2 + device[2]


def slot_of(device):
    return ((device[1] // 2) * 2 + device[2]) * 2 + device[1] % 2


def early_row(member, part):
    return pl.multiple_of(member * part, part)


def late_row(member, part):
    return pl.multiple_of((3 - member // 2) * 2 * part + (member % 2) * part, part)


class Gather:
    def __init__(self, own, land, send, recv):
        self.own, self.land, self.send, self.recv = own, land, send, recv
        self.pieces = range(len(own))

    def copy(self, src, owner, piece, slot, device):
        return remote(
            src,
            self.land(owner)[piece],
            self.send.at[piece, slot],
            self.recv.at[piece, slot_of(owner)],
            device,
        )

    def start(self):
        for k in (1, 2, 3, 0):
            device = chip_peer(k) if k else sibling()
            for piece in self.pieces:
                self.copy(self.own[piece], place(), piece, k, device).start()

    def wait(self, owner):
        for piece in self.pieces:
            dst = self.land(owner)[piece]
            self.copy(dst, owner, piece, 0, sibling()).wait_recv()

    def pass_on(self, k):
        owner = chip_peer(k)
        self.wait(owner)
        for piece in self.pieces:
            self.copy(self.land(owner)[piece], owner, piece, 4 + k, sibling()).start()

    def far(self, k):
        return chip_peer(k, 1)

    def finish(self):
        self.wait(self.far(0))
        for k in (1, 2, 3):
            self.wait(self.far(k))

    def drain(self):
        for slot in (0, 1, 2, 3, 5, 6, 7):
            for piece in self.pieces:
                self.copy(self.own[piece], place(), piece, slot, sibling()).wait_send()


def rms_rows(values, gain):
    inverse = lax.rsqrt(jnp.mean(values * values, axis=-1, keepdims=True) + EPS)
    return values * inverse * gain


def head_inverse(values, low):
    squares = values * values
    first = jnp.sum(jnp.where(low, squares, 0.0), axis=-1, keepdims=True)
    second = jnp.sum(jnp.where(low, 0.0, squares), axis=-1, keepdims=True)
    return jnp.where(
        low, lax.rsqrt(first * (1.0 / HEAD) + EPS), lax.rsqrt(second * (1.0 / HEAD) + EPS)
    )


def halves(values, front):
    quarter = HEAD // 2
    return jnp.where(
        front,
        pltpu.roll(values, values.shape[-1] - quarter, 1),
        pltpu.roll(values, quarter, 1),
    )


def front_kernel(
    x_ref,
    gain_ref,
    weights_any,
    far_any,
    cos_ref,
    sin_ref,
    qg_ref,
    kg_ref,
    normed_out,
    proj_ref,
    q_ref,
    qt_ref,
    kv_ref,
    own,
    land,
    mine_ref,
    other_ref,
    send,
    recv,
    load_sem,
    out_sem,
):
    _, inner, fsdp = place()
    cols = 4 * HEAD
    at = pl.ds(pl.multiple_of((fsdp * 4 + inner) * cols, cols), cols)
    loads = [
        pltpu.make_async_copy(weights_any.at[:, at], mine_ref, load_sem.at[0]),
        pltpu.make_async_copy(far_any, other_ref, load_sem.at[1]),
    ]
    for copy in loads:
        copy.start()
    part = x_ref.shape[1]
    half = land.shape[1]
    width = land.shape[2]
    sub = half // 2
    depth = width // 2
    ready = greet([sibling()] + [chip_peer(k) for k in (1, 2, 3)])
    for late in range(2):
        rows = x_ref[late].astype(F32)
        own[late] = rms_rows(rows, gain_ref[...]).astype(BF16)
    ready()

    def slots(device):
        member = member_of(device)
        return [
            land.at[0, pl.ds(early_row(member, part), part)],
            land.at[1, pl.ds(late_row(member, part), part)],
        ]

    gather = Gather([own.at[0], own.at[1]], slots, send, recv)
    gather.start()
    member = member_of(place())
    land[0, pl.ds(early_row(member, part), part)] = own[0]
    land[1, pl.ds(late_row(member, part), part)] = own[1]
    for k in (1, 3, 2):
        gather.pass_on(k)
    gather.finish()
    out = pltpu.make_async_copy(land, normed_out, out_sem)
    out.start()
    for copy in loads:
        copy.wait()

    lane = lax.broadcasted_iota(jnp.int32, (sub, 2 * HEAD), 1)
    low = lane < HEAD
    front = lane % HEAD < HEAD // 2
    mine_at = pl.ds(pl.multiple_of(fsdp * depth, depth), depth)
    other_at = pl.ds(pl.multiple_of((1 - fsdp) * depth, depth), depth)

    @pl.loop(0, 4)
    def _(tile):
        late = tile // 2
        inside = pl.ds(pl.multiple_of((tile % 2) * sub, sub), sub)
        rows = pl.ds(pl.multiple_of(tile * sub, sub), sub)
        proj = dot(land[late, inside, mine_at], mine_ref[...])
        proj = proj + dot(land[late, inside, other_at], other_ref[...])
        proj_ref[rows, :] = proj
        cos, sin = cos_ref[rows, :], sin_ref[rows, :]
        raw = proj[:, : 2 * HEAD]
        normed = raw * head_inverse(raw, low) * qg_ref[...]
        rotated = normed * cos + halves(normed, front) * sin
        second = pltpu.roll(rotated, HEAD, 1)
        for head, values in enumerate((rotated, second)):
            values = jnp.where(low, values, 0.0)
            cols = pl.ds(pl.multiple_of(tile * 2 * sub + head * sub, sub), sub)
            q_ref[cols, :] = values.astype(BF16)
            qt_ref[:, cols] = values.T.astype(BF16)
        raw = proj[:, 2 * HEAD :]
        normed = raw * head_inverse(raw, low) * kg_ref[...]
        rotated = normed * cos + halves(normed, front) * sin
        kv_ref[rows, :] = jnp.where(low, rotated, raw).astype(BF16)

    gather.drain()
    out.wait()


def middle_kernel(
    steps,
    x_ref,
    dy_ref,
    qt_ref,
    kv_ref,
    wo_mine,
    wo_other,
    gain_ref,
    kv_out,
    cot_out,
    attn_t_ref,
    log_ref,
    attn_ref,
    residual_ref,
    ffn_ref,
    kv_all,
    acc_ref,
    total_ref,
    token_rows,
    dy_send,
    dy_recv,
    kv_send,
    kv_recv,
    swap_send,
    swap_recv,
    out_sem,
):
    outer, inner, fsdp = place()
    me = member_of((outer, inner, fsdp))
    part = x_ref.shape[1]
    half = kv_ref.shape[0] // 2
    sub = half // 2
    wide = 2 * sub
    width = x_ref.shape[2]
    depth = width // 2

    def outer_peer(k):
        return ((outer + k) % steps, inner, fsdp)

    ready = greet(
        [outer_peer(k) for k in range(1, steps)] + [group_peer(k) for k in range(1, 8)]
    )
    kv_all[outer] = kv_ref[...]
    acc_ref[...] = jnp.zeros_like(acc_ref)
    total_ref[...] = jnp.zeros_like(total_ref)
    ready()
    for k in range(1, steps):
        remote(
            kv_ref, kv_all.at[outer], kv_send.at[k], kv_recv.at[outer], outer_peer(steps - k)
        ).start()
    cot = Gather(
        [dy_ref.at[n] for n in range(2)],
        lambda device: [cot_out.at[slot_of(device), n] for n in range(2)],
        dy_send,
        dy_recv,
    )
    cot.start()
    own_dy = pltpu.make_async_copy(dy_ref, cot_out.at[slot_of(place())], out_sem.at[0])
    own_dy.start()

    def block(slot, row, size, col, mask):
        kv = kv_all[slot, pl.ds(pl.multiple_of(row, sub), size), :]
        cols = pl.ds(pl.multiple_of(col, wide), wide)
        probs = jnp.exp2(dot(kv, qt_ref[:, cols]) * SCORE2)
        if mask is not None:
            probs = jnp.where(mask, probs, 0.0)
        total_ref[:, cols] += jnp.sum(probs.reshape(size // 8, 8, wide), axis=0)
        acc_ref[:, cols] += dot(kv, probs.astype(BF16), ((0,), (0,)))

    key = lax.broadcasted_iota(jnp.int32, (sub, wide), 0)
    query = lax.broadcasted_iota(jnp.int32, (sub, wide), 1) % sub
    diagonal = key <= query

    @pl.loop(0, 2)
    def _(late):
        block(outer, late * half, sub, late * 2 * wide, diagonal)
        block(outer, late * half, sub, late * 2 * wide + wide, None)
        block(outer, late * half + sub, sub, late * 2 * wide + wide, diagonal)

    @pl.loop(0, 2)
    def _(n):
        block(outer, 0, half, (2 + n) * wide, None)

    @pl.loop(1, steps)
    def _(k):
        slot = (outer + k) % steps
        late = jnp.where(slot < outer, 0, 1)
        remote(
            kv_ref, kv_all.at[slot], kv_send.at[k], kv_recv.at[slot], outer_peer(k)
        ).wait_recv()

        @pl.loop(0, 2)
        def _(n):
            block(slot, 0, half, (2 + n) * wide, None)
            block(slot, late * half, half, (late * 2 + n) * wide, None)

    kv_copy = pltpu.make_async_copy(kv_all, kv_out, out_sem.at[1])
    kv_copy.start()

    @pl.loop(0, 4)
    def _(tile):
        heads = []
        for head in range(2):
            cols = pl.ds(pl.multiple_of(tile * wide + head * sub, sub), sub)
            total = jnp.sum(total_ref[:, cols], axis=0, keepdims=True)
            values = acc_ref[HEAD:, cols] / total
            attn_t_ref[:, cols] = values
            log_ref[:, cols] = jnp.log2(total)
            heads.append(values)
        inside = pl.ds(pl.multiple_of((tile % 2) * sub, sub), sub)
        attn_ref[tile // 2, inside, :] = jnp.concatenate(heads, axis=0).T.astype(BF16)

    lane = fsdp * 4 + inner

    def chunk(member):
        return [
            attn_ref.at[0, pl.ds(early_row(member, part), part)],
            attn_ref.at[1, pl.ds(late_row(member, part), part)],
        ]

    def landing(source):
        cols = pl.ds(pl.multiple_of(source * 2 * HEAD, 2 * HEAD), 2 * HEAD)
        return [token_rows.at[n, :, cols] for n in range(2)]

    swaps = []
    for k in range(1, 8):
        device = group_peer(k)
        for n in range(2):
            swaps.append(
                remote(
                    chunk(member_of(device))[n],
                    landing(lane)[n],
                    swap_send.at[n, k],
                    swap_recv.at[n, lane],
                    device,
                )
            )
            swaps[-1].start()
    own_cols = pl.ds(pl.multiple_of(lane * 2 * HEAD, 2 * HEAD), 2 * HEAD)
    token_rows[0, :, own_cols] = attn_ref[0, pl.ds(early_row(me, part), part), :]
    token_rows[1, :, own_cols] = attn_ref[1, pl.ds(late_row(me, part), part), :]
    for k in range(1, 8):
        device = group_peer(k)
        source = device[2] * 4 + device[1]
        for n in range(2):
            remote(
                landing(source)[n],
                landing(source)[n],
                swap_send.at[n, k],
                swap_recv.at[n, source],
                device,
            ).wait_recv()

    mine_at = pl.ds(pl.multiple_of(fsdp * depth, depth), depth)
    other_at = pl.ds(pl.multiple_of((1 - fsdp) * depth, depth), depth)
    for n in range(2):
        values = dot(token_rows[n, :, mine_at], wo_mine[...])
        values = values + dot(token_rows[n, :, other_at], wo_other[...])
        values = values + x_ref[n].astype(F32)
        residual_ref[n] = values
        ffn_ref[n] = rms_rows(values, gain_ref[...]).astype(BF16)

    for k in (1, 3, 2):
        cot.pass_on(k)
    cot.finish()
    cot.drain()
    for copy in swaps:
        copy.wait_send()
    for k in range(1, steps):
        remote(
            kv_ref, kv_all.at[outer], kv_send.at[k], kv_recv.at[outer], outer_peer(steps - k)
        ).wait_send()
    own_dy.wait()
    kv_copy.wait()


SMEM = pl.BlockSpec(memory_space=pltpu.SMEM)
VMEM = pl.BlockSpec(memory_space=pltpu.VMEM)
ANY = pl.BlockSpec(memory_space=pl.ANY)
DMA = pltpu.SemaphoreType.DMA


def params(collective):
    return pltpu.CompilerParams(
        collective_id=collective, has_side_effects=True, vmem_limit_bytes=60 << 20
    )


def front(x, gain, weights, far, cos, sin, q_gain, k_gain):
    part, width = x.shape[1:]
    tokens = cos.shape[0]
    half = tokens // 2
    return pl.pallas_call(
        front_kernel,
        out_shape=(
            jax.ShapeDtypeStruct((2, half, width), BF16),
            jax.ShapeDtypeStruct((tokens, 4 * HEAD), F32),
            jax.ShapeDtypeStruct((2 * tokens, 2 * HEAD), BF16),
            jax.ShapeDtypeStruct((2 * HEAD, 2 * tokens), BF16),
            jax.ShapeDtypeStruct((tokens, 2 * HEAD), BF16),
        ),
        in_specs=[VMEM] * 2 + [ANY] * 2 + [VMEM] * 4,
        out_specs=[ANY, VMEM, VMEM, VMEM, VMEM],
        scratch_shapes=[
            pltpu.VMEM((2, part, width), BF16),
            pltpu.VMEM((2, half, width), BF16),
            pltpu.VMEM(far.shape, BF16),
            pltpu.VMEM(far.shape, BF16),
            DMA((2, 8)),
            DMA((2, 8)),
            DMA((2,)),
            DMA,
        ],
        compiler_params=params(0),
        name="front",
    )(x, gain, weights, far, cos, sin, q_gain, k_gain)


def middle(x, dy, qt, kv, wo_mine, wo_other, gain, steps):
    part, width = x.shape[1:]
    tokens = kv.shape[0]
    half = tokens // 2
    return pl.pallas_call(
        functools.partial(middle_kernel, steps),
        out_shape=(
            jax.ShapeDtypeStruct((steps, tokens, 2 * HEAD), BF16),
            jax.ShapeDtypeStruct((8, 2, part, width), BF16),
            jax.ShapeDtypeStruct((HEAD, 2 * tokens), F32),
            jax.ShapeDtypeStruct((1, 2 * tokens), F32),
            jax.ShapeDtypeStruct((2, half, 2 * HEAD), BF16),
            jax.ShapeDtypeStruct((2, part, width), F32),
            jax.ShapeDtypeStruct((2, part, width), BF16),
        ),
        in_specs=[VMEM] * 7,
        out_specs=[ANY, ANY] + [VMEM] * 5,
        scratch_shapes=[
            pltpu.VMEM((steps, tokens, 2 * HEAD), BF16),
            pltpu.VMEM((2 * HEAD, 2 * tokens), F32),
            pltpu.VMEM((8, 2 * tokens), F32),
            pltpu.VMEM((2, part, width), BF16),
            DMA((2, 8)),
            DMA((2, 8)),
            DMA((steps,)),
            DMA((steps,)),
            DMA((2, 8)),
            DMA((2, 8)),
            DMA((2,)),
        ],
        compiler_params=params(1),
        name="middle",
    )(x, dy, qt, kv, wo_mine, wo_other, gain)


def ffn_kernel(
    steps,
    ffn_ref,
    residual_ref,
    dy_ref,
    attn_ref,
    gain_ref,
    cot_any,
    gate_any,
    gate_far,
    up_any,
    up_far,
    down_any,
    wo_any,
    wo_far,
    out_ref,
    d_res_ref,
    grad_ref,
    d_gain_ref,
    d_gate_ref,
    d_up_ref,
    d_down_ref,
    d_wo_ref,
    gate,
    up,
    down,
    wo,
    cot,
    land,
    d_hidden,
    hidden,
    d_gate,
    d_up,
    sum_send,
    sum_land,
    out_send,
    out_land,
    d_down,
    res_own,
    res_land,
    swap_own,
    load_sem,
    ffn_send,
    ffn_recv,
    sum_ssem,
    sum_rsem,
    out_ssem,
    out_rsem,
    res_send,
    res_recv,
    swap_send,
    swap_recv,
):
    here = place()
    outer, inner, fsdp = here
    part = ffn_ref.shape[1]
    width = ffn_ref.shape[2]
    depth = width // 2
    rows = 2 * part
    pair = 2 * rows
    reach = gate.shape[1]
    odd = inner % 2
    chip = (inner // 2) * 2 + fsdp
    my_slot = slot_of(here)
    me = member_of(here)
    lane = fsdp * 4 + inner
    tiles = 2 * (reach // BLOCK) - 1
    step = (reach // BLOCK - 1) * BLOCK
    start = pl.multiple_of((lane // 2) * tiles * BLOCK + odd * step, BLOCK)
    down_start = pl.multiple_of((inner // 2) * tiles * BLOCK + odd * step, BLOCK)
    mine_at = pl.ds(pl.multiple_of(fsdp * depth, depth), depth)
    far_at = pl.ds(pl.multiple_of((1 - fsdp) * depth, depth), depth)
    pad = BLOCK // 2

    ready = greet([group_peer(k) for k in range(1, 8)])
    loads = [
        pltpu.make_async_copy(src, dst, load_sem.at[n])
        for n, (src, dst) in enumerate(
            (
                (down_any.at[pl.ds(down_start, reach)], down),
                (cot_any, cot),
                (gate_any.at[:, pl.ds(start, reach)], gate.at[mine_at]),
                (gate_far, gate.at[far_at]),
                (up_any.at[:, pl.ds(start, reach)], up.at[mine_at]),
                (up_far, up.at[far_at]),
                (wo_any, wo.at[mine_at]),
                (wo_far, wo.at[far_at]),
            )
        )
    ]
    for copy in loads:
        copy.start()
    ready()
    gather = Gather(
        [ffn_ref],
        lambda device: [land.at[pl.ds(pl.multiple_of(slot_of(device) * 2, 2), 2)]],
        ffn_send,
        ffn_recv,
    )
    gather.start()
    land[pl.ds(pl.multiple_of(my_slot * 2, 2), 2)] = ffn_ref[...]
    loads[0].wait()
    loads[1].wait()

    def chip_rows(n):
        return pl.ds(pl.multiple_of(((chip + n) % 4) * pair, pair), pair)

    def four(n):
        return pl.ds(pl.multiple_of(((chip + n) % 4) * 4, 4), 4)

    @pl.loop(0, 4)
    def _(n):
        values = cot[four(n)].reshape(pair, width)
        d_hidden[chip_rows(n), :] = dot(values, down[...], ((1,), (1,)))

    for copy in loads[2:6]:
        copy.wait()
    col = lax.broadcasted_iota(jnp.int32, (pair, reach), 1)
    valid = (col >= odd * pad) & (col < reach - pad + odd * pad)

    def outgoing(n, core):
        device_chip = (chip + n) % 4
        return (outer, (device_chip // 2) * 2 + core, device_chip % 2)

    def send_rows(n, src, dst, ssem, rsem):
        for flip in range(2):
            core = (odd + flip) % 2
            device = outgoing(n, core)
            slot = slot_of(device)
            copy = remote(src.at[slot], dst.at[my_slot], ssem.at[slot], rsem.at[my_slot], device)
            if flip:
                copy.start()
            else:
                pl.when(n > 0)(copy.start)

    @pl.loop(0, 4)
    def _(n):
        @pl.when(n > 0)
        def _():
            gather.pass_on(n)

        gather.wait(chip_peer(n, 1))
        at = chip_rows(n)
        values = land[four(n)].reshape(pair, width)
        gate_pre = dot(values, gate[...])
        up_pre = dot(values, up[...])
        sigmoid = jax.nn.sigmoid(gate_pre)
        silu = gate_pre * sigmoid
        hidden[at, :] = jnp.where(valid, silu * up_pre, 0.0).astype(BF16)
        back = jnp.where(valid, d_hidden[at, :], 0.0)
        d_gate[at, :] = (back * up_pre * sigmoid * (1.0 + gate_pre * (1.0 - sigmoid))).astype(BF16)
        d_up[at, :] = (back * silu).astype(BF16)
        total = dot(d_gate[at, :], gate[...], ((1,), (1,)))
        total = total + dot(d_up[at, :], up[...], ((1,), (1,)))
        slots = pl.ds(pl.multiple_of(((chip + n) % 4) * 2, 2), 2)
        sum_send[slots] = total.reshape(2, rows, width).astype(BF16)
        send_rows(n, sum_send, sum_land, sum_ssem, sum_rsem)

    @pl.loop(0, 4)
    def _(n):
        total = dot(hidden[chip_rows(n), :], down[...])
        slots = pl.ds(pl.multiple_of(((chip + n) % 4) * 2, 2), 2)
        out_send[slots] = total.reshape(2, rows, width).astype(BF16)
        send_rows(n, out_send, out_land, out_ssem, out_rsem)

    def receive(src, land_ref, ssem, rsem):
        total = src[my_slot].astype(F32)
        for k in range(1, 8):
            device = group_peer(k)
            slot = slot_of(device)
            remote(
                src.at[slot], land_ref.at[slot], ssem.at[slot], rsem.at[slot], device
            ).wait_recv()
            total = total + land_ref[slot].astype(F32)
        return total

    def weight_tile(left, right, ref, tile, per):
        at = pl.ds(pl.multiple_of(tile * BLOCK, BLOCK), BLOCK)
        value = dot(left[:, at], right[...], ((0,), (0,)))
        count = BLOCK // per
        ref[pl.ds(tile * count, count)] = value.reshape(count, per, reach).astype(BF16)

    cot_rows = cot.reshape(8 * rows, width)
    land_rows = land.reshape(8 * rows, width)

    @pl.loop(0, reach // BLOCK)
    def _(tile):
        at = pl.ds(pl.multiple_of(tile * BLOCK, BLOCK), BLOCK)
        d_down[at, :] = dot(hidden[:, at], cot_rows[...], ((0,), (0,)))

    for copy in loads[6:]:
        copy.wait()
    error = receive(sum_send, sum_land, sum_ssem, sum_rsem)
    residual = residual_ref[...].reshape(rows, width)
    inverse = lax.rsqrt(jnp.mean(residual * residual, axis=-1, keepdims=True) + EPS)
    scaled = error * gain_ref[...]
    inner_mean = jnp.mean(scaled * residual, axis=-1, keepdims=True)
    back = inverse * scaled - residual * (inverse * inverse * inverse) * inner_mean
    d_gain_ref[...] = jnp.sum(error * residual * inverse, axis=0, keepdims=True)
    d_residual = dy_ref[...].reshape(rows, width).astype(F32) + back
    d_res_ref[...] = d_residual.reshape(2, part, width)
    res_own[...] = d_residual.astype(BF16).reshape(2, part, width)
    attn_grad = dot(d_residual.astype(BF16), wo[...], ((1,), (1,)))
    swap_own[...] = attn_grad.astype(BF16).reshape(2, part, width)

    def head_cols(device):
        source = device[2] * 4 + device[1]
        return pl.ds(pl.multiple_of(source * 2 * HEAD, 2 * HEAD), 2 * HEAD)

    def token_at(ref, device):
        member = member_of(device)
        return [
            ref.at[0, pl.ds(early_row(member, part), part)],
            ref.at[1, pl.ds(late_row(member, part), part)],
        ]

    def swap_copy(k, n, owner):
        device = group_peer(k)
        return remote(
            swap_own.at[n, :, head_cols(device)],
            token_at(grad_ref, owner)[n],
            swap_send.at[n, k],
            swap_recv.at[n, slot_of(owner)],
            device,
        )

    for k in range(1, 8):
        for n in range(2):
            swap_copy(k, n, here).start()
    wide = Gather(
        [res_own.at[0], res_own.at[1]],
        lambda device: token_at(res_land, device),
        res_send,
        res_recv,
    )
    wide.start()
    grad_ref[0, pl.ds(early_row(me, part), part)] = swap_own[0, :, head_cols(here)]
    grad_ref[1, pl.ds(late_row(me, part), part)] = swap_own[1, :, head_cols(here)]
    res_land[0, pl.ds(early_row(me, part), part)] = res_own[0]
    res_land[1, pl.ds(late_row(me, part), part)] = res_own[1]

    per = d_gate_ref.shape[1]

    @pl.loop(0, width // BLOCK)
    def _(tile):
        weight_tile(land_rows, d_gate, d_gate_ref, tile, per)
        weight_tile(land_rows, d_up, d_up_ref, tile, per)

    for k in (1, 3, 2):
        wide.pass_on(k)
    total = receive(out_send, out_land, out_ssem, out_rsem)
    out_ref[...] = (total + residual_ref[...].reshape(rows, width)).reshape(
        2, part, width
    ).astype(BF16)

    down_per = d_down_ref.shape[1]

    for z in range(steps):
        at = z * down_per
        even_rows = d_down[at : at + down_per, :]
        odd_rows = d_down[at + pad : at + pad + down_per, :]
        d_down_ref[z] = jnp.where(odd > 0, odd_rows, even_rows).astype(BF16)

    wide.finish()
    half = res_land.shape[1]
    value = dot(
        attn_ref[...].reshape(2 * half, 2 * HEAD),
        res_land[...].reshape(2 * half, width),
        ((0,), (0,)),
    )
    d_wo_ref[...] = value.reshape(d_wo_ref.shape).astype(BF16)
    for k in range(1, 8):
        device = group_peer(k)
        for n in range(2):
            swap_copy(k, n, device).wait_recv()
            swap_copy(k, n, here).wait_send()
        slot = slot_of(device)
        remote(
            sum_send.at[slot], sum_land.at[slot], sum_ssem.at[slot], sum_rsem.at[slot], device
        ).wait_send()
        remote(
            out_send.at[slot], out_land.at[slot], out_ssem.at[slot], out_rsem.at[slot], device
        ).wait_send()
    gather.drain()
    wide.drain()


def ffn(ffn_rows, residual, dy, attn, gain, cot, weights, steps, devices):
    part, width = ffn_rows.shape[1:]
    gate, gate_far, up, up_far, down, wo, wo_far = weights
    reach = gate_far.shape[1]
    own_ff = reach - BLOCK // 2
    rows = 2 * part
    half = attn.shape[1]
    tokens = 2 * half
    block = pltpu.VMEM((8, rows, width), BF16)
    return pl.pallas_call(
        functools.partial(ffn_kernel, steps),
        out_shape=(
            jax.ShapeDtypeStruct((2, part, width), BF16),
            jax.ShapeDtypeStruct((2, part, width), F32),
            jax.ShapeDtypeStruct((2, half, 2 * HEAD), BF16),
            jax.ShapeDtypeStruct((1, width), F32),
            jax.ShapeDtypeStruct((devices, width // devices, reach), BF16),
            jax.ShapeDtypeStruct((devices, width // devices, reach), BF16),
            jax.ShapeDtypeStruct((steps, own_ff // steps, width), BF16),
            jax.ShapeDtypeStruct((steps, 2 * HEAD // steps, width), BF16),
        ),
        in_specs=[VMEM] * 5 + [ANY] * 8,
        out_specs=[VMEM] * 8,
        scratch_shapes=[
            pltpu.VMEM((width, reach), BF16),
            pltpu.VMEM((width, reach), BF16),
            pltpu.VMEM((reach, width), BF16),
            pltpu.VMEM((width, width), BF16),
            pltpu.VMEM((16, part, width), BF16),
            pltpu.VMEM((16, part, width), BF16),
            pltpu.VMEM((tokens, reach), F32),
            pltpu.VMEM((tokens, reach), BF16),
            pltpu.VMEM((tokens, reach), BF16),
            pltpu.VMEM((tokens, reach), BF16),
            block,
            block,
            block,
            block,
            pltpu.VMEM((reach, width), F32),
            pltpu.VMEM((2, part, width), BF16),
            pltpu.VMEM((2, half, width), BF16),
            pltpu.VMEM((2, part, width), BF16),
            DMA((8,)),
            DMA((1, 8)),
            DMA((1, 8)),
            DMA((8,)),
            DMA((8,)),
            DMA((8,)),
            DMA((8,)),
            DMA((2, 8)),
            DMA((2, 8)),
            DMA((2, 8)),
            DMA((2, 8)),
        ],
        compiler_params=params(2),
        name="ffn",
    )(ffn_rows, residual, dy, attn, gain, cot, gate, gate_far, up, up_far, down, wo, wo_far)


def member_device(number):
    return (number // 8, number % 8 // 2, number % 2)


def number_of(device):
    return device[0] * 8 + device[1] * 2 + device[2]


def lane_of(device):
    return device[2] * 4 + device[1]


def lane_device(outer, lane):
    return (outer, lane % 4, lane // 4)


def back_kernel(
    steps,
    qt_ref,
    q_ref,
    grad_ref,
    attn_t_ref,
    log_ref,
    kv_ref,
    proj_ref,
    cos_ref,
    sin_ref,
    qg_ref,
    kg_ref,
    x_ref,
    d_res_ref,
    gain_ref,
    ffn_gain_ref,
    normed_any,
    weights_any,
    far_any,
    d_gate_any,
    d_up_any,
    d_down_any,
    d_wo_any,
    dx_ref,
    gains_ref,
    own_q_ref,
    own_k_ref,
    own_v_ref,
    own_o_ref,
    own_gate_ref,
    own_up_ref,
    own_down_ref,
    normed,
    weights,
    far,
    gt_ref,
    g_ref,
    delta_ref,
    acc_ref,
    dkv_ref,
    dkv_send,
    dkv_land,
    d_qkv,
    tokens_land,
    d_weights,
    gate_land,
    up_land,
    qkv_land,
    down_land,
    wo_land,
    sums,
    sums_land,
    load_sem,
    gate_send,
    gate_recv,
    up_send,
    up_recv,
    qkv_send,
    qkv_recv,
    down_send,
    down_recv,
    wo_send,
    wo_recv,
    kv_send,
    kv_recv,
    swap_send,
    swap_recv,
    near_send,
    near_recv,
    far_send,
    far_recv,
):
    here = place()
    outer, inner, fsdp = here
    lane = lane_of(here)
    number = number_of(here)
    me = member_of(here)
    count = steps * 8
    part, width = x_ref.shape[1:]
    rows = 2 * part
    half = normed.shape[1]
    sub = half // 2
    wide = 2 * sub
    depth = width // 2

    barrier = pltpu.get_barrier_semaphore()

    @pl.loop(1, count)
    def _(k):
        pl.semaphore_signal(
            barrier,
            inc=1,
            device_id=member_device((number + k) % count),
            device_id_type=pl.DeviceIdType.MESH,
        )

    loads = [
        pltpu.make_async_copy(src, dst, load_sem.at[n])
        for n, (src, dst) in enumerate(
            ((normed_any, normed), (weights_any, weights), (far_any, far))
        )
    ]
    for copy in loads:
        copy.start()
    acc_ref[...] = jnp.zeros_like(acc_ref)
    dkv_ref[...] = jnp.zeros_like(dkv_ref)
    low = lax.broadcasted_iota(jnp.int32, (sub, 2 * HEAD), 1) < HEAD
    front = lax.broadcasted_iota(jnp.int32, (sub, 2 * HEAD), 1) % HEAD < HEAD // 2

    @pl.loop(0, 4)
    def _(tile):
        inside = pl.ds(pl.multiple_of((tile % 2) * sub, sub), sub)
        values = grad_ref[tile // 2, inside, :].astype(F32)
        flipped = pltpu.roll(values, HEAD, 1)
        for head, shifted in enumerate((flipped, values)):
            cols = pl.ds(pl.multiple_of(tile * wide + head * sub, sub), sub)
            shifted = jnp.where(low, 0.0, shifted)
            turned = shifted.T
            g_ref[cols, :] = shifted.astype(BF16)
            gt_ref[:, cols] = turned.astype(BF16)
            delta_ref[:, cols] = jnp.sum(
                turned[HEAD:] * attn_t_ref[:, cols], axis=0, keepdims=True
            )

    pl.semaphore_wait(barrier, count - 1)

    def rows_copy(src, land, ssem, rsem, target, source):
        key = lane_of(source) * steps + source[0]
        owner = number_of(target)
        return remote(src.at[owner], land.at[key], ssem.at[owner], rsem.at[key], target)

    def slice_copy(src, land, ssem, rsem, chunk, source):
        target = member_device(lane * steps + chunk)
        return remote(src.at[chunk], land.at[source], ssem.at[chunk], rsem.at[source], target)

    slices = (
        (d_down_any, down_land, down_send, down_recv),
        (d_wo_any, wo_land, wo_send, wo_recv),
    )
    mine = number // steps == lane

    @pl.loop(0, steps)
    def _(k):
        chunk = (outer + k) % steps
        away = lane * steps + chunk != number

        @pl.when(away)
        def _():
            for refs in slices:
                slice_copy(*refs, chunk, outer).start()

    @pl.when(mine)
    def _():
        for n, (src, land, _, _) in enumerate(slices):
            copy = pltpu.make_async_copy(
                src.at[number % steps], land.at[outer], load_sem.at[3 + n]
            )
            copy.start()
            copy.wait()

    def outer_peer(k):
        return ((outer + k) % steps, inner, fsdp)

    def block(slot, row, size, col, mask):
        at = pl.ds(pl.multiple_of(row, sub), size)
        kv = kv_ref[slot, at, :]
        cols = pl.ds(pl.multiple_of(col, wide), wide)
        probs = jnp.exp2(dot(kv, qt_ref[:, cols]) * SCORE2 - log_ref[:, cols])
        if mask is not None:
            probs = jnp.where(mask, probs, 0.0)
        grads = dot(kv, gt_ref[:, cols])
        grads = (probs * (grads - delta_ref[:, cols]) * SCORE).astype(BF16)
        dkv_ref[slot, at, :] += dot(grads, q_ref[cols, :]) + dot(
            probs.astype(BF16), g_ref[cols, :]
        )
        acc_ref[:, cols] += dot(kv, grads, ((0,), (0,)))

    def kv_copy(slot, late, source):
        at = pl.ds(late * half, half)
        return remote(
            dkv_send.at[slot, at],
            dkv_land.at[source, at],
            kv_send.at[late, slot],
            kv_recv.at[late, source],
            (slot, inner, fsdp),
        )

    @pl.loop(1, steps)
    def _(k):
        slot = (outer + k) % steps
        late = jnp.where(slot < outer, 0, 1)

        @pl.loop(0, 2)
        def _(n):
            block(slot, 0, half, (2 + n) * wide, None)
            block(slot, late * half, half, (late * 2 + n) * wide, None)

        dkv_send[slot] = dkv_ref[slot].astype(BF16)
        kv_copy(slot, 0, outer).start()

        @pl.when(slot > outer)
        def _():
            kv_copy(slot, 1, outer).start()

    key = lax.broadcasted_iota(jnp.int32, (sub, wide), 0)
    query = lax.broadcasted_iota(jnp.int32, (sub, wide), 1) % sub
    diagonal = key <= query

    @pl.loop(0, 2)
    def _(late):
        block(outer, late * half, sub, late * 2 * wide, diagonal)
        block(outer, late * half, sub, late * 2 * wide + wide, None)
        block(outer, late * half + sub, sub, late * 2 * wide + wide, diagonal)

    @pl.loop(0, 2)
    def _(n):
        block(outer, 0, half, (2 + n) * wide, None)

    def rope_back(grads, at):
        return grads * cos_ref[at, :] + halves(grads * sin_ref[at, :], front)

    def norm_back(raw, grads, gain):
        inverse = head_inverse(raw, low)
        scaled = grads * gain
        product = scaled * raw
        first = jnp.sum(jnp.where(low, product, 0.0), axis=-1, keepdims=True)
        second = jnp.sum(jnp.where(low, 0.0, product), axis=-1, keepdims=True)
        inner_mean = jnp.where(low, first, second) * (1.0 / HEAD)
        back = inverse * scaled - raw * (inverse * inverse * inverse) * inner_mean
        return back, jnp.sum(grads * raw * inverse, axis=0, keepdims=True)

    sums[...] = jnp.zeros_like(sums)

    @pl.loop(0, 4)
    def _(tile):
        heads = []
        for head in range(2):
            cols = pl.ds(pl.multiple_of(tile * wide + head * sub, sub), sub)
            heads.append(acc_ref[:HEAD, cols])
        at = pl.ds(pl.multiple_of(tile * sub, sub), sub)
        inside = pl.ds(pl.multiple_of((tile % 2) * sub, sub), sub)
        grads = rope_back(jnp.concatenate(heads, axis=0).T, at)
        back, gain = norm_back(proj_ref[at, : 2 * HEAD], grads, qg_ref[...])
        d_qkv[tile // 2, inside, : 2 * HEAD] = back.astype(BF16)
        sums[2:3, : 2 * HEAD] += gain

    @pl.loop(1, steps)
    def _(k):
        source = (outer + k) % steps
        kv_copy(source, 0, source).wait_recv()
        early = pl.ds(0, half)
        dkv_ref[outer, early, :] += dkv_land[source, early, :].astype(F32)

        @pl.when(source < outer)
        def _():
            kv_copy(source, 1, source).wait_recv()
            at = pl.ds(half, half)
            dkv_ref[outer, at, :] += dkv_land[source, at, :].astype(F32)

    @pl.loop(1, count)
    def _(k):
        target = member_device((number + k) % count)
        rows_copy(d_gate_any, gate_land, gate_send, gate_recv, target, here).start()
        rows_copy(d_up_any, up_land, up_send, up_recv, target, here).start()

    own_key = lane * steps + outer
    own_rows = [
        pltpu.make_async_copy(src.at[number], land.at[own_key], load_sem.at[n])
        for n, (src, land) in ((3, (d_gate_any, gate_land)), (4, (d_up_any, up_land)))
    ]
    for copy in own_rows:
        copy.start()

    @pl.loop(0, 4)
    def _(tile):
        at = pl.ds(pl.multiple_of(tile * sub, sub), sub)
        inside = pl.ds(pl.multiple_of((tile % 2) * sub, sub), sub)
        grads = dkv_ref[outer, at, :]
        raw = proj_ref[at, 2 * HEAD :]
        back, gain = norm_back(raw, jnp.where(low, rope_back(grads, at), 0.0), kg_ref[...])
        d_qkv[tile // 2, inside, 2 * HEAD :] = jnp.where(low, back, grads).astype(BF16)
        sums[2:3, 2 * HEAD : 4 * HEAD] += gain

    def token_at(ref, device):
        member = member_of(device)
        return [
            ref.at[0, pl.ds(early_row(member, part), part)],
            ref.at[1, pl.ds(late_row(member, part), part)],
        ]

    def lane_cols(device):
        return pl.ds(pl.multiple_of(lane_of(device) * 4 * HEAD, 4 * HEAD), 4 * HEAD)

    def swap_copy(k, n, owner):
        device = group_peer(k)
        return remote(
            token_at(d_qkv, device)[n],
            tokens_land.at[n, :, lane_cols(owner)],
            swap_send.at[n, k],
            swap_recv.at[n, slot_of(owner)],
            device,
        )

    for k in range(1, 8):
        for n in range(2):
            swap_copy(k, n, here).start()
    tokens_land[0, :, lane_cols(here)] = d_qkv[0, pl.ds(early_row(me, part), part), :]
    tokens_land[1, :, lane_cols(here)] = d_qkv[1, pl.ds(late_row(me, part), part), :]

    for copy in loads:
        copy.wait()
    per = d_weights.shape[1]
    normed_rows = normed.reshape(2 * half, width)
    d_rows = d_qkv.reshape(2 * half, 4 * HEAD)

    @pl.loop(0, width // BLOCK)
    def _(tile):
        at = pl.ds(pl.multiple_of(tile * BLOCK, BLOCK), BLOCK)
        value = dot(normed_rows[:, at], d_rows[...], ((0,), (0,)))
        many = BLOCK // per
        d_weights[pl.ds(tile * many, many)] = value.reshape(many, per, 4 * HEAD).astype(BF16)

    @pl.loop(1, count)
    def _(k):
        target = member_device((number + k) % count)
        rows_copy(d_weights, qkv_land, qkv_send, qkv_recv, target, here).start()

    qkv_land[own_key] = d_weights[number]

    for k in range(1, 8):
        for n in range(2):
            swap_copy(k, n, group_peer(k)).wait_recv()
    mine_at = pl.ds(pl.multiple_of(fsdp * depth, depth), depth)
    far_at = pl.ds(pl.multiple_of((1 - fsdp) * depth, depth), depth)
    grads = tokens_land[...].reshape(rows, 8 * 4 * HEAD)
    flat = dx_ref.reshape(rows, width)
    flat[:, mine_at] = dot(grads, weights[...], ((1,), (1,)))
    flat[:, far_at] = dot(grads, far[...], ((1,), (1,)))
    error = flat[...]
    inputs = x_ref[...].reshape(rows, width).astype(F32)
    inverse = lax.rsqrt(jnp.mean(inputs * inputs, axis=-1, keepdims=True) + EPS)
    scaled = error * gain_ref[...]
    inner_mean = jnp.mean(scaled * inputs, axis=-1, keepdims=True)
    back = inverse * scaled - inputs * (inverse * inverse * inverse) * inner_mean
    flat[...] = d_res_ref[...].reshape(rows, width) + back
    sums[0:1, :] = jnp.sum(error * inputs * inverse, axis=0, keepdims=True)
    sums[1:2, :] = ffn_gain_ref[...]

    def near_copy(k, owner):
        return remote(
            sums, sums_land.at[slot_of(owner)], near_send.at[k], near_recv.at[slot_of(owner)],
            group_peer(k),
        )

    def far_copy(k, owner):
        return remote(
            gains_ref, sums_land.at[8 + owner], far_send.at[k], far_recv.at[owner], outer_peer(k)
        )

    for k in range(1, 8):
        near_copy(k, here).start()
    total = sums[...]
    for k in range(1, 8):
        near_copy(k, group_peer(k)).wait_recv()
        total = total + sums_land[slot_of(group_peer(k))]
    gains_ref[...] = total

    @pl.loop(1, steps)
    def _(k):
        far_copy(k, outer).start()

    @pl.loop(0, steps)
    def _(z):
        source = lane_device(z, number // steps)

        @pl.when(number_of(source) != number)
        def _():
            for src, land, ssem, rsem in slices:
                remote(
                    src.at[0], land.at[z], ssem.at[0], rsem.at[z], here
                ).wait_recv()

    own_down_ref[...] = jnp.zeros_like(own_down_ref)
    own_o_ref[...] = jnp.zeros_like(own_o_ref)

    @pl.loop(0, steps)
    def _(z):
        own_down_ref[...] += down_land[z].astype(F32)
        own_o_ref[...] += wo_land[z].astype(F32)

    for copy in own_rows:
        copy.wait()

    @pl.loop(1, count)
    def _(k):
        source = member_device((number + k) % count)
        rows_copy(d_gate_any, gate_land, gate_send, gate_recv, here, source).wait_recv()
        rows_copy(d_up_any, up_land, up_send, up_recv, here, source).wait_recv()
        rows_copy(d_weights, qkv_land, qkv_send, qkv_recv, here, source).wait_recv()

    def added(land, which):
        total = land[which * steps].astype(F32)
        for z in range(1, steps):
            total = total + land[which * steps + z].astype(F32)
        return total

    reach = gate_land.shape[2]
    tiles = 2 * (reach // BLOCK) - 1
    step = reach - BLOCK
    for pair in range(4):
        base = pair * tiles * BLOCK
        for land, ref in ((gate_land, own_gate_ref), (up_land, own_up_ref)):
            first, second = added(land, 2 * pair), added(land, 2 * pair + 1)
            ref[:, base : base + step] = first[:, :step]
            ref[:, base + step : base + reach] = first[:, step:] + second[:, :BLOCK]
            ref[:, base + reach : base + tiles * BLOCK] = second[:, BLOCK:]
        first, second = added(qkv_land, 2 * pair), added(qkv_land, 2 * pair + 1)
        twice = 2 * HEAD
        own_q_ref[:, 2 * pair * twice : (2 * pair + 1) * twice] = first[:, :twice]
        own_q_ref[:, (2 * pair + 1) * twice : (2 * pair + 2) * twice] = second[:, :twice]
        first, second = first[:, twice:], second[:, twice:]
        lower = lax.broadcasted_iota(jnp.int32, first.shape, 1) < HEAD
        at = slice(pair * twice, (pair + 1) * twice)
        own_k_ref[:, at] = jnp.where(lower, first, pltpu.roll(second, HEAD, 1))
        own_v_ref[:, at] = jnp.where(lower, pltpu.roll(first, HEAD, 1), second)

    @pl.loop(1, steps)
    def _(k):
        far_copy(k, outer).wait_send()

    total = gains_ref[...]

    @pl.loop(1, steps)
    def _(k):
        source = (outer + k) % steps
        far_copy(k, source).wait_recv()
        gains_ref[...] += sums_land[8 + source]

    for k in range(1, 8):
        near_copy(k, here).wait_send()
        for n in range(2):
            swap_copy(k, n, here).wait_send()

    @pl.loop(0, steps)
    def _(chunk):
        @pl.when(lane * steps + chunk != number)
        def _():
            for refs in slices:
                slice_copy(*refs, chunk, outer).wait_send()

    @pl.loop(1, steps)
    def _(k):
        slot = (outer + k) % steps
        kv_copy(slot, 0, outer).wait_send()

        @pl.when(slot > outer)
        def _():
            kv_copy(slot, 1, outer).wait_send()

    @pl.loop(1, count)
    def _(k):
        target = member_device((number + k) % count)
        rows_copy(d_gate_any, gate_land, gate_send, gate_recv, target, here).wait_send()
        rows_copy(d_up_any, up_land, up_send, up_recv, target, here).wait_send()
        rows_copy(d_weights, qkv_land, qkv_send, qkv_recv, target, here).wait_send()


def back(args, steps):
    q_t, q_cols = args[0], args[1]
    kv, x = args[5], args[11]
    normed, weights = args[15], args[16]
    d_gate, d_down, d_wo = args[18], args[20], args[21]
    part, width = x.shape[1:]
    half = normed.shape[1]
    tokens = 2 * half
    count = steps * 8
    per = width // count
    reach = d_gate.shape[2]
    ff = (2 * (reach // BLOCK) - 1) * BLOCK * 4
    own = lambda *shape: jax.ShapeDtypeStruct(shape, F32)
    kv_cols = 8 * HEAD
    return pl.pallas_call(
        functools.partial(back_kernel, steps),
        out_shape=(
            own(2, part, width),
            own(8, width),
            own(per, 16 * HEAD),
            own(per, kv_cols),
            own(per, kv_cols),
            own(*d_wo.shape[1:]),
            own(per, ff),
            own(per, ff),
            own(*d_down.shape[1:]),
        ),
        in_specs=[VMEM] * 15 + [ANY] * 7,
        out_specs=[VMEM] * 9,
        scratch_shapes=[
            pltpu.VMEM(normed.shape, BF16),
            pltpu.VMEM(weights.shape, BF16),
            pltpu.VMEM(weights.shape, BF16),
            pltpu.VMEM(q_t.shape, BF16),
            pltpu.VMEM(q_cols.shape, BF16),
            pltpu.VMEM((1, 2 * tokens), F32),
            pltpu.VMEM(q_t.shape, F32),
            pltpu.VMEM(kv.shape, F32),
            pltpu.VMEM(kv.shape, BF16),
            pltpu.VMEM(kv.shape, BF16),
            pltpu.VMEM((2, half, 4 * HEAD), BF16),
            pltpu.VMEM((2, part, 32 * HEAD), BF16),
            pltpu.VMEM((count, per, 4 * HEAD), BF16),
            pltpu.VMEM((count, per, reach), BF16),
            pltpu.VMEM((count, per, reach), BF16),
            pltpu.VMEM((count, per, 4 * HEAD), BF16),
            pltpu.VMEM(d_down.shape, BF16),
            pltpu.VMEM(d_wo.shape, BF16),
            pltpu.VMEM((8, width), F32),
            pltpu.VMEM((8 + steps, 8, width), F32),
            DMA((5,)),
            DMA((count,)),
            DMA((count,)),
            DMA((count,)),
            DMA((count,)),
            DMA((count,)),
            DMA((count,)),
            DMA((steps,)),
            DMA((steps,)),
            DMA((steps,)),
            DMA((steps,)),
            DMA((2, steps)),
            DMA((2, steps)),
            DMA((2, 8)),
            DMA((2, 8)),
            DMA((8,)),
            DMA((8,)),
            DMA((steps,)),
            DMA((steps,)),
        ],
        compiler_params=params(3),
        name="back",
    )(*args)


def swap(array, axis_size):
    return lax.ppermute(array, "fsdp", [(k, (k + 1) % axis_size) for k in range(axis_size)])


def local(
    block_input, dy, attn_gain, q_gain, k_gain, ffn_gain, wq, wk, wv, wo, w_gate, w_up, w_down
):
    steps = lax.axis_size("outer")
    inner_size = lax.axis_size("inner")
    fsdp_size = lax.axis_size("fsdp")
    outer = lax.axis_index("outer")
    inner = lax.axis_index("inner")
    fsdp = lax.axis_index("fsdp")
    group = inner_size * fsdp_size
    part, width = block_input.shape[2:]
    half = inner_size * fsdp_size * part
    ff = w_gate.shape[1]
    tiles = 2 * ff // group // BLOCK
    reach = (tiles + 1) // 2 * BLOCK
    far_lane = (1 - fsdp) * inner_size + inner
    far_start = (far_lane // 2 * tiles + inner % 2 * (tiles // 2)) * BLOCK

    def window(arr, start, size):
        return lax.dynamic_slice_in_dim(arr, start, size, 1)

    depth = wq.shape[0]
    weights = jnp.concatenate(
        [
            wq.reshape(depth, group, 2 * HEAD),
            wk.reshape(depth, group, HEAD),
            wv.reshape(depth, group, HEAD),
        ],
        axis=2,
    ).reshape(depth, group * 4 * HEAD)
    qkv_far = swap(window(weights, far_lane * 4 * HEAD, 4 * HEAD), fsdp_size)
    wo_far = swap(wo, fsdp_size)
    gate_far = swap(window(w_gate, far_start, reach), fsdp_size)
    up_far = swap(window(w_up, far_start, reach), fsdp_size)

    x = block_input.reshape(2, part, width)
    cot = dy.reshape(2, part, width)
    within = jnp.arange(half, dtype=jnp.int32)
    positions = jnp.concatenate(
        [outer * half + within, (2 * steps - 1 - outer) * half + within], axis=0
    )
    index = jnp.arange(2 * HEAD, dtype=jnp.int32) % (HEAD // 2)
    frequency = ROPE_BASE ** (-2.0 * index.astype(F32) / HEAD)
    angles = positions.astype(F32)[:, None] * frequency[None, :]
    sign = jnp.where(jnp.arange(2 * HEAD) % HEAD < HEAD // 2, -1.0, 1.0).astype(F32)
    cos = jnp.cos(angles)
    sin = jnp.sin(angles) * sign
    q_gain2 = jnp.tile(q_gain, 2)[None]
    k_gain2 = jnp.tile(k_gain, 2)[None]
    normed, proj, q_cols, q_t, kv_own = front(
        x, attn_gain[None], weights, qkv_far, cos, sin, q_gain2, k_gain2
    )
    kv, cot_group, attn_t, log_total, attn, residual, ffn_rows = middle(
        x, cot, q_t, kv_own, wo, wo_far, ffn_gain[None], steps
    )
    later, ffn_rows = lax.optimization_barrier((weights, ffn_rows))
    weights_far = swap(later, fsdp_size)
    result, d_residual, attn_grad, d_ffn_gain, d_gate, d_up, d_down, d_wo = ffn(
        ffn_rows,
        residual,
        cot,
        attn,
        ffn_gain[None],
        cot_group.reshape(2 * group, part, width),
        (w_gate, gate_far, w_up, up_far, w_down, wo, wo_far),
        steps,
        steps * group,
    )
    grad_in, gains, own_q, own_k, own_v, own_o, own_gate, own_up, own_down = back(
        (
            q_t,
            q_cols,
            attn_grad,
            attn_t,
            log_total,
            kv,
            proj,
            cos,
            sin,
            q_gain2,
            k_gain2,
            x,
            d_residual,
            attn_gain[None],
            d_ffn_gain,
            normed,
            weights,
            weights_far,
            d_gate,
            d_up,
            d_down,
            d_wo,
        ),
        steps,
    )
    return (
        result.reshape(block_input.shape),
        grad_in.reshape(block_input.shape),
        gains[0],
        gains[2, :HEAD] + gains[2, HEAD : 2 * HEAD],
        gains[2, 2 * HEAD : 3 * HEAD],
        gains[1],
        own_q,
        own_k,
        own_v,
        own_o,
        own_gate,
        own_up,
        own_down,
    )


def solution(mesh):
    ctx, fsdp = mesh.shape["ctx"], mesh.shape["fsdp"]
    inner = 8 // fsdp
    grid = Mesh(mesh.devices.reshape(ctx // inner, inner, fsdp), EVERY)
    tokens = P(None, ("outer", "inner"), "fsdp", None)
    shard = P("fsdp", None)
    owned = P(EVERY, None)
    return jax.shard_map(
        local,
        mesh=grid,
        in_specs=(tokens, tokens) + (P(),) * 4 + (shard,) * 7,
        out_specs=(tokens, tokens) + (P(),) * 4 + (owned,) * 7,
        check_vma=False,
    )
```

time: 637 us -> 478 us (0.75)
  Pallas kernels: 97.8 us -> 349 us
  waiting for transfers between devices: 257 us -> 85.9 us
  blocking collectives: 74.8 us -> 0 us
  matrix products: 54.6 us -> 0 us
  local copies, waits for them, and re-layouts: 70.2 us -> 25.6 us
  starting transfers between devices: 33.5 us -> 5.78 us
  other arithmetic: 23.5 us -> 5.08 us
  between operations: 15.4 us -> 0.88 us
    pallas_call x1 -> x2, Pallas kernels: 16.9 us -> 285 us  [the longest x1 197 us: back(): pl.pallas_call(functools.partial(back_kernel, steps), out_shape=(own(2, p...]
    reduce_scatter x8 -> x0, waiting for transfers between devices: 216 us -> none  [the longest x2 83.6 us: scatter_members(): lax.psum_scatter(arr.reshape(group, rows, width), GROUP, scatter_dimensio...]
    psum x1 -> x0, blocking collectives: 74.8 us -> none  [local(): lax.psum(jnp.concatenate([d_attn_gain, d_ffn_gain, jnp.pad(d_q_gain, (0,...]
    ppermute x7 -> x5, waiting for transfers between devices: 18.2 us -> 85.9 us  [swap(): lax.ppermute(array, 'fsdp', [(k, (k + 1) % axis_size) for k in range(axis...]
    dot_general x15 -> x0, matrix products: 54.6 us -> none  [dot(): return lax.dot_general(a, b, (dims, ((), ())), preferred_element_type=F32)]
    all_to_all x5 -> x0, starting transfers between devices: 23 us -> none  [the longest x3 13.6 us: rows_out(): lax.all_to_all(part_sum, GROUP, split_axis=0, concat_axis=0, tiled=True)]
    pallas_call x1, Pallas kernels: 37 us -> 19.9 us  [front(): pl.pallas_call(front_kernel, out_shape=(jax.ShapeDtypeStruct((2, half, wi...]
    all_to_all x5 -> x0, waiting for transfers between devices: 14.6 us -> none  [the longest x3 10.5 us: rows_out(): lax.all_to_all(part_sum, GROUP, split_axis=0, concat_axis=0, tiled=True)]
  transfers between devices with their start and end apart: 23 -> 5, of which waited for: 13 -> 3; matrix products, arithmetic and copies ran while one was open for 19% -> 3% of each run, Pallas kernels for 9% -> 23%
where the time goes in v3:
time: 478 us; the launch traced here: 472 us
  Pallas kernels  349 us (73%)
  waiting for transfers between devices  85.9 us (18%)
  local copies, waits for them, and re-layouts  25.6 us (5%)
  starting transfers between devices  5.78 us (1%)
  other arithmetic  5.08 us (1%)
    pallas_call x1, Pallas kernels, back(): pl.pallas_call(functools.partial(back_kernel, steps), out_shape=(own(2, p...  197 us
    pallas_call x1, Pallas kernels, ffn(): pl.pallas_call(functools.partial(ffn_kernel, steps), out_shape=(jax.Shape...  88.1 us
    ppermute x5, waiting for transfers between devices, swap(): lax.ppermute(array, 'fsdp', [(k, (k + 1) % axis_size) for k in range(axis...  85.9 us
    pallas_call x1, Pallas kernels, middle(): pl.pallas_call(functools.partial(middle_kernel, steps), out_shape=(jax.Sh...  44.5 us
    pallas_call x1, Pallas kernels, front(): pl.pallas_call(front_kernel, out_shape=(jax.ShapeDtypeStruct((2, half, wi...  19.9 us
    unnamed x41, local copies, waits for them, and re-layouts  17.3 us
  transfers between devices with their start and end apart: 5, of which 3 were waited for; matrix products, arithmetic and copies ran while one was open for 3% of the time, Pallas kernels for 23%

profile of v3, /device:TPU:6, one launch (start us, length us, event | category | flops | bytes accessed | tf_op | source)
XLA Modules:
  0.0 472.3 jit_solution(3351436577538776656)
XLA Ops:
  0.6 0.0 copy-start.8
  0.7 0.6 collective-permute-start.1
  1.3 1.3 copy.28
  2.5 0.8 copy.30
  3.3 1.0 copy.29
  4.3 1.8 copy.31
  6.1 1.5 copy.34
  7.6 0.6 pad_maximum_fusion
  8.3 0.0 copy-start.12
  8.3 0.0 copy-start.13
  8.3 0.7 copy.35
  9.0 0.8 constant_dynamic-slice_fusion.2
  9.8 1.5 collective-permute-start
  11.4 0.0 copy-done.12
  11.4 0.6 broadcast_in_dim_tile.6.qg_ref
  12.0 0.6 broadcast_in_dim_tile.7.kg_ref
  12.6 3.0 fusion
  15.6 15.8 %collective-permute-done.far_any = bf16[512,256]{1,0:T(8,128)(2,1)S(1)} collective-permute-done((bf16[512,256]{1,0:T(8,128)(2,1)}, bf16[512,256]{1,0:T(8,128)(2,1)S(1)}, u32[]{:S(2)}, u32[]{:S(2)}) %collective-permute-start) | collective-permute-done | bytes 262176 | tf_op jit(solution)/shard_map/ppermute | solution.py:1412
  31.4 0.0 copy-done
  31.5 0.7 copy-done.9
  32.1 19.9 %front.1 = (bf16[2,512,1024]{2,1,0:T(8,128)(2,1)}, f32[1024,256]{1,0:T(8,128)}, bf16[2048,128]{1,0:T(8,128)(2,1)}, bf16[128,2048]{1,0:T(8,128)(2,1)}, bf16[1024,128]{1,0:T(8,128)(2,1)}) custom-call(bf16[2,64,1024]{2,1,0:T(8,128)(2,1)} %bitcast.29, f32[1,1024]{1,0:T(1,128)} %bitcast.40, bf16[512,2048]{1,0:T(8,128)(2,1)} %bitcast.24, ...), custom_call_target="tpu_custom_call" | custom-call | tf_op jit(solution)/shard_map/front/pallas_call | solution.py:445
  52.1 0.0 collective-permute-done.1.wo_other.wo_far
  52.1 1.0 copy-done.2
  53.1 44.5 %middle.1 = (bf16[4,1024,128]{2,1,0:T(8,128)(2,1)}, bf16[8,2,64,1024]{3,2,1,0:T(8,128)(2,1)}, f32[64,2048]{1,0:T(8,128)}, f32[1,2048]{1,0:T(1,128)}, bf16[2,512,...) custom-call(bf16[2,64,1024]{2,1,0:T(8,128)(2,1)} %bitcast.30, ...), custom_call_target="tpu_custom_call" | custom-call | tf_op jit(solution)/shard_map/middle/pallas_call | solution.py:475
  97.5 0.0 copy-done.1
  97.6 1.5 collective-permute-start.4
  99.1 1.1 constant_dynamic-slice_fusion
  100.2 0.6 collective-permute-start.3
  100.9 1.1 constant_dynamic-slice_fusion.1
  102.0 1.5 collective-permute-start.2
  103.5 56.6 %collective-permute-done.3.up_far = bf16[512,640]{1,0:T(8,128)(2,1)S(1)} collective-permute-done((bf16[512,640]{1,0:T(8,128)(2,1)S(1)}, bf16[512,640]{1,0:T(8,128)(2,1)S(1)}, u32[]{:S(2)}, u32[]{:S(2)}) %collective-permute-start.3) | collective-permute-done | bytes 655392 | tf_op jit(solution)/shard_map/ppermute | solution.py:1412
  160.2 13.4 %collective-permute-done.2.gate_far = bf16[512,640]{1,0:T(8,128)(2,1)S(1)} collective-permute-done((bf16[512,640]{1,0:T(8,128)(2,1)S(1)}, bf16[512,640]{1,0:T(8,128)(2,1)S(1)}, u32[]{:S(2)}, u32[]{:S(2)}) %collective-permute-start.2) | collective-permute-done | bytes 655392 | tf_op jit(solution)/shard_map/ppermute | solution.py:1412
  173.6 0.0 copy-done.3
  173.6 0.9 copy-done.4
  174.5 88.1 %ffn.1 = (bf16[2,64,1024]{2,1,0:T(8,128)(2,1)}, f32[2,64,1024]{2,1,0:T(8,128)}, bf16[2,512,128]{2,1,0:T(8,128)(2,1)}, f32[1,1024]{1,0:T(1,128)}, bf16[32,32,640]...) custom-call(bf16[2,64,1024]{2,1,0:T(8,128)(2,1)} %get-tuple-element., ...), custom_call_target="tpu_custom_call" | custom-call | tf_op jit(solution)/shard_map/ffn/pallas_call | solution.py:802
  262.5 0.0 collective-permute-done.4.far_any
  262.6 196.6 %back.1 = (f32[2,64,1024]{2,1,0:T(8,128)}, f32[8,1024]{1,0:T(8,128)}, f32[32,1024]{1,0:T(8,128)}, f32[32,512]{1,0:T(8,128)}, f32[32,512]{1,0:T(8,128)}, /*index=...) custom-call(bf16[128,2048]{1,0:T(8,128)(2,1)} %get-tuple-element.44.qt_ref, ...), custom_call_target="tpu_custom_call" | custom-call | tf_op jit(solution)/shard_map/back/pallas_call | solution.py:1350
  459.2 1.4 slice_bitcast_fusion
  460.6 1.4 fusion.4
  462.0 0.7 copy.45
  462.7 1.9 copy.46
  464.7 1.6 copy.47
  466.2 1.5 copy.48
  467.7 1.5 copy.49
  469.2 0.7 copy.50
  469.9 0.8 copy.51
  470.7 0.8 copy.52
  471.5 0.8 copy.53
  (23 shorter events, 0.1 us)
Async XLA Ops:
  0.6 2.7 copy-start.8
  0.7 51.4 %collective-permute-start.1 = (bf16[512,1024]{1,0:T(8,128)(2,1)}, bf16[512,1024]{1,0:T(8,128)(2,1)S(1)}, u32[]{:S(2)}, u32[]{:S(2)}) collective-permute-start(bf16[512,1024]{1,0:T(8,128)(2,1)} %wo_any.1), channel_id=1, source_target_pairs={{0,1},{1,0},{2,3},{3,2},{4,5},{5,4},{6,7},{7,6},{8,9},{9,8},{10,11... | collective-permute-start | bytes 3145736 | tf_op jit(solution)/shard_map/ppermute | solution.py:1412
  8.3 3.1 copy-start.12
  8.3 3.7 copy-start.13
  9.0 22.4 %copy-start = (bf16[64,8,8,256]{3,1,2,0:T(8,128)(2,1)}, bf16[64,8,8,256]{3,1,2,0:T(8,128)(2,1)S(1)}, u32[]{:S(2)}) copy-start(bf16[64,8,8,256]{3,1,2,0:T(8,128)(2,1)S(1)} %copy.35) | copy-start | bytes 6291460
  9.8 21.6 %collective-permute-start = (bf16[512,256]{1,0:T(8,128)(2,1)}, bf16[512,256]{1,0:T(8,128)(2,1)S(1)}, u32[]{:S(2)}, u32[]{:S(2)}) collective-permute-start(bf16[512,256]{1,0:T(8,128)(2,1)} %constant_dynamic-slice_fusion.2), channel_id=1, source_target_pairs={{0,1},{1,0},{2,3},{3,2},{4,5},{5,4},{6,7},{7,6},{8,9},{9,8},{10,11... | collective-permute-start | bytes 786440 | tf_op jit(solution)/shard_map/ppermute | solution.py:1412
  31.4 0.7 copy-start.9
  52.0 45.5 %copy-start.1 = (bf16[64,8,8,256]{3,1,2,0:T(8,128)(2,1)S(1)}, bf16[64,8,8,256]{3,1,2,0:T(8,128)(2,1)}, u32[]{:S(2)}) copy-start(bf16[64,8,8,256]{3,1,2,0:T(8,128)(2,1)} %copy-done) | copy-start | bytes 6291460
  52.1 1.0 copy-start.2
  97.6 165.0 %collective-permute-start.4 = (bf16[512,2048]{1,0:T(8,128)(2,1)S(1)}, bf16[512,2048]{1,0:T(8,128)(2,1)}, u32[]{:S(2)}, u32[]{:S(2)}) collective-permute-start(bf16[512,2048]{1,0:T(8,128)(2,1)S(1)} %bitcast.26), channel_id=1, source_target_pairs={{0,1},{1,0},{2,3},{3,2},{4,5},{5,4},{6,7},{7,6},{8,9},{9,8},{10,11... | collective-permute-start | bytes 6291464 | tf_op jit(solution)/shard_map/ppermute | solution.py:1412
  100.2 59.9 %collective-permute-start.3 = (bf16[512,640]{1,0:T(8,128)(2,1)S(1)}, bf16[512,640]{1,0:T(8,128)(2,1)S(1)}, u32[]{:S(2)}, u32[]{:S(2)}) collective-permute-start(bf16[512,640]{1,0:T(8,128)(2,1)S(1)} %constant_dynamic-slice_fusion), channel_id=1, source_target_pairs={{0,1},{1,0},{2,3},{3,2},{4,5},{5,4},{6,7},{7,6},{8,9},{9,8},{10,11... | collective-permute-start | bytes 1966088 | tf_op jit(solution)/shard_map/ppermute | solution.py:1412
  102.0 71.6 %collective-permute-start.2 = (bf16[512,640]{1,0:T(8,128)(2,1)S(1)}, bf16[512,640]{1,0:T(8,128)(2,1)S(1)}, u32[]{:S(2)}, u32[]{:S(2)}) collective-permute-start(bf16[512,640]{1,0:T(8,128)(2,1)S(1)} %constant_dynamic-slice_fusion.1), channel_id=1, source_target_pairs={{0,1},{1,0},{2,3},{3,2},{4,5},{5,4},{6,7},{7,6},{8,9},{9,8},{10,11... | collective-permute-start | bytes 1966088 | tf_op jit(solution)/shard_map/ppermute | solution.py:1412
  160.2 13.4 %copy-start.3 = (bf16[512,640]{1,0:T(8,128)(2,1)}, bf16[512,640]{1,0:T(8,128)(2,1)S(1)}, u32[]{:S(2)}) copy-start(bf16[512,640]{1,0:T(8,128)(2,1)S(1)} %collective-permute-done.3.up_far) | copy-start | bytes 1966084
  173.6 0.9 copy-start.4
  262.5 199.5 %copy-start.10 = (bf16[2,64,1024]{2,1,0:T(8,128)(2,1)S(1)}, bf16[2,64,1024]{2,1,0:T(8,128)(2,1)}, u32[]{:S(2)}) copy-start(bf16[2,64,1024]{2,1,0:T(8,128)(2,1)} %get-tuple-element.51) | copy-start | bytes 786436
  459.2 10.0 %copy-start.11 = (f32[32,1024]{1,0:T(8,128)S(1)}, f32[32,1024]{1,0:T(8,128)}, u32[]{:S(2)}) copy-start(f32[32,1024]{1,0:T(8,128)} %get-tuple-element.133) | copy-start | bytes 393220
  459.2 10.7 %copy-start.7 = (f32[32,4608]{1,0:T(8,128)S(1)}, f32[32,4608]{1,0:T(8,128)}, u32[]{:S(2)}) copy-start(f32[32,4608]{1,0:T(8,128)} %get-tuple-element.134) | copy-start | bytes 1769476
  459.2 11.5 %copy-start.6 = (f32[32,4608]{1,0:T(8,128)S(1)}, f32[32,4608]{1,0:T(8,128)}, u32[]{:S(2)}) copy-start(f32[32,4608]{1,0:T(8,128)} %get-tuple-element.135) | copy-start | bytes 1769476
  462.7 8.8 %copy-start.5 = (f32[144,1024]{1,0:T(8,128)S(1)}, f32[144,1024]{1,0:T(8,128)}, u32[]{:S(2)}) copy-start(f32[144,1024]{1,0:T(8,128)} %get-tuple-element.136) | copy-start | bytes 1769476

commit v4 on v3

v4 whole, which is shorter than its diff:
```python
import functools
import math

import jax
import jax.numpy as jnp
from jax import lax
from jax.experimental import pallas as pl
from jax.experimental.pallas import tpu as pltpu
from jax.sharding import Mesh
from jax.sharding import PartitionSpec as P

EPS = 1e-05
ROPE_BASE = 1000000.0
F32 = jnp.float32
BF16 = jnp.bfloat16
HEAD = 64
BLOCK = 128
GROUP = ("inner", "fsdp")
EVERY = ("outer", "inner", "fsdp")


def dot(a, b, dims=((1,), (0,))):
    return lax.dot_general(a, b, (dims, ((), ())), preferred_element_type=F32)


SCORE = 1.0 / math.sqrt(HEAD)
SCORE2 = SCORE * math.log2(math.e)


def place():
    return tuple(lax.axis_index(name) for name in EVERY)


def remote(src, dst, send, recv, device):
    return pltpu.make_async_remote_copy(
        src_ref=src,
        dst_ref=dst,
        send_sem=send,
        recv_sem=recv,
        device_id=device,
        device_id_type=pl.DeviceIdType.MESH,
    )


def greet(devices):
    barrier = pltpu.get_barrier_semaphore()
    for device in devices:
        pl.semaphore_signal(
            barrier, inc=1, device_id=device, device_id_type=pl.DeviceIdType.MESH
        )
    return lambda: pl.semaphore_wait(barrier, len(devices))


def chip_peer(n, other_core=0):
    outer, inner, fsdp = place()
    row = (inner // 2 + n // 2) % 2
    return (outer, row * 2 + (inner + other_core) % 2, (fsdp + n) % 2)


def sibling():
    return chip_peer(0, 1)


def group_peer(k):
    outer, inner, fsdp = place()
    member = (inner * 2 + fsdp + k) % 8
    return (outer, member // 2, member % 2)


def member_of(device):
    return device[1] * 2 + device[2]


def slot_of(device):
    return ((device[1] // 2) * 2 + device[2]) * 2 + device[1] % 2


def member_device(number):
    return (number // 8, number % 8 // 2, number % 2)


def number_of(device):
    return device[0] * 8 + device[1] * 2 + device[2]


def lane_of(device):
    return device[2] * 4 + device[1]


def early_row(member, part):
    return pl.multiple_of(member * part, part)


def late_row(member, part):
    return pl.multiple_of((3 - member // 2) * 2 * part + (member % 2) * part, part)


def token_at(ref, device, part):
    member = member_of(device)
    return [
        ref.at[0, pl.ds(early_row(member, part), part)],
        ref.at[1, pl.ds(late_row(member, part), part)],
    ]


class Gather:
    def __init__(self, own, land, send, recv):
        self.own, self.land, self.send, self.recv = own, land, send, recv
        self.pieces = range(len(own))

    def copy(self, src, owner, piece, slot, device):
        return remote(
            src,
            self.land(owner)[piece],
            self.send.at[piece, slot],
            self.recv.at[piece, slot_of(owner)],
            device,
        )

    def start(self):
        for slot, device in ((1, chip_peer(1)), (2, chip_peer(2)), (0, sibling())):
            for piece in self.pieces:
                self.copy(self.own[piece], place(), piece, slot, device).start()

    def wait(self, owner):
        for piece in self.pieces:
            dst = self.land(owner)[piece]
            self.copy(dst, owner, piece, 0, sibling()).wait_recv()

    def pass_on(self, n):
        owner = chip_peer(n)
        self.wait(owner)

        def row_copies():
            for piece in self.pieces:
                self.copy(self.land(owner)[piece], owner, piece, 3, chip_peer(2)).start()

        pl.when(n == 1)(row_copies)
        for piece in self.pieces:
            self.copy(self.land(owner)[piece], owner, piece, 3 + n, sibling()).start()

    def finish(self):
        for n in range(4):
            self.wait(chip_peer(n, 1))

    def drain(self):
        for slot in range(7):
            for piece in self.pieces:
                self.copy(self.own[piece], place(), piece, slot, sibling()).wait_send()


class Exchange:
    def __init__(self, src, land, there, send, recv):
        self.src, self.land, self.there = src, land, there
        self.send, self.recv = send, recv
        self.rows = src.shape[0] // 4

    def at(self, ref, quarter):
        return ref.at[pl.ds(pl.multiple_of(quarter * self.rows, self.rows), self.rows)]

    def copy(self, src, quarter, slot, device):
        land = self.land if slot else self.there
        return remote(
            src, self.at(land, quarter), self.send.at[slot], self.recv.at[quarter], device
        )

    def start(self):
        inner = place()[1]
        self.copy(self.at(self.src, inner), inner, 0, chip_peer(1)).start()

    def shares(self):
        inner = place()[1]
        src = self.at(self.land, inner)
        peers = (chip_peer(2), chip_peer(2, 1), sibling())
        return [self.copy(src, inner, 1 + n, device) for n, device in enumerate(peers)]

    def wait(self, quarter):
        self.copy(self.at(self.land, quarter), quarter, 1, chip_peer(1)).wait_recv()

    def share(self):
        self.wait(place()[1])
        for copy in self.shares():
            copy.start()

    def finish(self):
        inner = place()[1]
        for k in range(1, 4):
            self.wait((inner + k) % 4)
        self.copy(self.at(self.src, inner), inner, 0, chip_peer(1)).wait_send()
        for copy in self.shares():
            copy.wait_send()


def rms_rows(values, gain):
    inverse = lax.rsqrt(jnp.mean(values * values, axis=-1, keepdims=True) + EPS)
    return values * inverse * gain


def head_inverse(values, low):
    squares = values * values
    first = jnp.sum(jnp.where(low, squares, 0.0), axis=-1, keepdims=True)
    second = jnp.sum(jnp.where(low, 0.0, squares), axis=-1, keepdims=True)
    return jnp.where(
        low, lax.rsqrt(first * (1.0 / HEAD) + EPS), lax.rsqrt(second * (1.0 / HEAD) + EPS)
    )


def halves(values, front):
    quarter = HEAD // 2
    return jnp.where(
        front,
        pltpu.roll(values, values.shape[-1] - quarter, 1),
        pltpu.roll(values, quarter, 1),
    )


def both(first, second, odd, flip):
    first, second = first.astype(F32), second.astype(F32)
    low = lax.broadcasted_iota(jnp.int32, first.shape, 1) < HEAD
    even = jnp.where(low, first, pltpu.roll(second, HEAD, 1))
    other = jnp.where(low, pltpu.roll(first, HEAD, 1), second)
    return jnp.where(odd > 0, other, even)


def front_kernel(
    steps,
    x_ref,
    gain_ref,
    wq_any,
    wk_any,
    wv_any,
    freq_ref,
    qg_ref,
    kg_ref,
    normed_out,
    proj_ref,
    q_ref,
    qt_ref,
    kv_ref,
    cos_ref,
    sin_ref,
    own,
    land,
    windows,
    mine_ref,
    give_ref,
    other_ref,
    send,
    recv,
    load_sem,
    far_sem,
    out_sem,
):
    outer, inner, fsdp = here = place()
    odd = inner % 2
    wide = 2 * HEAD
    loads = []
    for n, (lane, dst) in enumerate(
        ((lane_of(here), mine_ref), (lane_of(chip_peer(1)), give_ref))
    ):
        one = pl.ds(pl.multiple_of(lane * wide, wide), wide)
        two = pl.ds(pl.multiple_of(lane // 2 * wide, wide), wide)
        loads.append(
            [
                pltpu.make_async_copy(src, ref, load_sem.at[n, k])
                for k, (src, ref) in enumerate(
                    (
                        (wq_any.at[:, one], dst.at[:, pl.ds(0, wide)]),
                        (wk_any.at[:, two], windows.at[n, 0]),
                        (wv_any.at[:, two], windows.at[n, 1]),
                    )
                )
            ]
        )
    for copy in loads[1] + loads[0]:
        copy.start()
    part = x_ref.shape[1]
    half = land.shape[1]
    width = land.shape[2]
    sub = half // 2
    depth = width // 2
    ready = greet([sibling()] + [chip_peer(n) for n in (1, 2)])
    for late in range(2):
        rows = x_ref[late].astype(F32)
        own[late] = rms_rows(rows, gain_ref[...]).astype(BF16)
    for copy in loads[1]:
        copy.wait()
    give_ref[:, wide:] = both(windows[1, 0], windows[1, 1], odd, None).astype(BF16)
    ready()
    gather = Gather(
        [own.at[0], own.at[1]], lambda device: token_at(land, device, part), send, recv
    )
    gather.start()
    far = remote(give_ref, other_ref, far_sem.at[0], far_sem.at[1], chip_peer(1))
    far.start()
    me = member_of(here)
    land[0, pl.ds(early_row(me, part), part)] = own[0]
    land[1, pl.ds(late_row(me, part), part)] = own[1]
    for copy in loads[0]:
        copy.wait()
    mine_ref[:, wide:] = both(windows[0, 0], windows[0, 1], odd, None).astype(BF16)

    lane = lax.broadcasted_iota(jnp.int32, (sub, wide), 1)
    low = lane < HEAD
    front = lane % HEAD < HEAD // 2
    within = lax.broadcasted_iota(jnp.int32, (sub, wide), 0)

    @pl.loop(0, 4)
    def _(tile):
        block = jnp.where(tile < 2, outer, 2 * steps - 1 - outer)
        position = block * half + (tile % 2) * sub + within
        angle = position.astype(F32) * freq_ref[...]
        at = pl.ds(pl.multiple_of(tile * sub, sub), sub)
        sine = jnp.sin(angle)
        cos_ref[at, :] = jnp.cos(angle)
        sin_ref[at, :] = jnp.where(front, -sine, sine)

    for n in (1, 2, 3):
        gather.pass_on(n)
    gather.finish()
    out = pltpu.make_async_copy(land, normed_out, out_sem)
    out.start()
    far.wait_recv()
    mine_at = pl.ds(pl.multiple_of(fsdp * depth, depth), depth)
    other_at = pl.ds(pl.multiple_of((1 - fsdp) * depth, depth), depth)

    @pl.loop(0, 4)
    def _(tile):
        late = tile // 2
        inside = pl.ds(pl.multiple_of((tile % 2) * sub, sub), sub)
        rows = pl.ds(pl.multiple_of(tile * sub, sub), sub)
        proj = dot(land[late, inside, mine_at], mine_ref[...])
        proj = proj + dot(land[late, inside, other_at], other_ref[...])
        proj_ref[rows, :] = proj
        cos, sin = cos_ref[rows, :], sin_ref[rows, :]
        raw = proj[:, :wide]
        normed = raw * head_inverse(raw, low) * qg_ref[...]
        rotated = normed * cos + halves(normed, front) * sin
        second = pltpu.roll(rotated, HEAD, 1)
        for head, values in enumerate((rotated, second)):
            values = jnp.where(low, values, 0.0)
            cols = pl.ds(pl.multiple_of(tile * 2 * sub + head * sub, sub), sub)
            q_ref[cols, :] = values.astype(BF16)
            qt_ref[:, cols] = values.T.astype(BF16)
        raw = proj[:, wide:]
        normed = raw * head_inverse(raw, low) * kg_ref[...]
        rotated = normed * cos + halves(normed, front) * sin
        kv_ref[rows, :] = jnp.where(low, rotated, raw).astype(BF16)

    gather.drain()
    far.wait_send()
    out.wait()


def middle_kernel(
    steps,
    x_ref,
    dy_ref,
    qt_ref,
    kv_ref,
    gain_ref,
    wo_any,
    gate_any,
    up_any,
    kv_out,
    cot_out,
    wo_far,
    gate_far,
    up_far,
    attn_t_ref,
    log_ref,
    attn_ref,
    residual_ref,
    ffn_ref,
    kv_all,
    acc_ref,
    total_ref,
    token_rows,
    wo,
    dy_send,
    dy_recv,
    kv_send,
    kv_recv,
    swap_send,
    swap_recv,
    wo_send,
    wo_recv,
    window_send,
    window_recv,
    out_sem,
):
    outer, inner, fsdp = here = place()
    me = member_of(here)
    lane = lane_of(here)
    part = x_ref.shape[1]
    half = kv_ref.shape[0] // 2
    sub = half // 2
    wide = 2 * sub
    width = x_ref.shape[2]
    depth = width // 2
    reach = gate_far.shape[1]
    tiles = 2 * (reach // BLOCK) - 1
    their = lane_of(chip_peer(1))
    start = (their // 2 * tiles + their % 2 * (reach // BLOCK - 1)) * BLOCK
    window = pl.ds(pl.multiple_of(start, BLOCK), reach)
    rows = depth // 4

    def outer_peer(k):
        return ((outer + k) % steps, inner, fsdp)

    def window_copy(n):
        src, dst = ((gate_any, gate_far), (up_any, up_far))[n // 4]
        at = pl.ds(n % 4 * rows, rows)
        return remote(
            src.at[at, window], dst.at[at], window_send.at[n], window_recv.at[n], chip_peer(1)
        )

    ready = greet(
        [outer_peer(k) for k in range(1, steps)] + [group_peer(k) for k in range(1, 8)]
    )
    mine_at = pl.ds(pl.multiple_of(fsdp * depth, depth), depth)
    far_at = pl.ds(pl.multiple_of((1 - fsdp) * depth, depth), depth)
    wo_load = pltpu.make_async_copy(wo_any, wo.at[mine_at], out_sem.at[2])
    wo_load.start()
    own_dy = pltpu.make_async_copy(dy_ref, cot_out.at[slot_of(here)], out_sem.at[0])
    own_dy.start()
    kv_all[outer] = kv_ref[...]
    acc_ref[...] = jnp.zeros_like(acc_ref)
    total_ref[...] = jnp.zeros_like(total_ref)
    ready()

    def kv_copy(slot, late, source):
        at = pl.ds(late * half, half)
        return remote(
            kv_ref.at[at],
            kv_all.at[source, at],
            kv_send.at[late, slot],
            kv_recv.at[late, source],
            (slot, inner, fsdp),
        )

    @pl.loop(1, steps)
    def _(k):
        slot = (outer + steps - k) % steps
        kv_copy(slot, 0, outer).start()

        @pl.when(slot < outer)
        def _():
            kv_copy(slot, 1, outer).start()

    share = Exchange(wo_any, wo_far, wo_far, wo_send, wo_recv)
    share.start()
    cot = Gather(
        [dy_ref.at[n] for n in range(2)],
        lambda device: [cot_out.at[slot_of(device), n] for n in range(2)],
        dy_send,
        dy_recv,
    )
    cot.start()
    for n in range(4):
        window_copy(n).start()

    def block(slot, row, size, col, mask):
        kv = kv_all[slot, pl.ds(pl.multiple_of(row, sub), size), :]
        cols = pl.ds(pl.multiple_of(col, wide), wide)
        probs = jnp.exp2(dot(kv, qt_ref[:, cols]) * SCORE2)
        if mask is not None:
            probs = jnp.where(mask, probs, 0.0)
        total_ref[:, cols] += jnp.sum(probs.reshape(size // 8, 8, wide), axis=0)
        acc_ref[:, cols] += dot(kv, probs.astype(BF16), ((0,), (0,)))

    key = lax.broadcasted_iota(jnp.int32, (sub, wide), 0)
    query = lax.broadcasted_iota(jnp.int32, (sub, wide), 1) % sub
    diagonal = key <= query

    @pl.loop(0, 2)
    def _(late):
        block(outer, late * half, sub, late * 2 * wide, diagonal)
        block(outer, late * half, sub, late * 2 * wide + wide, None)
        block(outer, late * half + sub, sub, late * 2 * wide + wide, diagonal)

    @pl.loop(0, 2)
    def _(n):
        block(outer, 0, half, (2 + n) * wide, None)

    share.share()
    cot.pass_on(1)

    @pl.loop(1, steps)
    def _(k):
        slot = (outer + k) % steps
        late = jnp.where(slot < outer, 0, 1)
        kv_copy(slot, 0, slot).wait_recv()

        @pl.when(slot > outer)
        def _():
            kv_copy(slot, 1, slot).wait_recv()

        @pl.loop(0, 2)
        def _(n):
            block(slot, 0, half, (2 + n) * wide, None)
            block(slot, late * half, half, (late * 2 + n) * wide, None)

    @pl.loop(0, 4)
    def _(tile):
        heads = []
        for head in range(2):
            cols = pl.ds(pl.multiple_of(tile * wide + head * sub, sub), sub)
            total = jnp.sum(total_ref[:, cols], axis=0, keepdims=True)
            values = acc_ref[HEAD:, cols] / total
            attn_t_ref[:, cols] = values
            log_ref[:, cols] = jnp.log2(total)
            heads.append(values)
        inside = pl.ds(pl.multiple_of((tile % 2) * sub, sub), sub)
        attn_ref[tile // 2, inside, :] = jnp.concatenate(heads, axis=0).T.astype(BF16)

    def landing(device):
        cols = pl.ds(pl.multiple_of(lane_of(device) * 2 * HEAD, 2 * HEAD), 2 * HEAD)
        return [token_rows.at[n, :, cols] for n in range(2)]

    def swap_copy(k, n, owner):
        device = group_peer(k)
        return remote(
            token_at(attn_ref, device, part)[n],
            landing(owner)[n],
            swap_send.at[n, k],
            swap_recv.at[n, slot_of(owner)],
            device,
        )

    for k in range(1, 8):
        for n in range(2):
            swap_copy(k, n, here).start()
    for n in range(4, 8):
        window_copy(n).start()
    own_cols = pl.ds(pl.multiple_of(lane * 2 * HEAD, 2 * HEAD), 2 * HEAD)
    token_rows[0, :, own_cols] = attn_ref[0, pl.ds(early_row(me, part), part), :]
    token_rows[1, :, own_cols] = attn_ref[1, pl.ds(late_row(me, part), part), :]
    @pl.loop(1, steps)
    def _(k):
        slot = (outer + k) % steps

        @pl.when(slot < outer)
        def _():
            kv_all[slot, pl.ds(half, half), :] = jnp.zeros((half, 2 * HEAD), BF16)

    kv_store = pltpu.make_async_copy(kv_all, kv_out, out_sem.at[1])
    kv_store.start()
    share.finish()
    far_load = pltpu.make_async_copy(wo_far, wo.at[far_at], out_sem.at[3])
    far_load.start()
    cot.pass_on(2)
    cot.pass_on(3)
    wo_load.wait()
    far_load.wait()
    for k in range(1, 8):
        for n in range(2):
            swap_copy(k, n, group_peer(k)).wait_recv()
    for n in range(2):
        values = dot(token_rows[n], wo[...]) + x_ref[n].astype(F32)
        residual_ref[n] = values
        ffn_ref[n] = rms_rows(values, gain_ref[...]).astype(BF16)

    cot.finish()
    cot.drain()
    for k in range(1, 8):
        for n in range(2):
            swap_copy(k, n, here).wait_send()

    @pl.loop(1, steps)
    def _(k):
        slot = (outer + k) % steps
        kv_copy(slot, 0, outer).wait_send()

        @pl.when(slot < outer)
        def _():
            kv_copy(slot, 1, outer).wait_send()

    for n in range(8):
        window_copy(n).wait_recv()
        window_copy(n).wait_send()
    own_dy.wait()
    kv_store.wait()


SMEM = pl.BlockSpec(memory_space=pltpu.SMEM)
VMEM = pl.BlockSpec(memory_space=pltpu.VMEM)
ANY = pl.BlockSpec(memory_space=pl.ANY)
DMA = pltpu.SemaphoreType.DMA


def params(collective):
    return pltpu.CompilerParams(
        collective_id=collective, has_side_effects=True, vmem_limit_bytes=60 << 20
    )


def shape(dims, dtype=BF16):
    return jax.ShapeDtypeStruct(tuple(dims), dtype)


def front(x, gain, wq, wk, wv, freq, q_gain, k_gain, steps):
    part, width = x.shape[1:]
    half = 8 * part
    tokens = 2 * half
    depth = wq.shape[0]
    wide = 2 * HEAD
    window = pltpu.VMEM((depth, 2 * wide), BF16)
    return pl.pallas_call(
        functools.partial(front_kernel, steps),
        out_shape=(
            shape((2, half, width)),
            shape((tokens, 2 * wide), F32),
            shape((2 * tokens, wide)),
            shape((wide, 2 * tokens)),
            shape((tokens, wide)),
            shape((tokens, wide), F32),
            shape((tokens, wide), F32),
        ),
        in_specs=[VMEM] * 2 + [ANY] * 3 + [VMEM] * 3,
        out_specs=[ANY] + [VMEM] * 6,
        scratch_shapes=[
            pltpu.VMEM((2, part, width), BF16),
            pltpu.VMEM((2, half, width), BF16),
            pltpu.VMEM((2, 2, depth, wide), BF16),
            window,
            window,
            window,
            DMA((2, 8)),
            DMA((2, 8)),
            DMA((2, 3)),
            DMA((2,)),
            DMA,
        ],
        compiler_params=params(0),
        name="front",
    )(x, gain, wq, wk, wv, freq, q_gain, k_gain)


def middle(x, dy, qt, kv, gain, wo, gate, up, reach, steps):
    part, width = x.shape[1:]
    tokens = kv.shape[0]
    half = tokens // 2
    depth = wo.shape[0]
    return pl.pallas_call(
        functools.partial(middle_kernel, steps),
        out_shape=(
            shape((steps, tokens, 2 * HEAD)),
            shape((8, 2, part, width)),
            shape((depth, width)),
            shape((depth, reach)),
            shape((depth, reach)),
            shape((HEAD, 2 * tokens), F32),
            shape((1, 2 * tokens), F32),
            shape((2, half, 2 * HEAD)),
            shape((2, part, width), F32),
            shape((2, part, width)),
        ),
        in_specs=[VMEM] * 5 + [ANY] * 3,
        out_specs=[ANY] * 5 + [VMEM] * 5,
        scratch_shapes=[
            pltpu.VMEM((steps, tokens, 2 * HEAD), BF16),
            pltpu.VMEM((2 * HEAD, 2 * tokens), F32),
            pltpu.VMEM((8, 2 * tokens), F32),
            pltpu.VMEM((2, part, width), BF16),
            pltpu.VMEM((width, width), BF16),
            DMA((2, 8)),
            DMA((2, 8)),
            DMA((2, steps)),
            DMA((2, steps)),
            DMA((2, 8)),
            DMA((2, 8)),
            DMA((4,)),
            DMA((4,)),
            DMA((8,)),
            DMA((8,)),
            DMA((4,)),
        ],
        compiler_params=params(1),
        name="middle",
    )(x, dy, qt, kv, gain, wo, gate, up)


def ffn_kernel(
    steps,
    ffn_ref,
    residual_ref,
    dy_ref,
    gain_ref,
    cot_any,
    gate_any,
    gate_far,
    up_any,
    up_far,
    down_any,
    wo_any,
    wo_far,
    out_ref,
    d_res_ref,
    grad_ref,
    d_gain_ref,
    d_gate_ref,
    d_up_ref,
    down_ref,
    gate,
    up,
    down,
    wo,
    cot,
    land,
    d_hidden,
    hidden,
    d_gate,
    d_up,
    keep,
    near_send,
    near_land,
    sum_send,
    sum_land,
    d_down,
    down_send,
    down_land,
    swap_own,
    load_sem,
    ffn_send,
    ffn_recv,
    near_ssem,
    near_rsem,
    sum_ssem,
    sum_rsem,
    down_ssem,
    down_rsem,
    swap_send,
    swap_recv,
):
    outer, inner, fsdp = here = place()
    part, width = ffn_ref.shape[1:]
    depth = width // 2
    rows = 2 * part
    pair = 2 * rows
    reach = gate.shape[1]
    odd = inner % 2
    my_slot = slot_of(here)
    me = member_of(here)
    lane = lane_of(here)
    tiles = 2 * (reach // BLOCK) - 1
    step = (reach // BLOCK - 1) * BLOCK
    start = pl.multiple_of((lane // 2) * tiles * BLOCK + odd * step, BLOCK)
    down_start = pl.multiple_of((inner // 2) * tiles * BLOCK + odd * step, BLOCK)
    mine_at = pl.ds(pl.multiple_of(fsdp * depth, depth), depth)
    far_at = pl.ds(pl.multiple_of((1 - fsdp) * depth, depth), depth)
    pad = BLOCK // 2

    def outer_peer(k):
        return ((outer + k) % steps, inner, fsdp)

    ready = greet(
        [outer_peer(k) for k in range(1, steps)] + [group_peer(k) for k in range(1, 8)]
    )
    loads = [
        pltpu.make_async_copy(src, dst, load_sem.at[n])
        for n, (src, dst) in enumerate(
            (
                (down_any.at[pl.ds(down_start, reach)], down),
                (cot_any, cot),
                (gate_any.at[:, pl.ds(start, reach)], gate.at[mine_at]),
                (gate_far, gate.at[far_at]),
                (up_any.at[:, pl.ds(start, reach)], up.at[mine_at]),
                (up_far, up.at[far_at]),
                (wo_any, wo.at[mine_at]),
                (wo_far, wo.at[far_at]),
            )
        )
    ]
    for copy in loads:
        copy.start()
    ready()
    gather = Gather(
        [ffn_ref],
        lambda device: [land.at[pl.ds(pl.multiple_of(slot_of(device) * 2, 2), 2)]],
        ffn_send,
        ffn_recv,
    )
    gather.start()
    land[pl.ds(pl.multiple_of(my_slot * 2, 2), 2)] = ffn_ref[...]
    loads[0].wait()
    loads[1].wait()

    def chip_at(n):
        return slot_of(chip_peer(n)) // 2

    def chip_rows(n):
        return pl.ds(pl.multiple_of(chip_at(n) * pair, pair), pair)

    def four(n):
        return pl.ds(pl.multiple_of(chip_at(n) * 4, 4), 4)

    @pl.loop(0, 4)
    def _(n):
        values = cot[four(n)].reshape(pair, width)
        d_hidden[chip_rows(n), :] = dot(values, down[...], ((1,), (1,)))

    for copy in loads[2:6]:
        copy.wait()
    col = lax.broadcasted_iota(jnp.int32, (pair, reach), 1)
    valid = (col >= odd * pad) & (col < reach - pad + odd * pad)

    def near_copy(n):
        return remote(
            near_send.at[n], near_land.at[n], near_ssem.at[n], near_rsem.at[n], sibling()
        )

    def sum_copy(n):
        return remote(
            sum_send.at[n], sum_land.at[n], sum_ssem.at[n], sum_rsem.at[n], chip_peer(n)
        )

    def add_up(n):
        near_copy(n).wait_recv()
        total = keep[n] + near_land[n].astype(F32)

        @pl.when(n == 0)
        def _():
            keep[0] = total

        @pl.when(n > 0)
        def _():
            sum_send[n] = total.astype(BF16)
            sum_copy(n).start()

    @pl.loop(0, 4)
    def _(n):
        @pl.when(n > 0)
        def _():
            gather.pass_on(n)

        gather.wait(chip_peer(n, 1))
        at = chip_rows(n)
        values = land[four(n)].reshape(pair, width)
        gate_pre = dot(values, gate[...])
        up_pre = dot(values, up[...])
        sigmoid = jax.nn.sigmoid(gate_pre)
        silu = gate_pre * sigmoid
        hidden[at, :] = jnp.where(valid, silu * up_pre, 0.0).astype(BF16)
        back = jnp.where(valid, d_hidden[at, :], 0.0)
        d_gate[at, :] = (back * up_pre * sigmoid * (1.0 + gate_pre * (1.0 - sigmoid))).astype(BF16)
        d_up[at, :] = (back * silu).astype(BF16)
        for core in range(2):
            some = pl.ds(pl.multiple_of(chip_at(n) * pair + core * rows, rows), rows)
            total = dot(d_gate[some, :], gate[...], ((1,), (1,)))
            total = total + dot(d_up[some, :], up[...], ((1,), (1,)))

            @pl.when(odd == core)
            def _():
                keep[n] = total

            @pl.when(odd != core)
            def _():
                near_send[n] = total.astype(BF16)

        near_copy(n).start()

        @pl.when(n > 0)
        def _():
            add_up(n - 1)

    cot_rows = cot.reshape(8 * rows, width)
    land_rows = land.reshape(8 * rows, width)

    @pl.loop(0, reach // BLOCK)
    def _(tile):
        at = pl.ds(pl.multiple_of(tile * BLOCK, BLOCK), BLOCK)
        d_down[at, :] = dot(hidden[:, at], cot_rows[...], ((0,), (0,)))

    add_up(3)
    down_per = down_send.shape[1]
    for z in range(steps):
        at = z * down_per
        even_rows = d_down[at : at + down_per, :]
        odd_rows = d_down[at + pad : at + pad + down_per, :]
        down_send[z] = jnp.where(odd > 0, odd_rows, even_rows).astype(BF16)

    def down_copy(slot, source):
        return remote(
            down_send.at[slot],
            down_land.at[source],
            down_ssem.at[slot],
            down_rsem.at[source],
            (slot, inner, fsdp),
        )

    @pl.loop(1, steps)
    def _(k):
        down_copy((outer + k) % steps, outer).start()

    @pl.loop(0, 4)
    def _(n):
        total = dot(hidden[chip_rows(n), :], down[...])
        slots = pl.ds(pl.multiple_of(chip_at(n) * 2, 2), 2)
        out_ref[slots] = total.reshape(2, rows, width).astype(BF16)

    for copy in loads[6:]:
        copy.wait()
    error = keep[0]
    for n in (1, 2, 3):
        sum_copy(n).wait_recv()
        error = error + sum_land[n].astype(F32)
    residual = residual_ref[...].reshape(rows, width)
    inverse = lax.rsqrt(jnp.mean(residual * residual, axis=-1, keepdims=True) + EPS)
    scaled = error * gain_ref[...]
    inner_mean = jnp.mean(scaled * residual, axis=-1, keepdims=True)
    back = inverse * scaled - residual * (inverse * inverse * inverse) * inner_mean
    d_gain_ref[...] = jnp.sum(error * residual * inverse, axis=0, keepdims=True)
    d_residual = dy_ref[...].reshape(rows, width).astype(F32) + back
    d_res_ref[...] = d_residual.reshape(2, part, width)
    attn_grad = dot(d_residual.astype(BF16), wo[...], ((1,), (1,)))
    swap_own[...] = attn_grad.astype(BF16).reshape(2, part, width)

    def head_cols(device):
        return pl.ds(pl.multiple_of(lane_of(device) * 2 * HEAD, 2 * HEAD), 2 * HEAD)

    def swap_copy(k, n, owner):
        device = group_peer(k)
        return remote(
            swap_own.at[n, :, head_cols(device)],
            token_at(grad_ref, owner, part)[n],
            swap_send.at[n, k],
            swap_recv.at[n, slot_of(owner)],
            device,
        )

    for k in range(1, 8):
        for n in range(2):
            swap_copy(k, n, here).start()
    grad_ref[0, pl.ds(early_row(me, part), part)] = swap_own[0, :, head_cols(here)]
    grad_ref[1, pl.ds(late_row(me, part), part)] = swap_own[1, :, head_cols(here)]

    per = d_gate_ref.shape[1]
    many = BLOCK // per

    @pl.loop(0, width // BLOCK)
    def _(tile):
        at = pl.ds(pl.multiple_of(tile * BLOCK, BLOCK), BLOCK)
        for right, ref in ((d_gate, d_gate_ref), (d_up, d_up_ref)):
            value = dot(land_rows[:, at], right[...], ((0,), (0,)))
            ref[pl.ds(tile * many, many)] = value.reshape(many, per, reach).astype(BF16)

    down_total = down_send[outer].astype(F32)
    for k in range(1, steps):
        source = (outer + k) % steps
        down_copy(source, source).wait_recv()
        down_total = down_total + down_land[source].astype(F32)
    down_ref[...] = down_total.astype(BF16)

    for k in range(1, 8):
        for n in range(2):
            swap_copy(k, n, group_peer(k)).wait_recv()
            swap_copy(k, n, here).wait_send()
    for n in range(4):
        near_copy(n).wait_send()
        if n:
            sum_copy(n).wait_send()
    for k in range(1, steps):
        down_copy((outer + k) % steps, outer).wait_send()
    gather.drain()


def ffn(ffn_rows, residual, dy, gain, cot, weights, steps):
    part, width = ffn_rows.shape[1:]
    reach = weights[1].shape[1]
    own_ff = reach - BLOCK // 2
    rows = 2 * part
    half = 8 * part
    tokens = 2 * half
    devices = 8 * steps
    slices = pltpu.VMEM((steps, own_ff // steps, width), BF16)
    some = pltpu.VMEM((4, rows, width), BF16)
    return pl.pallas_call(
        functools.partial(ffn_kernel, steps),
        out_shape=(
            shape((8, rows, width)),
            shape((2, part, width), F32),
            shape((2, half, 2 * HEAD)),
            shape((1, width), F32),
            shape((devices, width // devices, reach)),
            shape((devices, width // devices, reach)),
            shape((own_ff // steps, width)),
        ),
        in_specs=[VMEM] * 4 + [ANY] * 8,
        out_specs=[VMEM] * 7,
        scratch_shapes=[
            pltpu.VMEM((width, reach), BF16),
            pltpu.VMEM((width, reach), BF16),
            pltpu.VMEM((reach, width), BF16),
            pltpu.VMEM((width, width), BF16),
            pltpu.VMEM((16, part, width), BF16),
            pltpu.VMEM((16, part, width), BF16),
            pltpu.VMEM((tokens, reach), F32),
            pltpu.VMEM((tokens, reach), BF16),
            pltpu.VMEM((tokens, reach), BF16),
            pltpu.VMEM((tokens, reach), BF16),
            pltpu.VMEM((4, rows, width), F32),
            some,
            some,
            some,
            some,
            pltpu.VMEM((reach, width), F32),
            slices,
            slices,
            pltpu.VMEM((2, part, width), BF16),
            DMA((8,)),
            DMA((1, 8)),
            DMA((1, 8)),
            DMA((4,)),
            DMA((4,)),
            DMA((4,)),
            DMA((4,)),
            DMA((steps,)),
            DMA((steps,)),
            DMA((2, 8)),
            DMA((2, 8)),
        ],
        compiler_params=params(2),
        name="ffn",
    )(ffn_rows, residual, dy, gain, cot, *weights)


def back_kernel(
    steps,
    qt_ref,
    q_ref,
    grad_ref,
    attn_t_ref,
    log_ref,
    kv_ref,
    proj_ref,
    cos_ref,
    sin_ref,
    qg_ref,
    kg_ref,
    x_ref,
    d_res_ref,
    residual_ref,
    attn_ref,
    gain_ref,
    ffn_gain_ref,
    normed_any,
    wq_any,
    wk_any,
    wv_any,
    d_gate_any,
    d_up_any,
    d_down_any,
    out_any,
    block_ref,
    dx_ref,
    gains_ref,
    own_q_ref,
    own_k_ref,
    own_v_ref,
    own_o_ref,
    own_gate_ref,
    own_up_ref,
    own_down_ref,
    normed,
    wq,
    wk,
    wv,
    gt_ref,
    g_ref,
    delta_ref,
    acc_ref,
    dkv_ref,
    dkv_send,
    dkv_land,
    d_qkv,
    tokens_land,
    dq_rows,
    dk_rows,
    dv_rows,
    d_weights,
    d_wo,
    res_own,
    res_land,
    out_land,
    gate_land,
    up_land,
    qkv_land,
    down_land,
    wo_land,
    sums,
    sums_land,
    load_sem,
    gate_send,
    gate_recv,
    up_send,
    up_recv,
    qkv_send,
    qkv_recv,
    down_sem,
    wo_send,
    wo_recv,
    out_send,
    out_recv,
    res_send,
    res_recv,
    share_send,
    share_recv,
    kv_send,
    kv_recv,
    swap_send,
    swap_recv,
    near_send,
    near_recv,
    far_send,
    far_recv,
):
    outer, inner, fsdp = here = place()
    lane = lane_of(here)
    number = number_of(here)
    me = member_of(here)
    my_slot = slot_of(here)
    count = steps * 8
    part, width = x_ref.shape[1:]
    rows = 2 * part
    half = normed.shape[1]
    sub = half // 2
    wide = 2 * sub
    depth = width // 2
    twice = 2 * HEAD

    barrier = pltpu.get_barrier_semaphore()

    @pl.loop(1, count)
    def _(k):
        pl.semaphore_signal(
            barrier,
            inc=1,
            device_id=member_device((number + k) % count),
            device_id_type=pl.DeviceIdType.MESH,
        )

    mine_at = pl.ds(pl.multiple_of(fsdp * depth, depth), depth)
    far_at = pl.ds(pl.multiple_of((1 - fsdp) * depth, depth), depth)
    loads = [
        pltpu.make_async_copy(src, dst, load_sem.at[n])
        for n, (src, dst) in enumerate(
            (
                (normed_any, normed),
                (wq_any, wq.at[mine_at]),
                (wk_any, wk.at[mine_at]),
                (wv_any, wv.at[mine_at]),
            )
        )
    ]
    for copy in loads:
        copy.start()
    res_own[...] = d_res_ref[...].astype(BF16)
    acc_ref[...] = jnp.zeros_like(acc_ref)
    dkv_ref[...] = jnp.zeros_like(dkv_ref)
    low = lax.broadcasted_iota(jnp.int32, (sub, twice), 1) < HEAD
    front = lax.broadcasted_iota(jnp.int32, (sub, twice), 1) % HEAD < HEAD // 2

    @pl.loop(0, 4)
    def _(tile):
        inside = pl.ds(pl.multiple_of((tile % 2) * sub, sub), sub)
        values = grad_ref[tile // 2, inside, :].astype(F32)
        flipped = pltpu.roll(values, HEAD, 1)
        for head, shifted in enumerate((flipped, values)):
            cols = pl.ds(pl.multiple_of(tile * wide + head * sub, sub), sub)
            shifted = jnp.where(low, 0.0, shifted)
            turned = shifted.T
            g_ref[cols, :] = shifted.astype(BF16)
            gt_ref[:, cols] = turned.astype(BF16)
            delta_ref[:, cols] = jnp.sum(
                turned[HEAD:] * attn_t_ref[:, cols], axis=0, keepdims=True
            )

    pl.semaphore_wait(barrier, count - 1)

    def rows_copy(src, land, ssem, rsem, target, source):
        key = lane_of(source) * steps + source[0]
        owner = number_of(target)
        return remote(src.at[owner], land.at[key], ssem.at[owner], rsem.at[key], target)

    def outer_peer(k):
        return ((outer + k) % steps, inner, fsdp)

    def send_rows(first, last, *refs):
        @pl.loop(first, last)
        def _(k):
            target = member_device((number + k) % count)
            for group in refs:
                rows_copy(*group, target, here).start()

    gate_refs = (d_gate_any, gate_land, gate_send, gate_recv)
    up_refs = (d_up_any, up_land, up_send, up_recv)
    qkv_refs = (d_weights, qkv_land, qkv_send, qkv_recv)

    down_number = lane * steps + outer
    down_out = remote(
        d_down_any, down_land, down_sem.at[0], down_sem.at[1], member_device(down_number)
    )
    down_away = down_number != number
    down_stay = pltpu.make_async_copy(d_down_any, down_land, down_sem.at[2])

    shares = [
        Exchange(src, ref.at[far_at], ref.at[mine_at], share_send.at[n], share_recv.at[n])
        for n, (src, ref) in enumerate(((wq_any, wq), (wk_any, wk), (wv_any, wv)))
    ]

    def out_copy(device, source):
        return remote(
            out_any.at[slot_of(device)],
            out_land.at[slot_of(source)],
            out_send.at[slot_of(device)],
            out_recv.at[slot_of(source)],
            device,
        )

    spread = Gather(
        [res_own.at[0], res_own.at[1]],
        lambda device: token_at(res_land, device, part),
        res_send,
        res_recv,
    )

    @pl.when(down_away)
    def _():
        down_out.start()

    @pl.when(jnp.logical_not(down_away))
    def _():
        down_stay.start()

    for share in shares:
        share.start()
    spread.start()
    res_land[0, pl.ds(early_row(me, part), part)] = res_own[0]
    res_land[1, pl.ds(late_row(me, part), part)] = res_own[1]
    own_out = pltpu.make_async_copy(out_any.at[my_slot], out_land.at[my_slot], load_sem.at[6])
    own_out.start()
    send_rows(1, count // 2, gate_refs)

    def block(slot, row, size, col, mask):
        at = pl.ds(pl.multiple_of(row, sub), size)
        kv = kv_ref[slot, at, :]
        cols = pl.ds(pl.multiple_of(col, wide), wide)
        probs = jnp.exp2(dot(kv, qt_ref[:, cols]) * SCORE2 - log_ref[:, cols])
        if mask is not None:
            probs = jnp.where(mask, probs, 0.0)
        grads = dot(kv, gt_ref[:, cols])
        grads = (probs * (grads - delta_ref[:, cols]) * SCORE).astype(BF16)
        dkv_ref[slot, at, :] += dot(grads, q_ref[cols, :]) + dot(
            probs.astype(BF16), g_ref[cols, :]
        )
        acc_ref[:, cols] += dot(kv, grads, ((0,), (0,)))

    def kv_copy(slot, late, source):
        at = pl.ds(late * half, half)
        return remote(
            dkv_send.at[slot, at],
            dkv_land.at[source, at],
            kv_send.at[late, slot],
            kv_recv.at[late, source],
            (slot, inner, fsdp),
        )

    @pl.loop(1, steps)
    def _(k):
        slot = (outer + k) % steps
        late = jnp.where(slot < outer, 0, 1)

        @pl.loop(0, 2)
        def _(n):
            block(slot, 0, half, (2 + n) * wide, None)
            block(slot, late * half, half, (late * 2 + n) * wide, None)

        dkv_send[slot] = dkv_ref[slot].astype(BF16)
        kv_copy(slot, 0, outer).start()

        @pl.when(slot > outer)
        def _():
            kv_copy(slot, 1, outer).start()

    for k in range(1, 8):
        out_copy(group_peer(k), here).start()
    spread.pass_on(1)
    for share in shares:
        share.share()
    key = lax.broadcasted_iota(jnp.int32, (sub, wide), 0)
    query = lax.broadcasted_iota(jnp.int32, (sub, wide), 1) % sub
    diagonal = key <= query

    @pl.loop(0, 2)
    def _(late):
        block(outer, late * half, sub, late * 2 * wide, diagonal)
        block(outer, late * half, sub, late * 2 * wide + wide, None)
        block(outer, late * half + sub, sub, late * 2 * wide + wide, diagonal)

    @pl.loop(0, 2)
    def _(n):
        block(outer, 0, half, (2 + n) * wide, None)

    def rope_back(grads, at):
        return grads * cos_ref[at, :] + halves(grads * sin_ref[at, :], front)

    def norm_back(raw, grads, gain):
        inverse = head_inverse(raw, low)
        scaled = grads * gain
        product = scaled * raw
        first = jnp.sum(jnp.where(low, product, 0.0), axis=-1, keepdims=True)
        second = jnp.sum(jnp.where(low, 0.0, product), axis=-1, keepdims=True)
        inner_mean = jnp.where(low, first, second) * (1.0 / HEAD)
        back = inverse * scaled - raw * (inverse * inverse * inverse) * inner_mean
        return back, jnp.sum(grads * raw * inverse, axis=0, keepdims=True)

    sums[...] = jnp.zeros_like(sums)

    @pl.loop(0, 4)
    def _(tile):
        heads = []
        for head in range(2):
            cols = pl.ds(pl.multiple_of(tile * wide + head * sub, sub), sub)
            heads.append(acc_ref[:HEAD, cols])
        at = pl.ds(pl.multiple_of(tile * sub, sub), sub)
        inside = pl.ds(pl.multiple_of((tile % 2) * sub, sub), sub)
        grads = rope_back(jnp.concatenate(heads, axis=0).T, at)
        back, gain = norm_back(proj_ref[at, :twice], grads, qg_ref[...])
        d_qkv[tile // 2, inside, :twice] = back.astype(BF16)
        sums[2:3, :twice] += gain

    @pl.loop(1, steps)
    def _(k):
        source = (outer + k) % steps
        kv_copy(source, 0, source).wait_recv()
        early = pl.ds(0, half)
        dkv_ref[outer, early, :] += dkv_land[source, early, :].astype(F32)

        @pl.when(source < outer)
        def _():
            kv_copy(source, 1, source).wait_recv()
            at = pl.ds(half, half)
            dkv_ref[outer, at, :] += dkv_land[source, at, :].astype(F32)

    @pl.loop(0, 4)
    def _(tile):
        at = pl.ds(pl.multiple_of(tile * sub, sub), sub)
        inside = pl.ds(pl.multiple_of((tile % 2) * sub, sub), sub)
        grads = dkv_ref[outer, at, :]
        raw = proj_ref[at, twice:]
        back, gain = norm_back(raw, jnp.where(low, rope_back(grads, at), 0.0), kg_ref[...])
        d_qkv[tile // 2, inside, twice:] = jnp.where(low, back, grads).astype(BF16)
        sums[2:3, twice : 2 * twice] += gain

    def lane_cols(device):
        return pl.ds(pl.multiple_of(lane_of(device) * 2 * twice, 2 * twice), 2 * twice)

    def swap_copy(k, n, owner):
        device = group_peer(k)
        return remote(
            token_at(d_qkv, device, part)[n],
            tokens_land.at[n, :, lane_cols(owner)],
            swap_send.at[n, k],
            swap_recv.at[n, slot_of(owner)],
            device,
        )

    for k in range(1, 8):
        for n in range(2):
            swap_copy(k, n, here).start()
    tokens_land[0, :, lane_cols(here)] = d_qkv[0, pl.ds(early_row(me, part), part), :]
    tokens_land[1, :, lane_cols(here)] = d_qkv[1, pl.ds(late_row(me, part), part), :]
    send_rows(count // 2, count, gate_refs)

    loads[0].wait()
    per = d_weights.shape[1]
    normed_rows = normed.reshape(2 * half, width)
    d_rows = d_qkv.reshape(2 * half, 2 * twice)

    @pl.loop(0, width // BLOCK)
    def _(tile):
        at = pl.ds(pl.multiple_of(tile * BLOCK, BLOCK), BLOCK)
        value = dot(normed_rows[:, at], d_rows[...], ((0,), (0,)))
        many = BLOCK // per
        d_weights[pl.ds(tile * many, many)] = value.reshape(many, per, 2 * twice).astype(BF16)

    send_rows(1, count, qkv_refs, up_refs)
    own_key = lane * steps + outer
    qkv_land[own_key] = d_weights[number]
    own_rows = [
        pltpu.make_async_copy(src.at[number], land.at[own_key], load_sem.at[n])
        for n, (src, land) in ((4, (d_gate_any, gate_land)), (5, (d_up_any, up_land)))
    ]
    for copy in own_rows:
        copy.start()
    spread.pass_on(2)
    spread.pass_on(3)

    for copy in loads[1:]:
        copy.wait()
    for share in shares:
        share.finish()
    for k in range(1, 8):
        for n in range(2):
            swap_copy(k, n, group_peer(k)).wait_recv()
    lower = lax.broadcasted_iota(jnp.int32, (rows, twice), 1) < HEAD
    for m in range(4):
        kv_pair = []
        for n in range(2):
            base = (2 * m + n) * 2 * twice
            values = tokens_land[:, :, base : base + 2 * twice].reshape(rows, 2 * twice)
            dq_rows[:, (2 * m + n) * twice : (2 * m + n + 1) * twice] = values[:, :twice]
            kv_pair.append(values[:, twice:].astype(F32))
        first, second = kv_pair
        at = slice(m * twice, (m + 1) * twice)
        dk_rows[:, at] = jnp.where(lower, first, pltpu.roll(second, HEAD, 1)).astype(BF16)
        dv_rows[:, at] = jnp.where(lower, pltpu.roll(first, HEAD, 1), second).astype(BF16)
    error = dot(dq_rows[...], wq[...], ((1,), (1,)))
    error = error + dot(dk_rows[...], wk[...], ((1,), (1,)))
    error = error + dot(dv_rows[...], wv[...], ((1,), (1,)))
    inputs = x_ref[...].reshape(rows, width).astype(F32)
    inverse = lax.rsqrt(jnp.mean(inputs * inputs, axis=-1, keepdims=True) + EPS)
    scaled = error * gain_ref[...]
    inner_mean = jnp.mean(scaled * inputs, axis=-1, keepdims=True)
    back = inverse * scaled - inputs * (inverse * inverse * inverse) * inner_mean
    dx_ref[...] = (d_res_ref[...].reshape(rows, width) + back).reshape(2, part, width)
    sums[0:1, :] = jnp.sum(error * inputs * inverse, axis=0, keepdims=True)
    sums[1:2, :] = ffn_gain_ref[...]

    def near_copy(k, owner):
        return remote(
            sums,
            sums_land.at[slot_of(owner)],
            near_send.at[k],
            near_recv.at[slot_of(owner)],
            group_peer(k),
        )

    def far_copy(k, owner):
        return remote(
            gains_ref, sums_land.at[8 + owner], far_send.at[k], far_recv.at[owner], outer_peer(k)
        )

    for k in range(1, 8):
        near_copy(k, here).start()

    spread.finish()
    value = dot(
        attn_ref[...].reshape(2 * half, twice), res_land[...].reshape(2 * half, width), ((0,), (0,))
    )
    d_wo[...] = value.reshape(d_wo.shape).astype(BF16)

    def slice_copy(chunk, source):
        target = member_device(lane * steps + chunk)
        return remote(
            d_wo.at[chunk], wo_land.at[source], wo_send.at[chunk], wo_recv.at[source], target
        )

    @pl.loop(0, steps)
    def _(k):
        chunk = (outer + k) % steps
        pl.when(lane * steps + chunk != number)(slice_copy(chunk, outer).start)

    @pl.when(number // steps == lane)
    def _():
        wo_land[outer] = d_wo[number % steps]

    own_out.wait()
    total = residual_ref[...].reshape(rows, width) + out_land[my_slot].astype(F32)
    for k in range(1, 8):
        device = group_peer(k)
        out_copy(device, device).wait_recv()
        total = total + out_land[slot_of(device)].astype(F32)
    block_ref[...] = total.reshape(2, part, width).astype(BF16)

    total = sums[...]
    for k in range(1, 8):
        near_copy(k, group_peer(k)).wait_recv()
        total = total + sums_land[slot_of(group_peer(k))]
    gains_ref[...] = total

    @pl.loop(1, steps)
    def _(k):
        far_copy(k, outer).start()

    for copy in own_rows:
        copy.wait()

    @pl.loop(1, count)
    def _(k):
        source = member_device((number + k) % count)
        rows_copy(*gate_refs, here, source).wait_recv()

    def added(land, which):
        total = land[which * steps].astype(F32)
        for z in range(1, steps):
            total = total + land[which * steps + z].astype(F32)
        return total

    reach = gate_land.shape[2]
    tiles = 2 * (reach // BLOCK) - 1
    step = reach - BLOCK

    def join_windows(land, ref):
        for pair in range(4):
            base = pair * tiles * BLOCK
            first, second = added(land, 2 * pair), added(land, 2 * pair + 1)
            ref[:, base : base + step] = first[:, :step]
            ref[:, base + step : base + reach] = first[:, step:] + second[:, :BLOCK]
            ref[:, base + reach : base + tiles * BLOCK] = second[:, BLOCK:]

    join_windows(gate_land, own_gate_ref)

    @pl.when(down_away)
    def _():
        down_out.wait_send()
        down_out.wait_recv()

    @pl.when(jnp.logical_not(down_away))
    def _():
        down_stay.wait()

    own_down_ref[...] = down_land[...].astype(F32)

    @pl.loop(1, count)
    def _(k):
        source = member_device((number + k) % count)
        rows_copy(*qkv_refs, here, source).wait_recv()
        rows_copy(*up_refs, here, source).wait_recv()

    join_windows(up_land, own_up_ref)
    for pair in range(4):
        first, second = added(qkv_land, 2 * pair), added(qkv_land, 2 * pair + 1)
        own_q_ref[:, 2 * pair * twice : (2 * pair + 1) * twice] = first[:, :twice]
        own_q_ref[:, (2 * pair + 1) * twice : (2 * pair + 2) * twice] = second[:, :twice]
        first, second = first[:, twice:], second[:, twice:]
        lower = lax.broadcasted_iota(jnp.int32, first.shape, 1) < HEAD
        at = slice(pair * twice, (pair + 1) * twice)
        own_k_ref[:, at] = jnp.where(lower, first, pltpu.roll(second, HEAD, 1))
        own_v_ref[:, at] = jnp.where(lower, pltpu.roll(first, HEAD, 1), second)

    @pl.loop(0, steps)
    def _(z):
        source = (z, (number // steps) % 4, (number // steps) // 4)
        pl.when(number_of(source) != number)(slice_copy(0, z).wait_recv)

    own_o_ref[...] = jnp.zeros_like(own_o_ref)

    @pl.loop(0, steps)
    def _(z):
        own_o_ref[...] += wo_land[z].astype(F32)

    @pl.loop(1, steps)
    def _(k):
        far_copy(k, outer).wait_send()

    @pl.loop(1, steps)
    def _(k):
        source = (outer + k) % steps
        far_copy(k, source).wait_recv()
        gains_ref[...] += sums_land[8 + source]

    for k in range(1, 8):
        near_copy(k, here).wait_send()
        out_copy(group_peer(k), here).wait_send()
        for n in range(2):
            swap_copy(k, n, here).wait_send()
    spread.drain()

    @pl.loop(0, steps)
    def _(chunk):
        pl.when(lane * steps + chunk != number)(slice_copy(chunk, outer).wait_send)

    @pl.loop(1, steps)
    def _(k):
        slot = (outer + k) % steps
        kv_copy(slot, 0, outer).wait_send()

        @pl.when(slot > outer)
        def _():
            kv_copy(slot, 1, outer).wait_send()

    @pl.loop(1, count)
    def _(k):
        target = member_device((number + k) % count)
        for refs in (gate_refs, up_refs, qkv_refs):
            rows_copy(*refs, target, here).wait_send()


def back(args, steps):
    q_t, q_cols = args[0], args[1]
    kv, x = args[5], args[11]
    normed, wq, wk = args[17], args[18], args[19]
    d_gate, d_down = args[21], args[23]
    part, width = x.shape[1:]
    half = normed.shape[1]
    tokens = 2 * half
    rows = 2 * part
    count = steps * 8
    per = width // count
    reach = d_gate.shape[2]
    ff = (2 * (reach // BLOCK) - 1) * BLOCK * 4
    twice = 2 * HEAD
    q_cols_all, kv_cols = wq.shape[1], wk.shape[1]
    return pl.pallas_call(
        functools.partial(back_kernel, steps),
        out_shape=(
            shape((2, part, width)),
            shape((2, part, width), F32),
            shape((8, width), F32),
            shape((per, q_cols_all), F32),
            shape((per, kv_cols), F32),
            shape((per, kv_cols), F32),
            shape((twice // steps, width), F32),
            shape((per, ff), F32),
            shape((per, ff), F32),
            shape(d_down.shape, F32),
        ),
        in_specs=[VMEM] * 17 + [ANY] * 8,
        out_specs=[VMEM] * 10,
        scratch_shapes=[
            pltpu.VMEM(normed.shape, BF16),
            pltpu.VMEM((width, q_cols_all), BF16),
            pltpu.VMEM((width, kv_cols), BF16),
            pltpu.VMEM((width, kv_cols), BF16),
            pltpu.VMEM(q_t.shape, BF16),
            pltpu.VMEM(q_cols.shape, BF16),
            pltpu.VMEM((1, 2 * tokens), F32),
            pltpu.VMEM(q_t.shape, F32),
            pltpu.VMEM(kv.shape, F32),
            pltpu.VMEM(kv.shape, BF16),
            pltpu.VMEM(kv.shape, BF16),
            pltpu.VMEM((2, half, 2 * twice), BF16),
            pltpu.VMEM((2, part, 16 * twice), BF16),
            pltpu.VMEM((rows, q_cols_all), BF16),
            pltpu.VMEM((rows, kv_cols), BF16),
            pltpu.VMEM((rows, kv_cols), BF16),
            pltpu.VMEM((count, per, 2 * twice), BF16),
            pltpu.VMEM((steps, twice // steps, width), BF16),
            pltpu.VMEM((2, part, width), BF16),
            pltpu.VMEM((2, half, width), BF16),
            pltpu.VMEM((8, rows, width), BF16),
            pltpu.VMEM((count, per, reach), BF16),
            pltpu.VMEM((count, per, reach), BF16),
            pltpu.VMEM((count, per, 2 * twice), BF16),
            pltpu.VMEM(d_down.shape, BF16),
            pltpu.VMEM((steps, twice // steps, width), BF16),
            pltpu.VMEM((8, width), F32),
            pltpu.VMEM((8 + steps, 8, width), F32),
            DMA((7,)),
            DMA((count,)),
            DMA((count,)),
            DMA((count,)),
            DMA((count,)),
            DMA((count,)),
            DMA((count,)),
            DMA((3,)),
            DMA((steps,)),
            DMA((steps,)),
            DMA((8,)),
            DMA((8,)),
            DMA((2, 8)),
            DMA((2, 8)),
            DMA((3, 4)),
            DMA((3, 4)),
            DMA((2, steps)),
            DMA((2, steps)),
            DMA((2, 8)),
            DMA((2, 8)),
            DMA((8,)),
            DMA((8,)),
            DMA((steps,)),
            DMA((steps,)),
        ],
        compiler_params=params(3),
        name="back",
    )(*args)


def local(
    block_input, dy, attn_gain, q_gain, k_gain, ffn_gain, wq, wk, wv, wo, w_gate, w_up, w_down
):
    steps = lax.axis_size("outer")
    group = lax.axis_size("inner") * lax.axis_size("fsdp")
    part, width = block_input.shape[2:]
    tiles = 2 * w_gate.shape[1] // group // BLOCK
    reach = (tiles + 1) // 2 * BLOCK
    x = block_input.reshape(2, part, width)
    cot = dy.reshape(2, part, width)
    index = jnp.arange(2 * HEAD, dtype=jnp.int32) % (HEAD // 2)
    frequency = (ROPE_BASE ** (-2.0 * index.astype(F32) / HEAD))[None]
    q_gain2 = jnp.tile(q_gain, 2)[None]
    k_gain2 = jnp.tile(k_gain, 2)[None]
    normed, proj, q_cols, q_t, kv_own, cos, sin = front(
        x, attn_gain[None], wq, wk, wv, frequency, q_gain2, k_gain2, steps
    )
    kv, cot_group, wo_far, gate_far, up_far, attn_t, log_total, attn, residual, ffn_rows = middle(
        x, cot, q_t, kv_own, ffn_gain[None], wo, w_gate, w_up, reach, steps
    )
    partial, d_residual, attn_grad, d_ffn_gain, d_gate, d_up, d_down = ffn(
        ffn_rows,
        residual,
        cot,
        ffn_gain[None],
        cot_group.reshape(2 * group, part, width),
        (w_gate, gate_far, w_up, up_far, w_down, wo, wo_far),
        steps,
    )
    result, grad_in, gains, own_q, own_k, own_v, own_o, own_gate, own_up, own_down = back(
        (
            q_t,
            q_cols,
            attn_grad,
            attn_t,
            log_total,
            kv,
            proj,
            cos,
            sin,
            q_gain2,
            k_gain2,
            x,
            d_residual,
            residual,
            attn,
            attn_gain[None],
            d_ffn_gain,
            normed,
            wq,
            wk,
            wv,
            d_gate,
            d_up,
            d_down,
            partial,
        ),
        steps,
    )
    return (
        result.reshape(block_input.shape),
        grad_in.reshape(block_input.shape),
        gains[0],
        gains[2, :HEAD] + gains[2, HEAD : 2 * HEAD],
        gains[2, 2 * HEAD : 3 * HEAD],
        gains[1],
        own_q,
        own_k,
        own_v,
        own_o,
        own_gate,
        own_up,
        own_down,
    )


def solution(mesh):
    ctx, fsdp = mesh.shape["ctx"], mesh.shape["fsdp"]
    inner = 8 // fsdp
    grid = Mesh(mesh.devices.reshape(ctx // inner, inner, fsdp), EVERY)
    tokens = P(None, ("outer", "inner"), "fsdp", None)
    shard = P("fsdp", None)
    owned = P(EVERY, None)
    return jax.shard_map(
        local,
        mesh=grid,
        in_specs=(tokens, tokens) + (P(),) * 4 + (shard,) * 7,
        out_specs=(tokens, tokens) + (P(),) * 4 + (owned,) * 7,
        check_vma=False,
    )
```

time: 478 us -> 294 us (0.62); the launches traced: 472 us -> 294 us
  waiting for transfers between devices: 85.9 us -> 0 us
  Pallas kernels: 349 us -> 276 us
  local copies, waits for them, and re-layouts: 25.6 us -> 15.2 us
  starting transfers between devices: 5.78 us -> 0 us
    ppermute x5 -> x0, waiting for transfers between devices: 85.9 us -> none  [swap(): lax.ppermute(array, 'fsdp', [(k, (k + 1) % axis_size) for k in range(axis...]
    pallas_call x4, Pallas kernels: 349 us -> 276 us  [the longest x1 152 us: back(): pl.pallas_call(functools.partial(back_kernel, steps), out_shape=(shape((2...]
    unnamed x41 -> x17, local copies, waits for them, and re-layouts: 17.3 us -> 11.2 us
    ppermute x5 -> x0, starting transfers between devices: 5.78 us -> none  [swap(): lax.ppermute(array, 'fsdp', [(k, (k + 1) % axis_size) for k in range(axis...]
  transfers between devices with their start and end apart: 5 -> 0, of which waited for: 3 -> 0; matrix products, arithmetic and copies ran while one was open for 3% -> 0% of each run, Pallas kernels for 23% -> 0%
where the time goes in v4:
time: 294 us
  Pallas kernels  276 us (94%)
  local copies, waits for them, and re-layouts  15.2 us (5%)
    pallas_call x1, Pallas kernels, back(): pl.pallas_call(functools.partial(back_kernel, steps), out_shape=(shape((2...  152 us
    pallas_call x1, Pallas kernels, middle(): pl.pallas_call(functools.partial(middle_kernel, steps), out_shape=(shape(...  54.9 us
    pallas_call x1, Pallas kernels, ffn(): pl.pallas_call(functools.partial(ffn_kernel, steps), out_shape=(shape((8,...  48.7 us
    pallas_call x1, Pallas kernels, front(): pl.pallas_call(functools.partial(front_kernel, steps), out_shape=(shape((...  20.2 us
    unnamed x17, local copies, waits for them, and re-layouts  11.2 us

profile of v4, /device:TPU:6, one launch (start us, length us, event | category | flops | bytes accessed | tf_op | source)
XLA Modules:
  0.0 293.9 jit_solution(13204868103439939809)
XLA Ops:
  0.6 0.5 fusion.2.freq_ref
  1.2 0.7 tile.4
  1.8 0.6 broadcast_in_dim_tile.6.qg_ref
  2.4 0.7 tile.5
  3.1 0.6 broadcast_in_dim_tile.7.kg_ref
  3.7 20.2 %front.1 = (bf16[2,512,1024]{2,1,0:T(8,128)(2,1)}, f32[1024,256]{1,0:T(8,128)}, bf16[2048,128]{1,0:T(8,128)(2,1)}, bf16[128,2048]{1,0:T(8,128)(2,1)}, bf16[1024,...) custom-call(bf16[2,64,1024]{2,1,0:T(8,128)(2,1)} %bitcast.17, f32[1,1024]{1,0:T(1,128)} %bitcast.25, ...), custom_call_target="tpu_custom_call" | custom-call | tf_op jit(solution)/shard_map/front/pallas_call | solution.py:609
  23.9 54.9 %middle.1 = (bf16[4,1024,128]{2,1,0:T(8,128)(2,1)}, bf16[8,2,64,1024]{3,2,1,0:T(8,128)(2,1)}, bf16[512,1024]{1,0:T(8,128)(2,1)}, bf16[512,640]{1,0:T(8,128)(2,1)...) custom-call(bf16[2,64,1024]{2,1,0:T(8,128)(2,1)} %bitcast.18, ...), custom_call_target="tpu_custom_call" | custom-call | tf_op jit(solution)/shard_map/middle/pallas_call | solution.py:645
  78.8 48.7 %ffn.1 = (bf16[8,128,1024]{2,1,0:T(8,128)(2,1)}, f32[2,64,1024]{2,1,0:T(8,128)}, bf16[2,512,128]{2,1,0:T(8,128)(2,1)}, f32[1,1024]{1,0:T(1,128)}, bf16[32,32,640...) custom-call(bf16[2,64,1024]{2,1,0:T(8,128)(2,1)} %get-tuple-element.50.ffn_ref, ...), custom_call_target="tpu_custom_call" | custom-call | tf_op jit(solution)/shard_map/ffn/pallas_call | solution.py:978
  127.5 152.3 %back.1 = (bf16[2,64,1024]{2,1,0:T(8,128)(2,1)}, f32[2,64,1024]{2,1,0:T(8,128)}, f32[8,1024]{1,0:T(8,128)}, f32[32,1024]{1,0:T(8,128)}, f32[32,512]{1,0:T(8,128)...) custom-call(bf16[128,2048]{1,0:T(8,128)(2,1)} %get-tuple-element.47., ...), custom_call_target="tpu_custom_call" | custom-call | tf_op jit(solution)/shard_map/back/pallas_call | solution.py:1606
  279.8 0.0 copy-start.3
  279.8 0.0 copy-start.2
  279.8 0.0 copy-start.1
  279.8 1.4 slice_bitcast_fusion
  281.2 1.4 fusion.3
  282.6 1.7 copy.37
  284.3 0.0 copy-start
  284.3 1.9 copy.38
  286.2 1.6 copy.39
  287.8 1.5 copy.40
  289.3 1.5 copy.41
  290.8 0.0 copy-done.3
  290.8 0.7 copy.42
  291.4 0.0 copy-done.2
  291.4 0.8 copy.43
  292.2 0.0 copy-done.1
  292.2 0.8 copy.44
  293.1 0.0 copy-done
  293.1 0.8 copy.45
Async XLA Ops:
  279.8 11.0 %copy-start.3 = (f32[32,1024]{1,0:T(8,128)S(1)}, f32[32,1024]{1,0:T(8,128)}, u32[]{:S(2)}) copy-start(f32[32,1024]{1,0:T(8,128)} %get-tuple-element.120) | copy-start | bytes 393220
  279.8 11.6 %copy-start.2 = (f32[32,4608]{1,0:T(8,128)S(1)}, f32[32,4608]{1,0:T(8,128)}, u32[]{:S(2)}) copy-start(f32[32,4608]{1,0:T(8,128)} %get-tuple-element.121) | copy-start | bytes 1769476
  279.8 12.4 %copy-start.1 = (f32[32,4608]{1,0:T(8,128)S(1)}, f32[32,4608]{1,0:T(8,128)}, u32[]{:S(2)}) copy-start(f32[32,4608]{1,0:T(8,128)} %get-tuple-element.122) | copy-start | bytes 1769476
  284.3 8.8 %copy-start = (f32[144,1024]{1,0:T(8,128)S(1)}, f32[144,1024]{1,0:T(8,128)}, u32[]{:S(2)}) copy-start(f32[144,1024]{1,0:T(8,128)} %get-tuple-element.123) | copy-start | bytes 1769476
